TPU v7x, 128 devices: a whole 4x4x4 slice. The times are simulated.
128 devices in a mesh: expert: 2 (over x_hi), seq: 8 (over x_lo, z), fsdp: 8 (over y, core).
Axes of the slice: x: 4 (x_hi: 2, x_lo: 2; x = x_hi * 2 + x_lo), y: 4, z: 4, core: 2. Of those that a mesh axis runs over, the one named last changes fastest.
Arguments:
- queries: bfloat16 [16384, 5120], P(('expert', 'seq', 'fsdp')), parts along dimension 0, may hold values from -100 to 100
- keys: bfloat16 [16384, 5120], P(('expert', 'seq', 'fsdp')), parts along dimension 0, may hold values from -100 to 100
- values: bfloat16 [16384, 5120], P(('expert', 'seq', 'fsdp')), parts along dimension 0, may hold values from -6 to 6
- query_gain: float32 [10240], P('expert'), parts along dimension 0, may hold values from 1 to 3
- key_gain: float32 [10240], P('expert'), parts along dimension 0, may hold values from 1 to 3
- timestep: int32 [2], P('expert'), parts along dimension 0, may hold values from 0 to 999, as said below
- gate_base: float32 [10240], P('expert'), parts along dimension 0, may hold values from -3 to 3
- time_weight: float32 [512, 5120], P('expert'), parts along dimension 0, may hold values from -0.375 to 0.375
Outputs:
- attended: bfloat16 [16384, 5120], P(('expert', 'seq', 'fsdp')), parts along dimension 0
There are 2 independent parts, one for each index of `expert`. A program takes and returns all parts, laid end to end along the dimension named above; each array names one. Nothing has to cross between parts.
Inputs may be any that keep to these rules, and one draw needn't show every extreme that they name: Part 0 is the high-noise group, with a timestep from 875 to 999; part 1 the low-noise group, with one from 0 to 874.
All inputs are finite; a program needn't handle non-finite values.
Results may differ from a plain program's by a relative error of at most 0.012.
The roundings to bfloat16 on the way count: a program that leaves them out, or rounds other values in their place, can miss the bound.
Values may be sent and summed in bfloat16 or wider, within the bound.
No kernel may reach another device: no remote copies, remote signals or barrier semaphores. Data moves between devices by JAX's collectives and lax.ppermute only.
A program may use at most 384 MiB of HBM per device.

v0:
```python
import functools
import math

import jax
import jax.numpy as jnp
import numpy as np
from jax import lax
from jax.experimental import pallas as pl
from jax.experimental.pallas import tpu as pltpu
from jax.sharding import Mesh
from jax.sharding import PartitionSpec as P


HEAD_DIM = 128
FREQ = 256
HGT = 32
WID = 32
EPSILON = 1e-06
LOG2E = 1.4426950408889634
SCALE = LOG2E / math.sqrt(HEAD_DIM)
VMEM_BYTES = 63 * 1024 * 1024
F32 = jnp.float32
BF16 = jnp.bfloat16


def inverse_row():
    half = HEAD_DIM // 2
    sixth = HEAD_DIM // 6
    frame = (HEAD_DIM - 4 * sixth) // 2
    j = np.arange(half)
    in_frame = j < frame
    in_row = (j >= frame) & (j < frame + sixth)
    local = np.where(in_frame, j, np.where(in_row, j - frame, j - frame - sixth))
    dims = np.where(in_frame, 2 * frame, 2 * sixth)
    inverse = np.power(10000.0, -2.0 * local / dims).astype(np.float32)
    kind = np.where(in_frame, 0, np.where(in_row, 1, 2))
    return np.repeat(inverse, 2), np.repeat(kind, 2)


def prep_kernel(block_ref, inv_hbm, *refs, tensors, plan):
    count = len(tensors)
    turned = [n for n, kind in enumerate(tensors) if kind != "v"]
    sources, refs = refs[:count], refs[count:]
    gains, refs = refs[:len(turned)], refs[len(turned):]
    outs, refs = refs[:len(plan)], refs[len(plan):]
    inv_ref, swap_ref, cos_ref, sin_ref, sems = refs[:5]
    bufs, refs = refs[5:5 + count], refs[5 + count:]
    gain_bufs, rms_refs = refs[:len(turned)], refs[len(turned):]
    tokens, width = bufs[0].shape
    step = pl.program_id(0)

    @pl.when(step == 0)
    def _():
        pairs = [(inv_hbm, inv_ref)] + list(zip(sources, bufs)) + list(zip(gains, gain_bufs))
        copies = [pltpu.make_async_copy(a, b, sems.at[n]) for n, (a, b) in enumerate(pairs)]
        for copy in copies:
            copy.start()
        lane = lax.broadcasted_iota(jnp.int32, (HEAD_DIM, HEAD_DIM), 1)
        depth = lax.broadcasted_iota(jnp.int32, (HEAD_DIM, HEAD_DIM), 0)
        below = jnp.where((lane % 2 == 0) & (depth == lane + 1), -1.0, 0.0)
        above = jnp.where((lane % 2 == 1) & (depth == lane - 1), 1.0, 0.0)
        swap_ref[...] = (below + above).astype(BF16)
        copies[0].wait()
        token = block_ref[0] * tokens + lax.broadcasted_iota(jnp.int32, (tokens, HEAD_DIM), 0)
        pair = lax.broadcasted_iota(jnp.int32, (tokens, HEAD_DIM), 1) // 2
        sixth = HEAD_DIM // 6
        frame_pairs = (HEAD_DIM - 4 * sixth) // 2
        frame = token // (HGT * WID)
        row = (token // WID) % HGT
        column = token % WID
        coord = jnp.where(pair < frame_pairs, frame,
                          jnp.where(pair < frame_pairs + sixth, row, column)).astype(F32)
        angle = coord * inv_ref[...]
        cos_ref[...] = jnp.cos(angle)
        sin_ref[...] = jnp.sin(angle)
        for copy in copies[1:]:
            copy.wait()
        for src, dst in zip([bufs[n] for n in turned], rms_refs):
            total = jnp.zeros((tokens, HEAD_DIM), F32)
            for h in range(width // HEAD_DIM):
                x = src[:, h * HEAD_DIM:(h + 1) * HEAD_DIM].astype(F32)
                total = total + x * x
            mean = jnp.sum(total, axis=1, keepdims=True) / width
            dst[...] = jnp.broadcast_to(lax.rsqrt(mean + EPSILON), (tokens, HEAD_DIM))

    even = lax.broadcasted_iota(jnp.int32, (1, HEAD_DIM), 1) % 2 == 0

    def columns(n, head):
        return bufs[n][:, pl.ds(pl.multiple_of(head * HEAD_DIM, HEAD_DIM), HEAD_DIM)]

    def rotated(n, head):
        x = columns(n, head)
        xs = jnp.dot(x, swap_ref[...], preferred_element_type=F32)
        g = gain_bufs[turned.index(n)][pl.ds(head, 1), :]
        gs = jnp.where(even, pltpu.roll(g, HEAD_DIM - 1, 1), pltpu.roll(g, 1, 1))
        r = rms_refs[turned.index(n)][...]
        return (x.astype(F32) * r * g) * cos_ref[...] + (xs * r * gs) * sin_ref[...]

    for dst, (first, peers, heads, kinds) in zip(outs, plan):
        for peer in range(peers):
            for h in range(heads):
                head = first + (step * peers + peer) * heads + h
                for slot, kind in enumerate(kinds):
                    n = tensors.index(kind)
                    y = columns(n, head).astype(F32) if kind == "v" else rotated(n, head)
                    dst[peer, h, slot] = (y if kind == "k" else y.T).astype(BF16)


def prepare(steps, block, tensors, plan):
    kinds = tuple(tensors)
    tokens, width = tensors[kinds[0]][0].shape
    heads = width // HEAD_DIM
    inverse, _ = inverse_row()
    tile = (HEAD_DIM, tokens)
    gains = [tensors[k][1].reshape(heads, HEAD_DIM) for k in kinds if k != "v"]
    hbm = pl.BlockSpec(memory_space=pltpu.HBM)
    shapes = [(peers, count, len(slots)) + tile for _, peers, count, slots in plan]
    return pl.pallas_call(
        functools.partial(prep_kernel, tensors=kinds, plan=plan),
        grid=(steps,),
        in_specs=[pl.BlockSpec(memory_space=pltpu.SMEM)] + [hbm] * (1 + len(kinds) + len(gains)),
        out_specs=[pl.BlockSpec(shape, lambda i: (i, 0, 0, 0, 0)) for shape in shapes],
        out_shape=[jax.ShapeDtypeStruct((steps * shape[0],) + shape[1:], BF16)
                   for shape in shapes],
        scratch_shapes=[
            pltpu.VMEM((1, HEAD_DIM), F32),
            pltpu.VMEM((HEAD_DIM, HEAD_DIM), BF16),
            pltpu.VMEM((tokens, HEAD_DIM), F32),
            pltpu.VMEM((tokens, HEAD_DIM), F32),
            pltpu.SemaphoreType.DMA((1 + len(kinds) + len(gains),)),
        ] + [pltpu.VMEM((tokens, width), BF16) for _ in kinds]
        + [pltpu.VMEM((heads, HEAD_DIM), F32) for _ in gains]
        + [pltpu.VMEM((tokens, HEAD_DIM), F32) for _ in gains],
        compiler_params=pltpu.CompilerParams(vmem_limit_bytes=VMEM_BYTES),
    )(block, jnp.asarray(inverse)[None, :], *[tensors[k][0] for k in kinds], *gains)


def attend_kernel(*refs, sizes, shifts, resume, final, tk, sub):
    count = len(sizes)
    q_ref, gate_ref = refs[:2]
    pieces = refs[2:2 + count]
    at = 2 + count
    if resume:
        stat_in, mixed_in = refs[at:at + 2]
        at += 2
    if final:
        o_ref = refs[at]
        at += 1
    else:
        stat_out, mixed_out = refs[at:at + 2]
        at += 2
    k_bufs, v_bufs, s_buf, sems = refs[at:]
    head = pl.program_id(0)
    slot = head % 2

    def loads(head, slot):
        copies = []
        offset = 0
        for i, size in enumerate(sizes):
            for j, buf in enumerate((k_bufs, v_bufs)):
                copies.append(pltpu.make_async_copy(
                    pieces[i].at[:, head, shifts[i] + j], buf.at[slot, pl.ds(offset, size)],
                    sems.at[slot, 2 * i + j]))
            offset += size
        return copies

    @pl.when(pl.program_id(1) == 0)
    def _():
        @pl.when(head == 0)
        def _():
            for copy in loads(head, slot):
                copy.start()

        @pl.when(head + 1 < pl.num_programs(0))
        def _():
            for copy in loads(head + 1, 1 - slot):
                copy.start()

        for copy in loads(head, slot):
            copy.wait()

    k_buf, v_buf = k_bufs.at[slot], v_bufs.at[slot]
    tiles = q_ref.shape[0]
    tq = tiles * HEAD_DIM
    q = jnp.concatenate([q_ref[t, 0, 0] for t in range(tiles)], axis=1).astype(F32) * SCALE
    q_high = q.astype(BF16)
    q_low = (q - q_high.astype(F32)).astype(BF16)
    q_both = jnp.concatenate([q_high, q_low], axis=0)
    blocks = sum(sizes) * HEAD_DIM // tk
    subs = tk // sub
    per_sub = sub // HEAD_DIM

    def scores(j, i):
        first = (j * subs + i) * per_sub
        k = k_buf[first:first + per_sub].reshape(sub, HEAD_DIM)
        s = jnp.dot(jnp.concatenate([k, k], axis=1), q_both, preferred_element_type=F32)
        s_buf[j % 2, i * sub:(i + 1) * sub, :] = s
        return jnp.max(s.reshape(sub // 8, 8, tq), axis=0)

    top = scores(0, 0)
    for i in range(1, subs):
        top = jnp.maximum(top, scores(0, i))
    if resume:
        peak = stat_in[0, 0:1, :]
        total = stat_in[0, 8:16, :]
        mixed = mixed_in[0]
    else:
        peak = jnp.full((1, tq), -1e30, F32)
        total = jnp.zeros((8, tq), F32)
        mixed = jnp.zeros((HEAD_DIM, tq), F32)
    for j in range(blocks):
        new_peak = jnp.maximum(peak, jnp.max(top, axis=0, keepdims=True))
        shrink = jnp.exp2(peak - new_peak)
        total = total * shrink
        part = None
        top = None
        for i in range(subs):
            if j + 1 < blocks:
                t = scores(j + 1, i)
                top = t if top is None else jnp.maximum(top, t)
            e = jnp.exp2(s_buf[j % 2, i * sub:(i + 1) * sub, :] - new_peak)
            total = total + jnp.sum(e.reshape(sub // 8, 8, tq), axis=0)
            first = (j * subs + i) * per_sub
            v = jnp.concatenate([v_buf[first + t] for t in range(per_sub)], axis=1)
            d = jnp.dot(v, e.astype(BF16), preferred_element_type=F32)
            part = d if part is None else part + d
        mixed = mixed * shrink + part
        peak = new_peak
    if final:
        out = mixed / jnp.sum(total, axis=0, keepdims=True)
        gate = gate_ref[0]
        for t in range(tiles):
            o_ref[t, 0] = (out[:, t * HEAD_DIM:(t + 1) * HEAD_DIM] * gate).astype(BF16)
    else:
        stat_out[0, 0:8, :] = jnp.broadcast_to(peak, (8, tq))
        stat_out[0, 8:16, :] = total
        mixed_out[0] = mixed


def attend(query, gate, pieces, state=None, final=True, tq=512, tk=1024, sub=1024):
    sizes = tuple(p.shape[0] for p in pieces)
    shifts = tuple(p.shape[2] - 2 for p in pieces)
    query_tiles, heads = query.shape[:2]
    step = tq // HEAD_DIM
    keys = sum(sizes)
    slots = min(heads, 2)
    state_specs = [pl.BlockSpec((1, 16, tq), lambda h, i: (h, 0, i)),
                   pl.BlockSpec((1, HEAD_DIM, tq), lambda h, i: (h, 0, i))]
    state_shapes = [jax.ShapeDtypeStruct((heads, 16, query_tiles * HEAD_DIM), F32),
                    jax.ShapeDtypeStruct((heads, HEAD_DIM, query_tiles * HEAD_DIM), F32)]
    return pl.pallas_call(
        functools.partial(attend_kernel, sizes=sizes, shifts=shifts,
                          resume=state is not None, final=final, tk=tk, sub=sub),
        grid=(heads, query_tiles // step),
        in_specs=[
            pl.BlockSpec((step, 1, 1, HEAD_DIM, HEAD_DIM), lambda h, i: (i, h, 0, 0, 0)),
            pl.BlockSpec((1, HEAD_DIM, HEAD_DIM), lambda h, i: (h, 0, 0)),
        ] + [pl.BlockSpec(memory_space=pl.ANY) for _ in pieces]
        + (state_specs if state is not None else []),
        out_specs=(pl.BlockSpec((step, 1, HEAD_DIM, HEAD_DIM), lambda h, i: (i, h, 0, 0))
                   if final else state_specs),
        out_shape=(jax.ShapeDtypeStruct((query_tiles, heads, HEAD_DIM, HEAD_DIM), BF16)
                   if final else state_shapes),
        scratch_shapes=[
            pltpu.VMEM((slots, keys, HEAD_DIM, HEAD_DIM), BF16),
            pltpu.VMEM((slots, keys, HEAD_DIM, HEAD_DIM), BF16),
            pltpu.VMEM((2, tk, tq), F32),
            pltpu.SemaphoreType.DMA((slots, 2 * len(pieces))),
        ],
        compiler_params=pltpu.CompilerParams(vmem_limit_bytes=VMEM_BYTES),
        cost_estimate=pl.CostEstimate(
            flops=8 * heads * query_tiles * keys * HEAD_DIM**3,
            transcendentals=heads * query_tiles * keys * HEAD_DIM**2,
            bytes_accessed=4 * heads * keys * HEAD_DIM**2,
        ),
    )(query, gate, *pieces, *(state or ()))


def post_kernel(*refs):
    o_ref = refs[-1]
    head = 0
    for src in refs[:-1]:
        for peer in range(src.shape[0]):
            for h in range(src.shape[1]):
                tile = src[peer, h].astype(F32).T.astype(BF16)
                o_ref[:, head * HEAD_DIM:(head + 1) * HEAD_DIM] = tile
                head += 1


def collect(*parts):
    tokens = parts[0].shape[-1]
    width = HEAD_DIM * sum(p.shape[0] * p.shape[1] for p in parts)
    return pl.pallas_call(
        post_kernel,
        out_shape=jax.ShapeDtypeStruct((tokens, width), BF16),
        compiler_params=pltpu.CompilerParams(vmem_limit_bytes=VMEM_BYTES),
        name="post",
    )(*parts)


def shift(axis, amount):
    size = lax.axis_size(axis)
    return [(i, (i + amount) % size) for i in range(size)]


def ring(pair, axis):
    half = pair.shape[0] // 2
    up = lax.ppermute(pair, axis, shift(axis, 1))
    down = lax.ppermute(pair, axis, shift(axis, -1))
    up_far = lax.ppermute(up[:half], axis, shift(axis, 1))
    down_far = lax.ppermute(down[half:], axis, shift(axis, -1))
    return [up, down, up_far, down_far]


def gates(timestep, gate_base, time_weight, first, count):
    half_freq = FREQ // 2
    exponent = jnp.arange(half_freq, dtype=jnp.int32).astype(F32) / half_freq
    frequency = jnp.power(F32(10000.0), -exponent)
    phase = timestep.astype(F32)[:, None] * frequency[None, :]
    embedded = jnp.concatenate([jnp.cos(phase), jnp.sin(phase)], axis=1)
    start = first * HEAD_DIM
    width = count * HEAD_DIM
    weight = lax.dynamic_slice_in_dim(time_weight, start, width, 1)
    base = lax.dynamic_slice_in_dim(gate_base, start, width, 0)
    projected = jnp.dot(embedded, weight, precision=lax.Precision.HIGHEST,
                        preferred_element_type=F32)
    gate = base + projected[0]
    return jnp.broadcast_to(gate.reshape(count, HEAD_DIM, 1), (count, HEAD_DIM, HEAD_DIM))


def block_attention(queries, keys, values, query_gain, key_gain, timestep, gate_base, time_weight):
    x, z, y, core = (lax.axis_index(n) for n in ("x", "z", "y", "core"))
    block = (((x * 4 + z) * 4 + y) * 2 + core).reshape(1).astype(jnp.int32)
    wide, narrow = ("x", "z", "core"), ("x", "z")
    spread = functools.partial(lax.all_to_all, split_axis=0, concat_axis=0, tiled=True)
    gate_of = functools.partial(gates, timestep, gate_base, time_weight)
    q, k, v = (queries, query_gain), (keys, key_gain), (values, None)

    (a,) = prepare(4, block, {"k": k, "v": v}, ((0, 4, 1, "kv"),))
    a_query, b = prepare(8, block, {"q": q, "k": k, "v": v},
                         ((0, 2, 1, "q"), (16, 1, 3, "qkv")))
    a = spread(a, wide)
    ring_a = ring(a, "y")
    b, a = lax.optimization_barrier((b, a))
    b = spread(b, narrow)
    own_b = b[:, :, 1:]
    ring_b = ring(own_b, "y")
    a_query, b = lax.optimization_barrier((a_query, b))
    a_query = spread(a_query, wide)
    near_b = [own_b] + ring_b[:2]
    near_b = near_b + [lax.ppermute(p, "core", shift("core", 1)) for p in near_b]
    far_b = ring_b[2:] + [lax.ppermute(p, "core", shift("core", 1)) for p in ring_b[2:]]
    gate_a = gate_of((x * 4 + z) * 2 + core, 1)
    gate_b = gate_of(16 + (x * 4 + z) * 3, 3)

    out_a = attend(a_query, gate_a, [a] + ring_a)
    out_a = spread(out_a, wide)
    state = attend(b, gate_b, near_b, final=False)
    out_b = attend(b, gate_b, far_b, state)
    out_b = spread(out_b, narrow)
    return collect(out_a, out_b)


def solution(mesh):
    fine = Mesh(mesh.devices.reshape(2, 2, 4, 4, 2), ("expert", "x", "z", "y", "core"))
    rows = P(("expert", "x", "z", "y", "core"), None)
    part = P("expert")
    return jax.shard_map(
        block_attention,
        mesh=fine,
        in_specs=(rows, rows, rows, part, part, part, part, P("expert", None)),
        out_specs=rows,
        check_vma=False,
    )
```

profile of v0, /device:TPU:0, one launch (start us, length us, event | category | flops | bytes accessed | tf_op | source)
XLA Modules:
  0.0 232.5 jit_solution(17265566489552739234)
XLA Ops:
  0.0 4.1 %shard_map.101 = bf16[16,1,2,128,128]{4,3,2,1,0:T(8,128)(2,1)} custom-call(s32[1]{0:T(128)} %bitcast.block_ref, f32[1,128]{1,0:T(1,128)} %constant.38.inv_hbm, bf16[128,5120]{1,0:T(8,128)(2,1)} %refs_0_.3, bf16[128,5120]{1,0:T(8,128)(2,1)} %refs_1_.3, f32[40,128]{1,0:T(8,128)} %bitcast.16), custom_call_target="tpu_custom_call" | custom-call | tf_op jit(solution)/shard_map/pallas_call | solution.py:118
  4.2 6.5 %all-to-all-start = ((bf16[16,1,2,128,128]{4,3,2,1,0:T(8,128)(2,1)}), bf16[16,1,2,128,128]{4,3,2,1,0:T(8,128)(2,1)}, u32[]{:S(2)}, u32[]{:S(2)}) async-start(bf16[16,1,2,128,128]{4,3,2,1,0:T(8,128)(2,1)} %shard_map.101), calls=%async_computation | async-start | bytes 2097152 | tf_op jit(solution)/shard_map/all_to_all | solution.py:342
  10.7 7.6 %shard_map.100 = (bf16[16,1,1,128,128]{4,3,2,1,0:T(8,128)(2,1)}, bf16[8,3,3,128,128]{4,3,2,1,0:T(8,128)(2,1)}) custom-call(s32[1]{0:T(128)} %bitcast.block_ref, f32[1,128]{1,0:T(1,128)} %constant.38.inv_hbm, bf16[128,5120]{1,0:T(8,128)(2,1)} %refs_0_.2, bf16[128,5120]{1,0:T(8,128)(2,1)} %refs_0_.3, bf16[128,5120]{1,0:T(8,128)(2,1)} %refs_1_.3, ...), custom_call_target="tpu_custom_call" | custom-call | tf_op jit(solution)/shard_map/pallas_call | solution.py:118
  18.2 9.0 %all-to-all-done.refs_2_ = bf16[16,1,2,128,128]{4,3,2,1,0:T(8,128)(2,1)} async-done(((bf16[16,1,2,128,128]{4,3,2,1,0:T(8,128)(2,1)}), bf16[16,1,2,128,128]{4,3,2,1,0:T(8,128)(2,1)}, u32[]{:S(2)}, u32[]{:S(2)}) %all-to-all-start) | async-done | bytes 1048608 | tf_op jit(solution)/shard_map/all_to_all | solution.py:342
  27.3 33.5 %all_to_all.25.refs_0_ = bf16[8,3,3,128,128]{4,3,2,1,0:T(8,128)(2,1)S(1)} all-to-all(bf16[8,3,3,128,128]{4,3,2,1,0:T(8,128)(2,1)} %get-tuple-element.15), channel_id=1, replica_groups=mesh['expert'=2,'x'=2,'z'=4,'y'=4,'core'=2] {'x','z'}, dimensions={0} | all-to-all | bytes 4718592 | tf_op jit(solution)/shard_map/all_to_all | solution.py:345
  60.8 1.3 slice.22.refs_2_
  62.2 0.6 copy-done
  62.7 1.6 collective-permute-start.4
  64.3 1.6 collective-permute-start
  65.9 1.7 collective-permute-start.6
  67.6 0.5 collective-permute-start.1
  68.0 53.1 %collective-permute-done.refs_3_ = bf16[16,1,2,128,128]{4,3,2,1,0:T(8,128)(2,1)S(1)} collective-permute-done((bf16[16,1,2,128,128]{4,3,2,1,0:T(8,128)(2,1)}, bf16[16,1,2,128,128]{4,3,2,1,0:T(8,128)(2,1)S(1)}, u32[]{:S(2)}, u32[]{:S(2)}) %collective-permute-start) | collective-permute-done | bytes 1048608 | tf_op jit(solution)/shard_map/ppermute | solution.py:308
  121.1 0.4 collective-permute-start.2
  121.5 1.5 collective-permute-done.1.refs_4_
  123.1 2.3 %collective-permute-start.3 = (bf16[8,1,2,128,128]{4,3,2,1,0:T(8,128)(2,1)S(1)}, bf16[8,1,2,128,128]{4,3,2,1,0:T(8,128)(2,1)S(1)}, u32[]{:S(2)}, u32[]{:S(2)}) collective-permute-start(bf16[8,1,2,128,128]{4,3,2,1,0:T(8,128)(2,1)S(1)} %slice.21), channel_id=1, source_target_pairs={{0,6},{2,0},{4,2},{6,4},{1,7},{3,1},{5,3},{7,5},{8,14},{10,8},{12,... | collective-permute-start | bytes 1572872 | tf_op jit(solution)/shard_map/ppermute | solution.py:311
  125.4 3.6 %all-to-all-start.2 = ((bf16[16,1,1,128,128]{4,3,2,1,0:T(8,128)(2,1)}), bf16[16,1,1,128,128]{4,3,2,1,0:T(8,128)(2,1)S(1)}, u32[]{:S(2)}, u32[]{:S(2)}) async-start(bf16[16,1,1,128,128]{4,3,2,1,0:T(8,128)(2,1)} %get-tuple-element.16), calls=%async_computation.2 | async-start | bytes 1048576 | tf_op jit(solution)/shard_map/all_to_all | solution.py:349
  129.7 1.3 convolution_reduce_fusion
  131.0 1.1 fusion
  132.1 0.8 add_bitcast_fusion
  133.2 2.1 slice.23
  135.3 2.1 slice.24
  137.4 3.2 %collective-permute-start.7 = (bf16[4,3,2,128,128]{4,3,2,1,0:T(8,128)(2,1)}, bf16[4,3,2,128,128]{4,3,2,1,0:T(8,128)(2,1)}, u32[]{:S(2)}, u32[]{:S(2)}) collective-permute-start(bf16[4,3,2,128,128]{4,3,2,1,0:T(8,128)(2,1)} %slice.24), channel_id=1, source_target_pairs={{0,6},{2,0},{4,2},{6,4},{1,7},{3,1},{5,3},{7,5},{8,14},{10,8},{12,... | collective-permute-start | bytes 2359304 | tf_op jit(solution)/shard_map/ppermute | solution.py:311
  140.7 0.5 collective-permute-start.12
  141.7 0.8 broadcast_in_dim.24.refs_1_
  142.5 22.6 %shard_map.102 = bf16[16,1,128,128]{3,2,1,0:T(8,128)(2,1)} custom-call(bf16[16,1,1,128,128]{4,3,2,1,0:T(8,128)(2,1)} %copy-done.2, f32[1,128,128]{2,1,0:T(8,128)} %broadcast_in_dim.24.refs_1_, bf16[16,1,2,128,128]{4,3,2,1,0:T(8,128)(2,1)} %all-to-all-done.refs_2_, bf16[16,1,2,128,128]{4,3,2,1,0:T(8,128)(2,1)} %copy-done.3, ...), custom_call_target="tpu_custom_call" | custom-call | flops 17179869184 | bytes 4194304 | tf_op jit(solution)/shard_map/pallas_call | solution.py:251
  165.1 5.5 %all-to-all-start.3 = ((bf16[16,1,128,128]{3,2,1,0:T(8,128)(2,1)}), bf16[16,1,128,128]{3,2,1,0:T(8,128)(2,1)S(1)}, u32[]{:S(2)}, u32[]{:S(2)}) async-start(bf16[16,1,128,128]{3,2,1,0:T(8,128)(2,1)} %shard_map.102), calls=%async_computation.3 | async-start | bytes 1048576 | tf_op jit(solution)/shard_map/all_to_all | solution.py:357
  170.6 0.5 collective-permute-start.8
  171.2 0.8 broadcast_in_dim.26.refs_1_
  172.0 26.4 %shard_map.103 = (f32[3,16,1024]{2,1,0:T(8,128)}, f32[3,128,1024]{2,1,0:T(8,128)}) custom-call(bf16[8,3,3,128,128]{4,3,2,1,0:T(8,128)(2,1)} %copy-done, f32[3,128,128]{2,1,0:T(8,128)} %broadcast_in_dim.26.refs_1_, bf16[8,3,2,128,128]{4,3,2,1,0:T(8,128)(2,1)} %slice.22.refs_2_, bf16[8,3,2,128,128]{4,3,2,1,0:T(8,128)(2,1)} %collective-permute-done.4.refs_3_, ...), custom_call_target="tpu_custom_call" | custom-call | flops 19327352832 | bytes 9437184 | tf_op jit(solution)/shard_map/pallas_call | solution.py:251
  198.4 12.4 %shard_map.104 = bf16[8,3,128,128]{3,2,1,0:T(8,128)(2,1)} custom-call(bf16[8,3,3,128,128]{4,3,2,1,0:T(8,128)(2,1)} %copy-done, f32[3,128,128]{2,1,0:T(8,128)} %broadcast_in_dim.26.refs_1_, bf16[4,3,2,128,128]{4,3,2,1,0:T(8,128)(2,1)} %collective-permute-done.5.refs_2_, bf16[4,3,2,128,128]{4,3,2,1,0:T(8,128)(2,1)} %collective-permute-done.7.refs_3_, ...), custom_call_target="tpu_custom_call" | custom-call | flops 6442450944 | bytes 3145728 | tf_op jit(solution)/shard_map/pallas_call | solution.py:251
  210.9 18.8 %all_to_all.26.refs_1_ = bf16[8,3,128,128]{3,2,1,0:T(8,128)(2,1)} all-to-all(bf16[8,3,128,128]{3,2,1,0:T(8,128)(2,1)} %shard_map.104), channel_id=1, replica_groups=mesh['expert'=2,'x'=2,'z'=4,'y'=4,'core'=2] {'x','z'}, dimensions={0} | all-to-all | bytes 1572864 | tf_op jit(solution)/shard_map/all_to_all | solution.py:360
  229.7 2.8 %post.1 = bf16[128,5120]{1,0:T(8,128)(2,1)} custom-call(bf16[16,1,128,128]{3,2,1,0:T(8,128)(2,1)} %copy-done.1, bf16[8,3,128,128]{3,2,1,0:T(8,128)(2,1)} %all_to_all.26.refs_1_), custom_call_target="tpu_custom_call" | custom-call | tf_op jit(solution)/shard_map/post/pallas_call | solution.py:293
  (33 shorter events, 1.1 us)
Async XLA Ops:
  4.2 23.1 %all-to-all-start = ((bf16[16,1,2,128,128]{4,3,2,1,0:T(8,128)(2,1)}), bf16[16,1,2,128,128]{4,3,2,1,0:T(8,128)(2,1)}, u32[]{:S(2)}, u32[]{:S(2)}) async-start(bf16[16,1,2,128,128]{4,3,2,1,0:T(8,128)(2,1)} %shard_map.101), calls=%async_computation | async-start | bytes 2097152 | tf_op jit(solution)/shard_map/all_to_all | solution.py:342
  60.8 1.9 copy-start
  62.7 70.4 %collective-permute-start.4 = (bf16[8,3,2,128,128]{4,3,2,1,0:T(8,128)(2,1)}, bf16[8,3,2,128,128]{4,3,2,1,0:T(8,128)(2,1)}, u32[]{:S(2)}, u32[]{:S(2)}) collective-permute-start(bf16[8,3,2,128,128]{4,3,2,1,0:T(8,128)(2,1)} %slice.22.refs_2_), channel_id=1, source_target_pairs={{0,2},{2,4},{4,6},{6,0},{1,3},{3,5},{5,7},{7,1},{8,10},{10,12},{12... | collective-permute-start | bytes 4718600 | tf_op jit(solution)/shard_map/ppermute | solution.py:308
  64.3 56.8 %collective-permute-start = (bf16[16,1,2,128,128]{4,3,2,1,0:T(8,128)(2,1)}, bf16[16,1,2,128,128]{4,3,2,1,0:T(8,128)(2,1)S(1)}, u32[]{:S(2)}, u32[]{:S(2)}) collective-permute-start(bf16[16,1,2,128,128]{4,3,2,1,0:T(8,128)(2,1)} %all-to-all-done.refs_2_), channel_id=1, source_target_pairs={{0,2},{2,4},{4,6},{6,0},{1,3},{3,5},{5,7},{7,1},{8,10},{10,12},{12... | collective-permute-start | bytes 3145736 | tf_op jit(solution)/shard_map/ppermute | solution.py:308
  65.9 69.4 %collective-permute-start.6 = (bf16[8,3,2,128,128]{4,3,2,1,0:T(8,128)(2,1)}, bf16[8,3,2,128,128]{4,3,2,1,0:T(8,128)(2,1)}, u32[]{:S(2)}, u32[]{:S(2)}) collective-permute-start(bf16[8,3,2,128,128]{4,3,2,1,0:T(8,128)(2,1)} %slice.22.refs_2_), channel_id=1, source_target_pairs={{0,6},{2,0},{4,2},{6,4},{1,7},{3,1},{5,3},{7,5},{8,14},{10,8},{12,... | collective-permute-start | bytes 4718600 | tf_op jit(solution)/shard_map/ppermute | solution.py:309
  67.6 55.5 %collective-permute-start.1 = (bf16[16,1,2,128,128]{4,3,2,1,0:T(8,128)(2,1)}, bf16[16,1,2,128,128]{4,3,2,1,0:T(8,128)(2,1)S(1)}, u32[]{:S(2)}, u32[]{:S(2)}) collective-permute-start(bf16[16,1,2,128,128]{4,3,2,1,0:T(8,128)(2,1)} %all-to-all-done.refs_2_), channel_id=1, source_target_pairs={{0,6},{2,0},{4,2},{6,4},{1,7},{3,1},{5,3},{7,5},{8,14},{10,8},{12,... | collective-permute-start | bytes 3145736 | tf_op jit(solution)/shard_map/ppermute | solution.py:309
  121.1 4.3 %copy-start.3 = (bf16[16,1,2,128,128]{4,3,2,1,0:T(8,128)(2,1)}, bf16[16,1,2,128,128]{4,3,2,1,0:T(8,128)(2,1)S(1)}, u32[]{:S(2)}) copy-start(bf16[16,1,2,128,128]{4,3,2,1,0:T(8,128)(2,1)S(1)} %collective-permute-done.refs_3_) | copy-start | bytes 3145732
  121.1 19.5 %collective-permute-start.2 = (bf16[8,1,2,128,128]{4,3,2,1,0:T(8,128)(2,1)S(1)}, bf16[8,1,2,128,128]{4,3,2,1,0:T(8,128)(2,1)S(1)}, u32[]{:S(2)}, u32[]{:S(2)}) collective-permute-start(bf16[8,1,2,128,128]{4,3,2,1,0:T(8,128)(2,1)S(1)} %slice.20), channel_id=1, source_target_pairs={{0,2},{2,4},{4,6},{6,0},{1,3},{3,5},{5,7},{7,1},{8,10},{10,12},{12... | collective-permute-start | bytes 1572872 | tf_op jit(solution)/shard_map/ppermute | solution.py:310
  123.0 2.4 %copy-start.4 = (bf16[16,1,2,128,128]{4,3,2,1,0:T(8,128)(2,1)}, bf16[16,1,2,128,128]{4,3,2,1,0:T(8,128)(2,1)S(1)}, u32[]{:S(2)}) copy-start(bf16[16,1,2,128,128]{4,3,2,1,0:T(8,128)(2,1)S(1)} %collective-permute-done.1.refs_4_) | copy-start | bytes 3145732
  123.1 17.6 %collective-permute-start.3 = (bf16[8,1,2,128,128]{4,3,2,1,0:T(8,128)(2,1)S(1)}, bf16[8,1,2,128,128]{4,3,2,1,0:T(8,128)(2,1)S(1)}, u32[]{:S(2)}, u32[]{:S(2)}) collective-permute-start(bf16[8,1,2,128,128]{4,3,2,1,0:T(8,128)(2,1)S(1)} %slice.21), channel_id=1, source_target_pairs={{0,6},{2,0},{4,2},{6,4},{1,7},{3,1},{5,3},{7,5},{8,14},{10,8},{12,... | collective-permute-start | bytes 1572872 | tf_op jit(solution)/shard_map/ppermute | solution.py:311
  125.4 15.8 %all-to-all-start.2 = ((bf16[16,1,1,128,128]{4,3,2,1,0:T(8,128)(2,1)}), bf16[16,1,1,128,128]{4,3,2,1,0:T(8,128)(2,1)S(1)}, u32[]{:S(2)}, u32[]{:S(2)}) async-start(bf16[16,1,1,128,128]{4,3,2,1,0:T(8,128)(2,1)} %get-tuple-element.16), calls=%async_computation.2 | async-start | bytes 1048576 | tf_op jit(solution)/shard_map/all_to_all | solution.py:349
  132.9 38.3 %collective-permute-start.10 = (bf16[8,3,2,128,128]{4,3,2,1,0:T(8,128)(2,1)}, bf16[8,3,2,128,128]{4,3,2,1,0:T(8,128)(2,1)}, u32[]{:S(2)}, u32[]{:S(2)}) collective-permute-start(bf16[8,3,2,128,128]{4,3,2,1,0:T(8,128)(2,1)} %slice.22.refs_2_), channel_id=1, source_target_pairs={{0,1},{1,0},{2,3},{3,2},{4,5},{5,4},{6,7},{7,6},{8,9},{9,8},{10,11... | collective-permute-start | bytes 4718600 | tf_op jit(solution)/shard_map/ppermute | solution.py:351
  135.3 35.3 %collective-permute-start.5 = (bf16[4,3,2,128,128]{4,3,2,1,0:T(8,128)(2,1)}, bf16[4,3,2,128,128]{4,3,2,1,0:T(8,128)(2,1)}, u32[]{:S(2)}, u32[]{:S(2)}) collective-permute-start(bf16[4,3,2,128,128]{4,3,2,1,0:T(8,128)(2,1)} %slice.23), channel_id=1, source_target_pairs={{0,2},{2,4},{4,6},{6,0},{1,3},{3,5},{5,7},{7,1},{8,10},{10,12},{12... | collective-permute-start | bytes 2359304 | tf_op jit(solution)/shard_map/ppermute | solution.py:310
  137.4 33.7 %collective-permute-start.7 = (bf16[4,3,2,128,128]{4,3,2,1,0:T(8,128)(2,1)}, bf16[4,3,2,128,128]{4,3,2,1,0:T(8,128)(2,1)}, u32[]{:S(2)}, u32[]{:S(2)}) collective-permute-start(bf16[4,3,2,128,128]{4,3,2,1,0:T(8,128)(2,1)} %slice.24), channel_id=1, source_target_pairs={{0,6},{2,0},{4,2},{6,4},{1,7},{3,1},{5,3},{7,5},{8,14},{10,8},{12,... | collective-permute-start | bytes 2359304 | tf_op jit(solution)/shard_map/ppermute | solution.py:311
  140.7 0.8 copy-start.5
  140.7 30.6 %collective-permute-start.11 = (bf16[8,3,2,128,128]{4,3,2,1,0:T(8,128)(2,1)}, bf16[8,3,2,128,128]{4,3,2,1,0:T(8,128)(2,1)}, u32[]{:S(2)}, u32[]{:S(2)}) collective-permute-start(bf16[8,3,2,128,128]{4,3,2,1,0:T(8,128)(2,1)} %collective-permute-done.4.refs_3_), channel_id=1, source_target_pairs={{0,1},{1,0},{2,3},{3,2},{4,5},{5,4},{6,7},{7,6},{8,9},{9,8},{10,11... | collective-permute-start | bytes 4718600 | tf_op jit(solution)/shard_map/ppermute | solution.py:351
  140.7 1.0 copy-start.6
  140.7 30.5 %collective-permute-start.12 = (bf16[8,3,2,128,128]{4,3,2,1,0:T(8,128)(2,1)}, bf16[8,3,2,128,128]{4,3,2,1,0:T(8,128)(2,1)}, u32[]{:S(2)}, u32[]{:S(2)}) collective-permute-start(bf16[8,3,2,128,128]{4,3,2,1,0:T(8,128)(2,1)} %collective-permute-done.6.refs_4_), channel_id=1, source_target_pairs={{0,1},{1,0},{2,3},{3,2},{4,5},{5,4},{6,7},{7,6},{8,9},{9,8},{10,11... | collective-permute-start | bytes 4718600 | tf_op jit(solution)/shard_map/ppermute | solution.py:351
  141.7 0.8 copy-start.2
  165.1 45.7 %all-to-all-start.3 = ((bf16[16,1,128,128]{3,2,1,0:T(8,128)(2,1)}), bf16[16,1,128,128]{3,2,1,0:T(8,128)(2,1)S(1)}, u32[]{:S(2)}, u32[]{:S(2)}) async-start(bf16[16,1,128,128]{3,2,1,0:T(8,128)(2,1)} %shard_map.102), calls=%async_computation.3 | async-start | bytes 1048576 | tf_op jit(solution)/shard_map/all_to_all | solution.py:357
  170.6 27.8 %collective-permute-start.8 = (bf16[4,3,2,128,128]{4,3,2,1,0:T(8,128)(2,1)}, bf16[4,3,2,128,128]{4,3,2,1,0:T(8,128)(2,1)}, u32[]{:S(2)}, u32[]{:S(2)}) collective-permute-start(bf16[4,3,2,128,128]{4,3,2,1,0:T(8,128)(2,1)} %collective-permute-done.5.refs_2_), channel_id=1, source_target_pairs={{0,1},{1,0},{2,3},{3,2},{4,5},{5,4},{6,7},{7,6},{8,9},{9,8},{10,11... | collective-permute-start | bytes 2359304 | tf_op jit(solution)/shard_map/ppermute | solution.py:352
  171.1 27.3 %collective-permute-start.9 = (bf16[4,3,2,128,128]{4,3,2,1,0:T(8,128)(2,1)}, bf16[4,3,2,128,128]{4,3,2,1,0:T(8,128)(2,1)}, u32[]{:S(2)}, u32[]{:S(2)}) collective-permute-start(bf16[4,3,2,128,128]{4,3,2,1,0:T(8,128)(2,1)} %collective-permute-done.7.refs_3_), channel_id=1, source_target_pairs={{0,1},{1,0},{2,3},{3,2},{4,5},{5,4},{6,7},{7,6},{8,9},{9,8},{10,11... | collective-permute-start | bytes 2359304 | tf_op jit(solution)/shard_map/ppermute | solution.py:352
  210.9 18.8 %copy-start.1 = (bf16[16,1,128,128]{3,2,1,0:T(8,128)(2,1)}, bf16[16,1,128,128]{3,2,1,0:T(8,128)(2,1)S(1)}, u32[]{:S(2)}) copy-start(bf16[16,1,128,128]{3,2,1,0:T(8,128)(2,1)S(1)} %all-to-all-done.3.refs_0_) | copy-start | bytes 1572868
where the time goes:
time: 233 us; the launch traced here: 232 us
  Pallas kernels  75.9 us (33%)
  waiting for transfers between devices  63.6 us (27%)
  blocking collectives  52.4 us (22%)
  starting transfers between devices  28.2 us (12%)
  local copies, waits for them, and re-layouts  8.35 us (4%)
  matrix products  2.4 us (1%)
    pallas_call x3, Pallas kernels, attend(): pl.pallas_call(functools.partial(attend_kernel, sizes=sizes, shifts=shift...  61.4 us
    ppermute x2, waiting for transfers between devices, ring(): up = lax.ppermute(pair, axis, shift(axis, 1))  53.1 us
    all_to_all x1, blocking collectives, block_attention(): b = spread(b, narrow)  33.5 us
    all_to_all x1, blocking collectives, block_attention(): out_b = spread(out_b, narrow)  18.8 us
    pallas_call x2, Pallas kernels, prepare(): pl.pallas_call(functools.partial(prep_kernel, tensors=kinds, plan=plan),...  11.7 us
    all_to_all x1, waiting for transfers between devices, block_attention(): a = spread(a, wide)  9.03 us
    all_to_all x1, starting transfers between devices, block_attention(): a = spread(a, wide)  6.52 us
    ppermute x2, starting transfers between devices, ring(): down_far = lax.ppermute(down[half:], axis, shift(axis, -1))  5.56 us
  transfers between devices with their start and end apart: 16, of which 3 were waited for; matrix products, arithmetic and copies ran while one was open for 4% of the time, Pallas kernels for 30%

commit v1 on v0

--- a/solution.py
+++ b/solution.py
@@ -17,6 +17,8 @@
 WID = 32
 EPSILON = 1e-06
 LOG2E = 1.4426950408889634
+SMALLEST = 2.0**-80
+LARGEST = 2.0**100
 SCALE = LOG2E / math.sqrt(HEAD_DIM)
 VMEM_BYTES = 63 * 1024 * 1024
 F32 = jnp.float32
@@ -135,7 +137,7 @@
     )(block, jnp.asarray(inverse)[None, :], *[tensors[k][0] for k in kinds], *gains)
 
 
-def attend_kernel(*refs, sizes, shifts, resume, final, tk, sub):
+def attend_kernel(*refs, sizes, resume, final, sub, together):
     count = len(sizes)
     q_ref, gate_ref = refs[:2]
     pieces = refs[2:2 + count]
@@ -149,122 +151,159 @@
     else:
         stat_out, mixed_out = refs[at:at + 2]
         at += 2
-    k_bufs, v_bufs, s_buf, sems = refs[at:]
-    head = pl.program_id(0)
-    slot = head % 2
-
-    def loads(head, slot):
+    k_bufs, v_bufs, sems = refs[at:]
+    group = pl.program_id(0)
+    base = (group % 2) * together
+
+    def loads(group, base):
         copies = []
-        offset = 0
-        for i, size in enumerate(sizes):
-            for j, buf in enumerate((k_bufs, v_bufs)):
-                copies.append(pltpu.make_async_copy(
-                    pieces[i].at[:, head, shifts[i] + j], buf.at[slot, pl.ds(offset, size)],
-                    sems.at[slot, 2 * i + j]))
-            offset += size
+        for h in range(together):
+            offset = 0
+            for i, size in enumerate(sizes):
+                for j, buf in enumerate((k_bufs, v_bufs)):
+                    copies.append(pltpu.make_async_copy(
+                        pieces[i].at[:, group * together + h, j],
+                        buf.at[base + h, pl.ds(offset, size)],
+                        sems.at[base + h, 2 * i + j]))
+                offset += size
         return copies
 
     @pl.when(pl.program_id(1) == 0)
     def _():
-        @pl.when(head == 0)
+        @pl.when(group == 0)
         def _():
-            for copy in loads(head, slot):
+            for copy in loads(group, base):
                 copy.start()
 
-        @pl.when(head + 1 < pl.num_programs(0))
+        @pl.when(group + 1 < pl.num_programs(0))
         def _():
-            for copy in loads(head + 1, 1 - slot):
+            for copy in loads(group + 1, together - base):
                 copy.start()
 
-        for copy in loads(head, slot):
+        for copy in loads(group, base):
             copy.wait()
 
-    k_buf, v_buf = k_bufs.at[slot], v_bufs.at[slot]
     tiles = q_ref.shape[0]
     tq = tiles * HEAD_DIM
-    q = jnp.concatenate([q_ref[t, 0, 0] for t in range(tiles)], axis=1).astype(F32) * SCALE
-    q_high = q.astype(BF16)
-    q_low = (q - q_high.astype(F32)).astype(BF16)
-    q_both = jnp.concatenate([q_high, q_low], axis=0)
-    blocks = sum(sizes) * HEAD_DIM // tk
-    subs = tk // sub
+    key_tiles = sum(sizes)
     per_sub = sub // HEAD_DIM
-
-    def scores(j, i):
-        first = (j * subs + i) * per_sub
-        k = k_buf[first:first + per_sub].reshape(sub, HEAD_DIM)
-        s = jnp.dot(jnp.concatenate([k, k], axis=1), q_both, preferred_element_type=F32)
-        s_buf[j % 2, i * sub:(i + 1) * sub, :] = s
-        return jnp.max(s.reshape(sub // 8, 8, tq), axis=0)
-
-    top = scores(0, 0)
-    for i in range(1, subs):
-        top = jnp.maximum(top, scores(0, i))
-    if resume:
-        peak = stat_in[0, 0:1, :]
-        total = stat_in[0, 8:16, :]
-        mixed = mixed_in[0]
-    else:
-        peak = jnp.full((1, tq), -1e30, F32)
-        total = jnp.zeros((8, tq), F32)
-        mixed = jnp.zeros((HEAD_DIM, tq), F32)
-    for j in range(blocks):
-        new_peak = jnp.maximum(peak, jnp.max(top, axis=0, keepdims=True))
-        shrink = jnp.exp2(peak - new_peak)
-        total = total * shrink
-        part = None
-        top = None
-        for i in range(subs):
-            if j + 1 < blocks:
-                t = scores(j + 1, i)
-                top = t if top is None else jnp.maximum(top, t)
-            e = jnp.exp2(s_buf[j % 2, i * sub:(i + 1) * sub, :] - new_peak)
-            total = total + jnp.sum(e.reshape(sub // 8, 8, tq), axis=0)
-            first = (j * subs + i) * per_sub
-            v = jnp.concatenate([v_buf[first + t] for t in range(per_sub)], axis=1)
-            d = jnp.dot(v, e.astype(BF16), preferred_element_type=F32)
-            part = d if part is None else part + d
-        mixed = mixed * shrink + part
-        peak = new_peak
-    if final:
-        out = mixed / jnp.sum(total, axis=0, keepdims=True)
-        gate = gate_ref[0]
-        for t in range(tiles):
-            o_ref[t, 0] = (out[:, t * HEAD_DIM:(t + 1) * HEAD_DIM] * gate).astype(BF16)
-    else:
-        stat_out[0, 0:8, :] = jnp.broadcast_to(peak, (8, tq))
-        stat_out[0, 8:16, :] = total
-        mixed_out[0] = mixed
-
-
-def attend(query, gate, pieces, state=None, final=True, tq=512, tk=1024, sub=1024):
+    subs = key_tiles // per_sub
+
+    def scaled(q):
+        q = q.astype(F32) * SCALE
+        high = q.astype(BF16)
+        low = (q - high.astype(F32)).astype(BF16)
+        return jnp.concatenate([high, low], axis=0)
+
+    def scores(h, first, count, q_both):
+        k = k_bufs[base + h, pl.ds(first, count)].reshape(count * HEAD_DIM, HEAD_DIM)
+        return jnp.dot(jnp.concatenate([k, k], axis=1), q_both, preferred_element_type=F32)
+
+    def weighted(h, first, count, e):
+        v = jnp.concatenate([v_bufs[base + h, first + t] for t in range(count)], axis=1)
+        return jnp.dot(v, e.astype(BF16), preferred_element_type=F32)
+
+    def emit(h, tile, out):
+        o_ref[tile, h] = (out * gate_ref[h]).astype(BF16)
+
+    queries = [scaled(jnp.concatenate([q_ref[t, h, 0] for t in range(tiles)], axis=1))
+               for h in range(together)]
+    items = [(h, j) for h in range(together) for j in range(subs)]
+    safe = None
+    s = scores(0, 0, per_sub, queries[0])
+    for n, (h, j) in enumerate(items):
+        after = None
+        if n + 1 < len(items):
+            nh, nj = items[n + 1]
+            after = scores(nh, nj * per_sub, per_sub, queries[nh])
+        if j == 0:
+            total = jnp.zeros((8, tq), F32)
+            mixed = None
+        e = jnp.exp2(s)
+        total = total + jnp.sum(e.reshape(sub // 8, 8, tq), axis=0)
+        d = weighted(h, j * per_sub, per_sub, e)
+        mixed = d if mixed is None else mixed + d
+        s = after
+        if j + 1 < subs:
+            continue
+        if resume:
+            total = total + stat_in[h, 8:16, :]
+            mixed = mixed + mixed_in[h]
+        row = jnp.sum(total, axis=0, keepdims=True)
+        fine = (row > SMALLEST) & (row < LARGEST)
+        if resume:
+            fine = fine & (stat_in[h, 0:1, :] == 0.0)
+        fine = jnp.where(fine, 1.0, 0.0)
+        safe = fine if safe is None else jnp.minimum(safe, fine)
+        if final:
+            out = mixed / row
+            for t in range(tiles):
+                emit(h, t, out[:, t * HEAD_DIM:(t + 1) * HEAD_DIM])
+        else:
+            stat_out[h, 0:8, :] = jnp.zeros((8, tq), F32)
+            stat_out[h, 8:16, :] = total
+            mixed_out[h] = mixed
+
+    @pl.when(jnp.min(safe) < 0.5)
+    def _():
+        def one_tile(n, carry):
+            h = n // tiles
+            t = n % tiles
+            q_tile = scaled(q_ref[t, h, 0])
+            lanes = pl.ds(pl.multiple_of(t * HEAD_DIM, HEAD_DIM), HEAD_DIM)
+            if resume:
+                state = (stat_in[h, 0:1, lanes], stat_in[h, 8:16, lanes], mixed_in[h, :, lanes])
+            else:
+                state = (jnp.full((1, HEAD_DIM), -1e30, F32), jnp.zeros((8, HEAD_DIM), F32),
+                         jnp.zeros((HEAD_DIM, HEAD_DIM), F32))
+
+            def one_block(j, state):
+                peak, total, mixed = state
+                s = scores(h, j * 8, 8, q_tile)
+                new_peak = jnp.maximum(peak, jnp.max(s, axis=0, keepdims=True))
+                shrink = jnp.exp2(peak - new_peak)
+                e = jnp.exp2(s - new_peak)
+                total = total * shrink + jnp.sum(e.reshape(HEAD_DIM, 8, HEAD_DIM), axis=0)
+                return new_peak, total, mixed * shrink + weighted(h, j * 8, 8, e)
+
+            peak, total, mixed = lax.fori_loop(0, key_tiles // 8, one_block, state)
+            if final:
+                emit(h, t, mixed / jnp.sum(total, axis=0, keepdims=True))
+            else:
+                stat_out[h, 0:8, lanes] = jnp.broadcast_to(peak, (8, HEAD_DIM))
+                stat_out[h, 8:16, lanes] = total
+                mixed_out[h, :, lanes] = mixed
+            return carry
+
+        lax.fori_loop(0, together * tiles, one_tile, 0)
+
+
+def attend(query, gate, pieces, state=None, final=True, tq=1024, sub=512, together=1):
     sizes = tuple(p.shape[0] for p in pieces)
-    shifts = tuple(p.shape[2] - 2 for p in pieces)
     query_tiles, heads = query.shape[:2]
     step = tq // HEAD_DIM
     keys = sum(sizes)
-    slots = min(heads, 2)
-    state_specs = [pl.BlockSpec((1, 16, tq), lambda h, i: (h, 0, i)),
-                   pl.BlockSpec((1, HEAD_DIM, tq), lambda h, i: (h, 0, i))]
+    slots = together * min(heads // together, 2)
+    state_specs = [pl.BlockSpec((together, 16, tq), lambda h, i: (h, 0, i)),
+                   pl.BlockSpec((together, HEAD_DIM, tq), lambda h, i: (h, 0, i))]
     state_shapes = [jax.ShapeDtypeStruct((heads, 16, query_tiles * HEAD_DIM), F32),
                     jax.ShapeDtypeStruct((heads, HEAD_DIM, query_tiles * HEAD_DIM), F32)]
     return pl.pallas_call(
-        functools.partial(attend_kernel, sizes=sizes, shifts=shifts,
-                          resume=state is not None, final=final, tk=tk, sub=sub),
-        grid=(heads, query_tiles // step),
+        functools.partial(attend_kernel, sizes=sizes, resume=state is not None, final=final,
+                          sub=sub, together=together),
+        grid=(heads // together, query_tiles // step),
         in_specs=[
-            pl.BlockSpec((step, 1, 1, HEAD_DIM, HEAD_DIM), lambda h, i: (i, h, 0, 0, 0)),
-            pl.BlockSpec((1, HEAD_DIM, HEAD_DIM), lambda h, i: (h, 0, 0)),
+            pl.BlockSpec((step, together, 1, HEAD_DIM, HEAD_DIM), lambda h, i: (i, h, 0, 0, 0)),
+            pl.BlockSpec((together, HEAD_DIM, HEAD_DIM), lambda h, i: (h, 0, 0)),
         ] + [pl.BlockSpec(memory_space=pl.ANY) for _ in pieces]
         + (state_specs if state is not None else []),
-        out_specs=(pl.BlockSpec((step, 1, HEAD_DIM, HEAD_DIM), lambda h, i: (i, h, 0, 0))
+        out_specs=(pl.BlockSpec((step, together, HEAD_DIM, HEAD_DIM), lambda h, i: (i, h, 0, 0))
                    if final else state_specs),
         out_shape=(jax.ShapeDtypeStruct((query_tiles, heads, HEAD_DIM, HEAD_DIM), BF16)
                    if final else state_shapes),
         scratch_shapes=[
             pltpu.VMEM((slots, keys, HEAD_DIM, HEAD_DIM), BF16),
             pltpu.VMEM((slots, keys, HEAD_DIM, HEAD_DIM), BF16),
-            pltpu.VMEM((2, tk, tq), F32),
             pltpu.SemaphoreType.DMA((slots, 2 * len(pieces))),
         ],
         compiler_params=pltpu.CompilerParams(vmem_limit_bytes=VMEM_BYTES),
@@ -293,7 +332,7 @@
     return pl.pallas_call(
         post_kernel,
         out_shape=jax.ShapeDtypeStruct((tokens, width), BF16),
-        compiler_params=pltpu.CompilerParams(vmem_limit_bytes=VMEM_BYTES),
+        compiler_params=pltpu.CompilerParams(vmem_limit_bytes=16 * 1024 * 1024),
         name="post",
     )(*parts)
 
@@ -303,13 +342,14 @@
     return [(i, (i + amount) % size) for i in range(size)]
 
 
-def ring(pair, axis):
-    half = pair.shape[0] // 2
-    up = lax.ppermute(pair, axis, shift(axis, 1))
-    down = lax.ppermute(pair, axis, shift(axis, -1))
-    up_far = lax.ppermute(up[:half], axis, shift(axis, 1))
-    down_far = lax.ppermute(down[half:], axis, shift(axis, -1))
-    return [up, down, up_far, down_far]
+def ring(low, high, axis):
+    up_low = lax.ppermute(low, axis, shift(axis, 1))
+    down_high = lax.ppermute(high, axis, shift(axis, -1))
+    up_high = lax.ppermute(high, axis, shift(axis, 1))
+    down_low = lax.ppermute(low, axis, shift(axis, -1))
+    up_far = lax.ppermute(up_low, axis, shift(axis, 1))
+    down_far = lax.ppermute(down_high, axis, shift(axis, -1))
+    return [up_low, down_high, up_high, down_low], [up_far, down_far]
 
 
 def gates(timestep, gate_base, time_weight, first, count):
@@ -337,26 +377,34 @@
     q, k, v = (queries, query_gain), (keys, key_gain), (values, None)
 
     (a,) = prepare(4, block, {"k": k, "v": v}, ((0, 4, 1, "kv"),))
-    a_query, b = prepare(8, block, {"q": q, "k": k, "v": v},
-                         ((0, 2, 1, "q"), (16, 1, 3, "qkv")))
+    b, a_query, b_query = prepare(8, block, {"q": q, "k": k, "v": v},
+                                  ((16, 1, 3, "kv"), (0, 2, 1, "q"), (16, 1, 3, "q")))
     a = spread(a, wide)
-    ring_a = ring(a, "y")
+    up_a = lax.ppermute(a, "y", shift("y", 1))
+    down_a = lax.ppermute(a, "y", shift("y", -1))
+    far_a = [lax.ppermute(up_a[:8], "y", shift("y", 1)),
+             lax.ppermute(down_a[8:], "y", shift("y", -1))]
     b, a = lax.optimization_barrier((b, a))
     b = spread(b, narrow)
-    own_b = b[:, :, 1:]
-    ring_b = ring(own_b, "y")
+    own_b = [b[:4], b[4:]]
+    near_b, far_b = ring(*own_b, "y")
     a_query, b = lax.optimization_barrier((a_query, b))
     a_query = spread(a_query, wide)
-    near_b = [own_b] + ring_b[:2]
-    near_b = near_b + [lax.ppermute(p, "core", shift("core", 1)) for p in near_b]
-    far_b = ring_b[2:] + [lax.ppermute(p, "core", shift("core", 1)) for p in ring_b[2:]]
+    b_query, a_query = lax.optimization_barrier((b_query, a_query))
+    b_query = spread(b_query, narrow)
+
+    def other(parts):
+        return [lax.ppermute(p, "core", shift("core", 1)) for p in parts]
+
+    near_b = [b] + near_b + other(own_b) + other(near_b)
+    far_b = far_b + other(far_b)
     gate_a = gate_of((x * 4 + z) * 2 + core, 1)
     gate_b = gate_of(16 + (x * 4 + z) * 3, 3)
 
-    out_a = attend(a_query, gate_a, [a] + ring_a)
+    out_a = attend(a_query, gate_a, [a, up_a, down_a] + far_a)
     out_a = spread(out_a, wide)
-    state = attend(b, gate_b, near_b, final=False)
-    out_b = attend(b, gate_b, far_b, state)
+    state = attend(b_query, gate_b, near_b, final=False)
+    out_b = attend(b_query, gate_b, far_b, state, together=3)
     out_b = spread(out_b, narrow)
     return collect(out_a, out_b)
 

time: 233 us -> 253 us (1.086)
  the two profiles are of different devices: /device:TPU:0 before, /device:TPU:24 now
where the time goes in v1:
time: 253 us; the launch traced here: 252 us
  blocking collectives  83.2 us (33%)
  Pallas kernels  60.8 us (24%)
  waiting for transfers between devices  58.1 us (23%)
  starting transfers between devices  40.5 us (16%)
  local copies, waits for them, and re-layouts  5.22 us (2%)
    all_to_all x1, blocking collectives, block_attention(): out_b = spread(out_b, narrow)  83.2 us
    pallas_call x3, Pallas kernels, attend(): pl.pallas_call(functools.partial(attend_kernel, sizes=sizes, resume=state...  47.7 us
    ppermute x1, waiting for transfers between devices, block_attention(): lax.ppermute(up_a[:8], 'y', shift('y', 1))  22.1 us
    all_to_all x1, waiting for transfers between devices, block_attention(): b = spread(b, narrow)  18.2 us
    pallas_call x2, Pallas kernels, prepare(): pl.pallas_call(functools.partial(prep_kernel, tensors=kinds, plan=plan),...  11.7 us
    all_to_all x1, waiting for transfers between devices, block_attention(): a = spread(a, wide)  9.08 us
    all_to_all x1, waiting for transfers between devices, block_attention(): a_query = spread(a_query, wide)  6.92 us
    all_to_all x1, starting transfers between devices, block_attention(): a_query = spread(a_query, wide)  6.48 us
  transfers between devices with their start and end apart: 23, of which 6 were waited for; matrix products, arithmetic and copies ran while one was open for 3% of the time, Pallas kernels for 22%

profile of v1, /device:TPU:24, one launch (start us, length us, event | category | flops | bytes accessed | tf_op | source)
XLA Modules:
  0.0 251.9 jit_solution(1992204796091974885)
XLA Ops:
  0.0 4.1 %shard_map.101 = bf16[16,1,2,128,128]{4,3,2,1,0:T(8,128)(2,1)} custom-call(s32[1]{0:T(128)} %bitcast.block_ref, f32[1,128]{1,0:T(1,128)} %constant.38.inv_hbm, bf16[128,5120]{1,0:T(8,128)(2,1)} %refs_0_.3, bf16[128,5120]{1,0:T(8,128)(2,1)} %refs_1_.3, f32[40,128]{1,0:T(8,128)} %bitcast.16), custom_call_target="tpu_custom_call" | custom-call | tf_op jit(solution)/shard_map/pallas_call | solution.py:120
  4.2 6.4 %all-to-all-start = ((bf16[16,1,2,128,128]{4,3,2,1,0:T(8,128)(2,1)}), bf16[16,1,2,128,128]{4,3,2,1,0:T(8,128)(2,1)}, u32[]{:S(2)}, u32[]{:S(2)}) async-start(bf16[16,1,2,128,128]{4,3,2,1,0:T(8,128)(2,1)} %shard_map.101), calls=%async_computation | async-start | bytes 2097152 | tf_op jit(solution)/shard_map/all_to_all | solution.py:382
  10.6 7.5 %shard_map.100 = (bf16[8,3,2,128,128]{4,3,2,1,0:T(8,128)(2,1)}, bf16[16,1,1,128,128]{4,3,2,1,0:T(8,128)(2,1)}, bf16[8,3,1,128,128]{4,3,2,1,0:T(8,128)(2,1)}) custom-call(s32[1]{0:T(128)} %bitcast.block_ref, f32[1,128]{1,0:T(1,128)} %constant.38.inv_hbm, bf16[128,5120]{1,0:T(8,128)(2,1)} %refs_0_.2, bf16[128,5120]{1,0:T(8,128)(2,1)} %refs_0_.3, ...), custom_call_target="tpu_custom_call" | custom-call | tf_op jit(solution)/shard_map/pallas_call | solution.py:120
  18.1 9.1 %all-to-all-done.refs_2_ = bf16[16,1,2,128,128]{4,3,2,1,0:T(8,128)(2,1)} async-done(((bf16[16,1,2,128,128]{4,3,2,1,0:T(8,128)(2,1)}), bf16[16,1,2,128,128]{4,3,2,1,0:T(8,128)(2,1)}, u32[]{:S(2)}, u32[]{:S(2)}) %all-to-all-start) | async-done | bytes 1048608 | tf_op jit(solution)/shard_map/all_to_all | solution.py:382
  27.2 3.6 %all-to-all-start.1 = ((bf16[8,3,2,128,128]{4,3,2,1,0:T(8,128)(2,1)}), bf16[8,3,2,128,128]{4,3,2,1,0:T(8,128)(2,1)S(1)}, u32[]{:S(2)}, u32[]{:S(2)}) async-start(bf16[8,3,2,128,128]{4,3,2,1,0:T(8,128)(2,1)} %get-tuple-element.19), calls=%async_computation.1 | async-start | bytes 3145728 | tf_op jit(solution)/shard_map/all_to_all | solution.py:388
  31.0 1.8 collective-permute-start.1
  32.8 18.2 %all-to-all-done.1.refs_2_ = bf16[8,3,2,128,128]{4,3,2,1,0:T(8,128)(2,1)S(1)} async-done(((bf16[8,3,2,128,128]{4,3,2,1,0:T(8,128)(2,1)}), bf16[8,3,2,128,128]{4,3,2,1,0:T(8,128)(2,1)S(1)}, u32[]{:S(2)}, u32[]{:S(2)}) %all-to-all-start.1) | async-done | bytes 1572896 | tf_op jit(solution)/shard_map/all_to_all | solution.py:388
  51.1 1.2 fusion.7
  52.7 1.8 collective-permute-start.6
  54.5 1.7 collective-permute-done.refs_3_
  56.2 1.6 collective-permute-start.2
  57.8 1.1 slice.17
  58.9 0.5 collective-permute-start.3
  59.5 2.8 %collective-permute-start.10 = (bf16[4,3,2,128,128]{4,3,2,1,0:T(8,128)(2,1)S(1)}, bf16[4,3,2,128,128]{4,3,2,1,0:T(8,128)(2,1)}, u32[]{:S(2)}, u32[]{:S(2)}) collective-permute-start(bf16[4,3,2,128,128]{4,3,2,1,0:T(8,128)(2,1)S(1)} %get-tuple-element.27), channel_id=1, source_target_pairs={{0,2},{2,4},{4,6},{6,0},{1,3},{3,5},{5,7},{7,1},{8,10},{10,12},{12... | collective-permute-start | bytes 2359304 | tf_op jit(solution)/shard_map/ppermute | solution.py:348
  62.2 22.1 %collective-permute-done.2.refs_5_ = bf16[8,1,2,128,128]{4,3,2,1,0:T(8,128)(2,1)S(1)} collective-permute-done((bf16[8,1,2,128,128]{4,3,2,1,0:T(8,128)(2,1)S(1)}, bf16[8,1,2,128,128]{4,3,2,1,0:T(8,128)(2,1)S(1)}, u32[]{:S(2)}, u32[]{:S(2)}) %collective-permute-start.2) | collective-permute-done | bytes 524320 | tf_op jit(solution)/shard_map/ppermute | solution.py:385
  84.3 0.8 collective-permute-start.11
  85.7 6.5 %all-to-all-start.2 = ((bf16[16,1,1,128,128]{4,3,2,1,0:T(8,128)(2,1)}), bf16[16,1,1,128,128]{4,3,2,1,0:T(8,128)(2,1)S(1)}, u32[]{:S(2)}, u32[]{:S(2)}) async-start(bf16[16,1,1,128,128]{4,3,2,1,0:T(8,128)(2,1)} %get-tuple-element.20), calls=%async_computation.2 | async-start | bytes 1048576 | tf_op jit(solution)/shard_map/all_to_all | solution.py:392
  92.9 1.3 convolution_reduce_fusion
  94.2 1.1 fusion
  95.3 0.8 add_bitcast_fusion
  96.1 6.9 %all-to-all-done.2.refs_0_ = bf16[16,1,1,128,128]{4,3,2,1,0:T(8,128)(2,1)S(1)} async-done(((bf16[16,1,1,128,128]{4,3,2,1,0:T(8,128)(2,1)}), bf16[16,1,1,128,128]{4,3,2,1,0:T(8,128)(2,1)S(1)}, u32[]{:S(2)}, u32[]{:S(2)}) %all-to-all-start.2) | async-done | bytes 524320 | tf_op jit(solution)/shard_map/all_to_all | solution.py:392
  103.0 3.5 %all-to-all-start.4 = ((bf16[8,3,1,128,128]{4,3,2,1,0:T(8,128)(2,1)}), bf16[8,3,1,128,128]{4,3,2,1,0:T(8,128)(2,1)S(1)}, u32[]{:S(2)}, u32[]{:S(2)}) async-start(bf16[8,3,1,128,128]{4,3,2,1,0:T(8,128)(2,1)} %get-tuple-element.23), calls=%async_computation.4 | async-start | bytes 1572864 | tf_op jit(solution)/shard_map/all_to_all | solution.py:394
  106.6 2.6 %collective-permute-start.5 = (bf16[4,3,2,128,128]{4,3,2,1,0:T(8,128)(2,1)}, bf16[4,3,2,128,128]{4,3,2,1,0:T(8,128)(2,1)}, u32[]{:S(2)}, u32[]{:S(2)}) collective-permute-start(bf16[4,3,2,128,128]{4,3,2,1,0:T(8,128)(2,1)} %collective-permute-done.4.refs_3_), channel_id=1, source_target_pairs={{0,2},{2,4},{4,6},{6,0},{1,3},{3,5},{5,7},{7,1},{8,10},{10,12},{12... | collective-permute-start | bytes 2359304 | tf_op jit(solution)/shard_map/ppermute | solution.py:350
  110.6 0.7 broadcast_in_dim.24.refs_1_
  111.3 17.6 %shard_map.102 = bf16[16,1,128,128]{3,2,1,0:T(8,128)(2,1)} custom-call(bf16[16,1,1,128,128]{4,3,2,1,0:T(8,128)(2,1)} %copy-done.2, f32[1,128,128]{2,1,0:T(8,128)} %broadcast_in_dim.24.refs_1_, bf16[16,1,2,128,128]{4,3,2,1,0:T(8,128)(2,1)} %all-to-all-done.refs_2_, bf16[16,1,2,128,128]{4,3,2,1,0:T(8,128)(2,1)} %copy-done.3, ...), custom_call_target="tpu_custom_call" | custom-call | flops 17179869184 | bytes 4194304 | tf_op jit(solution)/shard_map/pallas_call | solution.py:291
  128.9 0.9 copy-done.1
  129.8 5.7 %all-to-all-start.3 = ((bf16[16,1,128,128]{3,2,1,0:T(8,128)(2,1)}), bf16[16,1,128,128]{3,2,1,0:T(8,128)(2,1)S(1)}, u32[]{:S(2)}, u32[]{:S(2)}) async-start(bf16[16,1,128,128]{3,2,1,0:T(8,128)(2,1)} %shard_map.102), calls=%async_computation.3 | async-start | bytes 1048576 | tf_op jit(solution)/shard_map/all_to_all | solution.py:405
  136.3 0.8 broadcast_in_dim.26.refs_1_
  137.1 19.7 %shard_map.103 = (f32[3,16,1024]{2,1,0:T(8,128)}, f32[3,128,1024]{2,1,0:T(8,128)}) custom-call(bf16[8,3,1,128,128]{4,3,2,1,0:T(8,128)(2,1)} %copy-done.1, f32[3,128,128]{2,1,0:T(8,128)} %broadcast_in_dim.26.refs_1_, bf16[8,3,2,128,128]{4,3,2,1,0:T(8,128)(2,1)} %copy-done, bf16[4,3,2,128,128]{4,3,2,1,0:T(8,128)(2,1)} %collective-permute-done.4.refs_3_, ...), custom_call_target="tpu_custom_call" | custom-call | flops 19327352832 | bytes 9437184 | tf_op jit(solution)/shard_map/pallas_call | solution.py:291
  156.9 10.4 %shard_map.104 = bf16[8,3,128,128]{3,2,1,0:T(8,128)(2,1)} custom-call(bf16[8,3,1,128,128]{4,3,2,1,0:T(8,128)(2,1)} %copy-done.1, f32[3,128,128]{2,1,0:T(8,128)} %broadcast_in_dim.26.refs_1_, bf16[4,3,2,128,128]{4,3,2,1,0:T(8,128)(2,1)} %collective-permute-done.5.refs_2_, bf16[4,3,2,128,128]{4,3,2,1,0:T(8,128)(2,1)} %collective-permute-done.7.refs_3_, ...), custom_call_target="tpu_custom_call" | custom-call | flops 6442450944 | bytes 3145728 | tf_op jit(solution)/shard_map/pallas_call | solution.py:291
  167.2 83.2 %all_to_all.30.refs_1_ = bf16[8,3,128,128]{3,2,1,0:T(8,128)(2,1)S(1)} all-to-all(bf16[8,3,128,128]{3,2,1,0:T(8,128)(2,1)} %shard_map.104), channel_id=1, replica_groups=mesh['expert'=2,'x'=2,'z'=4,'y'=4,'core'=2] {'x','z'}, dimensions={0} | all-to-all | bytes 1572864 | tf_op jit(solution)/shard_map/all_to_all | solution.py:408
  250.4 1.5 post.1
  (42 shorter events, 3.8 us)
Async XLA Ops:
  4.2 23.0 %all-to-all-start = ((bf16[16,1,2,128,128]{4,3,2,1,0:T(8,128)(2,1)}), bf16[16,1,2,128,128]{4,3,2,1,0:T(8,128)(2,1)}, u32[]{:S(2)}, u32[]{:S(2)}) async-start(bf16[16,1,2,128,128]{4,3,2,1,0:T(8,128)(2,1)} %shard_map.101), calls=%async_computation | async-start | bytes 2097152 | tf_op jit(solution)/shard_map/all_to_all | solution.py:382
  27.2 23.9 %all-to-all-start.1 = ((bf16[8,3,2,128,128]{4,3,2,1,0:T(8,128)(2,1)}), bf16[8,3,2,128,128]{4,3,2,1,0:T(8,128)(2,1)S(1)}, u32[]{:S(2)}, u32[]{:S(2)}) async-start(bf16[8,3,2,128,128]{4,3,2,1,0:T(8,128)(2,1)} %get-tuple-element.19), calls=%async_computation.1 | async-start | bytes 3145728 | tf_op jit(solution)/shard_map/all_to_all | solution.py:388
  30.7 25.4 %collective-permute-start = (bf16[16,1,2,128,128]{4,3,2,1,0:T(8,128)(2,1)}, bf16[16,1,2,128,128]{4,3,2,1,0:T(8,128)(2,1)S(1)}, u32[]{:S(2)}, u32[]{:S(2)}) collective-permute-start(bf16[16,1,2,128,128]{4,3,2,1,0:T(8,128)(2,1)} %all-to-all-done.refs_2_), channel_id=1, source_target_pairs={{0,2},{2,4},{4,6},{6,0},{1,3},{3,5},{5,7},{7,1},{8,10},{10,12},{12... | collective-permute-start | bytes 3145736 | tf_op jit(solution)/shard_map/ppermute | solution.py:383
  31.0 26.8 %collective-permute-start.1 = (bf16[16,1,2,128,128]{4,3,2,1,0:T(8,128)(2,1)}, bf16[16,1,2,128,128]{4,3,2,1,0:T(8,128)(2,1)}, u32[]{:S(2)}, u32[]{:S(2)}) collective-permute-start(bf16[16,1,2,128,128]{4,3,2,1,0:T(8,128)(2,1)} %all-to-all-done.refs_2_), channel_id=1, source_target_pairs={{0,6},{2,0},{4,2},{6,4},{1,7},{3,1},{5,3},{7,5},{8,14},{10,8},{12,... | collective-permute-start | bytes 3145736 | tf_op jit(solution)/shard_map/ppermute | solution.py:384
  51.1 1.4 copy-start
  52.5 32.6 %collective-permute-start.4 = (bf16[4,3,2,128,128]{4,3,2,1,0:T(8,128)(2,1)}, bf16[4,3,2,128,128]{4,3,2,1,0:T(8,128)(2,1)}, u32[]{:S(2)}, u32[]{:S(2)}) collective-permute-start(bf16[4,3,2,128,128]{4,3,2,1,0:T(8,128)(2,1)} %get-tuple-element.28), channel_id=1, source_target_pairs={{0,2},{2,4},{4,6},{6,0},{1,3},{3,5},{5,7},{7,1},{8,10},{10,12},{12... | collective-permute-start | bytes 2359304 | tf_op jit(solution)/shard_map/ppermute | solution.py:346
  52.7 32.9 %collective-permute-start.6 = (bf16[4,3,2,128,128]{4,3,2,1,0:T(8,128)(2,1)S(1)}, bf16[4,3,2,128,128]{4,3,2,1,0:T(8,128)(2,1)}, u32[]{:S(2)}, u32[]{:S(2)}) collective-permute-start(bf16[4,3,2,128,128]{4,3,2,1,0:T(8,128)(2,1)S(1)} %get-tuple-element.27), channel_id=1, source_target_pairs={{0,6},{2,0},{4,2},{6,4},{1,7},{3,1},{5,3},{7,5},{8,14},{10,8},{12,... | collective-permute-start | bytes 2359304 | tf_op jit(solution)/shard_map/ppermute | solution.py:347
  56.2 29.6 %copy-start.3 = (bf16[16,1,2,128,128]{4,3,2,1,0:T(8,128)(2,1)}, bf16[16,1,2,128,128]{4,3,2,1,0:T(8,128)(2,1)S(1)}, u32[]{:S(2)}) copy-start(bf16[16,1,2,128,128]{4,3,2,1,0:T(8,128)(2,1)S(1)} %collective-permute-done.refs_3_) | copy-start | bytes 3145732
  56.2 28.1 %collective-permute-start.2 = (bf16[8,1,2,128,128]{4,3,2,1,0:T(8,128)(2,1)S(1)}, bf16[8,1,2,128,128]{4,3,2,1,0:T(8,128)(2,1)S(1)}, u32[]{:S(2)}, u32[]{:S(2)}) collective-permute-start(bf16[8,1,2,128,128]{4,3,2,1,0:T(8,128)(2,1)S(1)} %slice.16), channel_id=1, source_target_pairs={{0,2},{2,4},{4,6},{6,0},{1,3},{3,5},{5,7},{7,1},{8,10},{10,12},{12... | collective-permute-start | bytes 1572872 | tf_op jit(solution)/shard_map/ppermute | solution.py:385
  58.9 26.2 %collective-permute-start.3 = (bf16[8,1,2,128,128]{4,3,2,1,0:T(8,128)(2,1)S(1)}, bf16[8,1,2,128,128]{4,3,2,1,0:T(8,128)(2,1)}, u32[]{:S(2)}, u32[]{:S(2)}) collective-permute-start(bf16[8,1,2,128,128]{4,3,2,1,0:T(8,128)(2,1)S(1)} %slice.17), channel_id=1, source_target_pairs={{0,6},{2,0},{4,2},{6,4},{1,7},{3,1},{5,3},{7,5},{8,14},{10,8},{12,... | collective-permute-start | bytes 1572872 | tf_op jit(solution)/shard_map/ppermute | solution.py:386
  59.5 47.1 %collective-permute-start.10 = (bf16[4,3,2,128,128]{4,3,2,1,0:T(8,128)(2,1)S(1)}, bf16[4,3,2,128,128]{4,3,2,1,0:T(8,128)(2,1)}, u32[]{:S(2)}, u32[]{:S(2)}) collective-permute-start(bf16[4,3,2,128,128]{4,3,2,1,0:T(8,128)(2,1)S(1)} %get-tuple-element.27), channel_id=1, source_target_pairs={{0,2},{2,4},{4,6},{6,0},{1,3},{3,5},{5,7},{7,1},{8,10},{10,12},{12... | collective-permute-start | bytes 2359304 | tf_op jit(solution)/shard_map/ppermute | solution.py:348
  84.3 1.4 copy-start.5
  84.3 24.8 %collective-permute-start.11 = (bf16[4,3,2,128,128]{4,3,2,1,0:T(8,128)(2,1)}, bf16[4,3,2,128,128]{4,3,2,1,0:T(8,128)(2,1)}, u32[]{:S(2)}, u32[]{:S(2)}) collective-permute-start(bf16[4,3,2,128,128]{4,3,2,1,0:T(8,128)(2,1)} %get-tuple-element.28), channel_id=1, source_target_pairs={{0,6},{2,0},{4,2},{6,4},{1,7},{3,1},{5,3},{7,5},{8,14},{10,8},{12,... | collective-permute-start | bytes 2359304 | tf_op jit(solution)/shard_map/ppermute | solution.py:349
  85.1 24.1 %collective-permute-start.12 = (bf16[4,3,2,128,128]{4,3,2,1,0:T(8,128)(2,1)}, bf16[4,3,2,128,128]{4,3,2,1,0:T(8,128)(2,1)S(1)}, u32[]{:S(2)}, u32[]{:S(2)}) collective-permute-start(bf16[4,3,2,128,128]{4,3,2,1,0:T(8,128)(2,1)} %get-tuple-element.28), channel_id=1, source_target_pairs={{0,1},{1,0},{2,3},{3,2},{4,5},{5,4},{6,7},{7,6},{8,9},{9,8},{10,11... | collective-permute-start | bytes 2359304 | tf_op jit(solution)/shard_map/ppermute | solution.py:397
  85.1 24.2 %collective-permute-start.13 = (bf16[4,3,2,128,128]{4,3,2,1,0:T(8,128)(2,1)S(1)}, bf16[4,3,2,128,128]{4,3,2,1,0:T(8,128)(2,1)}, u32[]{:S(2)}, u32[]{:S(2)}) collective-permute-start(bf16[4,3,2,128,128]{4,3,2,1,0:T(8,128)(2,1)S(1)} %get-tuple-element.27), channel_id=1, source_target_pairs={{0,1},{1,0},{2,3},{3,2},{4,5},{5,4},{6,7},{7,6},{8,9},{9,8},{10,11... | collective-permute-start | bytes 2359304 | tf_op jit(solution)/shard_map/ppermute | solution.py:397
  85.6 24.5 %collective-permute-start.14 = (bf16[4,3,2,128,128]{4,3,2,1,0:T(8,128)(2,1)}, bf16[4,3,2,128,128]{4,3,2,1,0:T(8,128)(2,1)}, u32[]{:S(2)}, u32[]{:S(2)}) collective-permute-start(bf16[4,3,2,128,128]{4,3,2,1,0:T(8,128)(2,1)} %collective-permute-done.4.refs_3_), channel_id=1, source_target_pairs={{0,1},{1,0},{2,3},{3,2},{4,5},{5,4},{6,7},{7,6},{8,9},{9,8},{10,11... | collective-permute-start | bytes 2359304 | tf_op jit(solution)/shard_map/ppermute | solution.py:397
  85.7 17.3 %all-to-all-start.2 = ((bf16[16,1,1,128,128]{4,3,2,1,0:T(8,128)(2,1)}), bf16[16,1,1,128,128]{4,3,2,1,0:T(8,128)(2,1)S(1)}, u32[]{:S(2)}, u32[]{:S(2)}) async-start(bf16[16,1,1,128,128]{4,3,2,1,0:T(8,128)(2,1)} %get-tuple-element.20), calls=%async_computation.2 | async-start | bytes 1048576 | tf_op jit(solution)/shard_map/all_to_all | solution.py:392
  103.0 6.2 %copy-start.2 = (bf16[16,1,1,128,128]{4,3,2,1,0:T(8,128)(2,1)}, bf16[16,1,1,128,128]{4,3,2,1,0:T(8,128)(2,1)S(1)}, u32[]{:S(2)}) copy-start(bf16[16,1,1,128,128]{4,3,2,1,0:T(8,128)(2,1)S(1)} %all-to-all-done.2.refs_0_) | copy-start | bytes 1572868
  103.0 25.9 %all-to-all-start.4 = ((bf16[8,3,1,128,128]{4,3,2,1,0:T(8,128)(2,1)}), bf16[8,3,1,128,128]{4,3,2,1,0:T(8,128)(2,1)S(1)}, u32[]{:S(2)}, u32[]{:S(2)}) async-start(bf16[8,3,1,128,128]{4,3,2,1,0:T(8,128)(2,1)} %get-tuple-element.23), calls=%async_computation.4 | async-start | bytes 1572864 | tf_op jit(solution)/shard_map/all_to_all | solution.py:394
  106.6 28.9 %collective-permute-start.5 = (bf16[4,3,2,128,128]{4,3,2,1,0:T(8,128)(2,1)}, bf16[4,3,2,128,128]{4,3,2,1,0:T(8,128)(2,1)}, u32[]{:S(2)}, u32[]{:S(2)}) collective-permute-start(bf16[4,3,2,128,128]{4,3,2,1,0:T(8,128)(2,1)} %collective-permute-done.4.refs_3_), channel_id=1, source_target_pairs={{0,2},{2,4},{4,6},{6,0},{1,3},{3,5},{5,7},{7,1},{8,10},{10,12},{12... | collective-permute-start | bytes 2359304 | tf_op jit(solution)/shard_map/ppermute | solution.py:350
  109.2 27.1 %collective-permute-start.15 = (bf16[4,3,2,128,128]{4,3,2,1,0:T(8,128)(2,1)}, bf16[4,3,2,128,128]{4,3,2,1,0:T(8,128)(2,1)}, u32[]{:S(2)}, u32[]{:S(2)}) collective-permute-start(bf16[4,3,2,128,128]{4,3,2,1,0:T(8,128)(2,1)} %collective-permute-done.6.refs_4_), channel_id=1, source_target_pairs={{0,1},{1,0},{2,3},{3,2},{4,5},{5,4},{6,7},{7,6},{8,9},{9,8},{10,11... | collective-permute-start | bytes 2359304 | tf_op jit(solution)/shard_map/ppermute | solution.py:397
  109.2 0.9 copy-start.4
  109.2 26.8 %collective-permute-start.7 = (bf16[4,3,2,128,128]{4,3,2,1,0:T(8,128)(2,1)}, bf16[4,3,2,128,128]{4,3,2,1,0:T(8,128)(2,1)}, u32[]{:S(2)}, u32[]{:S(2)}) collective-permute-start(bf16[4,3,2,128,128]{4,3,2,1,0:T(8,128)(2,1)} %collective-permute-done.6.refs_4_), channel_id=1, source_target_pairs={{0,6},{2,0},{4,2},{6,4},{1,7},{3,1},{5,3},{7,5},{8,14},{10,8},{12,... | collective-permute-start | bytes 2359304 | tf_op jit(solution)/shard_map/ppermute | solution.py:351
  109.3 27.0 %collective-permute-start.16 = (bf16[4,3,2,128,128]{4,3,2,1,0:T(8,128)(2,1)}, bf16[4,3,2,128,128]{4,3,2,1,0:T(8,128)(2,1)}, u32[]{:S(2)}, u32[]{:S(2)}) collective-permute-start(bf16[4,3,2,128,128]{4,3,2,1,0:T(8,128)(2,1)} %collective-permute-done.10.refs_5_), channel_id=1, source_target_pairs={{0,1},{1,0},{2,3},{3,2},{4,5},{5,4},{6,7},{7,6},{8,9},{9,8},{10,11... | collective-permute-start | bytes 2359304 | tf_op jit(solution)/shard_map/ppermute | solution.py:397
  110.1 26.2 %collective-permute-start.17 = (bf16[4,3,2,128,128]{4,3,2,1,0:T(8,128)(2,1)}, bf16[4,3,2,128,128]{4,3,2,1,0:T(8,128)(2,1)}, u32[]{:S(2)}, u32[]{:S(2)}) collective-permute-start(bf16[4,3,2,128,128]{4,3,2,1,0:T(8,128)(2,1)} %collective-permute-done.11.refs_6_), channel_id=1, source_target_pairs={{0,1},{1,0},{2,3},{3,2},{4,5},{5,4},{6,7},{7,6},{8,9},{9,8},{10,11... | collective-permute-start | bytes 2359304 | tf_op jit(solution)/shard_map/ppermute | solution.py:397
  128.9 0.9 copy-start.1
  129.8 37.4 %all-to-all-start.3 = ((bf16[16,1,128,128]{3,2,1,0:T(8,128)(2,1)}), bf16[16,1,128,128]{3,2,1,0:T(8,128)(2,1)S(1)}, u32[]{:S(2)}, u32[]{:S(2)}) async-start(bf16[16,1,128,128]{3,2,1,0:T(8,128)(2,1)} %shard_map.102), calls=%async_computation.3 | async-start | bytes 1048576 | tf_op jit(solution)/shard_map/all_to_all | solution.py:405
  135.5 21.4 %collective-permute-start.8 = (bf16[4,3,2,128,128]{4,3,2,1,0:T(8,128)(2,1)}, bf16[4,3,2,128,128]{4,3,2,1,0:T(8,128)(2,1)}, u32[]{:S(2)}, u32[]{:S(2)}) collective-permute-start(bf16[4,3,2,128,128]{4,3,2,1,0:T(8,128)(2,1)} %collective-permute-done.5.refs_2_), channel_id=1, source_target_pairs={{0,1},{1,0},{2,3},{3,2},{4,5},{5,4},{6,7},{7,6},{8,9},{9,8},{10,11... | collective-permute-start | bytes 2359304 | tf_op jit(solution)/shard_map/ppermute | solution.py:397
  136.0 20.9 %collective-permute-start.9 = (bf16[4,3,2,128,128]{4,3,2,1,0:T(8,128)(2,1)}, bf16[4,3,2,128,128]{4,3,2,1,0:T(8,128)(2,1)}, u32[]{:S(2)}, u32[]{:S(2)}) collective-permute-start(bf16[4,3,2,128,128]{4,3,2,1,0:T(8,128)(2,1)} %collective-permute-done.7.refs_3_), channel_id=1, source_target_pairs={{0,1},{1,0},{2,3},{3,2},{4,5},{5,4},{6,7},{7,6},{8,9},{9,8},{10,11... | collective-permute-start | bytes 2359304 | tf_op jit(solution)/shard_map/ppermute | solution.py:397

commit v2 on v1

--- a/solution.py
+++ b/solution.py
@@ -376,35 +376,31 @@
     gate_of = functools.partial(gates, timestep, gate_base, time_weight)
     q, k, v = (queries, query_gain), (keys, key_gain), (values, None)
 
-    (a,) = prepare(4, block, {"k": k, "v": v}, ((0, 4, 1, "kv"),))
-    b, a_query, b_query = prepare(8, block, {"q": q, "k": k, "v": v},
-                                  ((16, 1, 3, "kv"), (0, 2, 1, "q"), (16, 1, 3, "q")))
+    (a,) = prepare(4, block, {"q": q, "k": k, "v": v}, ((0, 4, 1, "qkv"),))
+    (b,) = prepare(8, block, {"q": q, "k": k, "v": v}, ((16, 1, 3, "qkv"),))
     a = spread(a, wide)
-    up_a = lax.ppermute(a, "y", shift("y", 1))
-    down_a = lax.ppermute(a, "y", shift("y", -1))
+    own_a = a[:, :, 1:]
+    up_a = lax.ppermute(own_a, "y", shift("y", 1))
+    down_a = lax.ppermute(own_a, "y", shift("y", -1))
     far_a = [lax.ppermute(up_a[:8], "y", shift("y", 1)),
              lax.ppermute(down_a[8:], "y", shift("y", -1))]
     b, a = lax.optimization_barrier((b, a))
     b = spread(b, narrow)
-    own_b = [b[:4], b[4:]]
+    own_b = [b[:4, :, 1:], b[4:, :, 1:]]
     near_b, far_b = ring(*own_b, "y")
-    a_query, b = lax.optimization_barrier((a_query, b))
-    a_query = spread(a_query, wide)
-    b_query, a_query = lax.optimization_barrier((b_query, a_query))
-    b_query = spread(b_query, narrow)
 
     def other(parts):
         return [lax.ppermute(p, "core", shift("core", 1)) for p in parts]
 
-    near_b = [b] + near_b + other(own_b) + other(near_b)
+    near_b = own_b + near_b + other(own_b) + other(near_b)
     far_b = far_b + other(far_b)
     gate_a = gate_of((x * 4 + z) * 2 + core, 1)
     gate_b = gate_of(16 + (x * 4 + z) * 3, 3)
 
-    out_a = attend(a_query, gate_a, [a, up_a, down_a] + far_a)
+    out_a = attend(a, gate_a, [own_a, up_a, down_a] + far_a)
     out_a = spread(out_a, wide)
-    state = attend(b_query, gate_b, near_b, final=False)
-    out_b = attend(b_query, gate_b, far_b, state, together=3)
+    state = attend(b, gate_b, near_b, final=False)
+    out_b = attend(b, gate_b, far_b, state)
     out_b = spread(out_b, narrow)
     return collect(out_a, out_b)
 

time: 253 us -> 237 us (0.937)
  blocking collectives: 83.2 us -> 61.5 us
  waiting for transfers between devices: 58.1 us -> 74.9 us
  starting transfers between devices: 40.5 us -> 27.8 us
    all_to_all x1, blocking collectives: 83.2 us -> 61.5 us  [block_attention(): out_b = spread(out_b, narrow)]
    all_to_all x2 -> x0, starting transfers between devices: 10 us -> none  [the longest x1 6.48 us: block_attention(): a_query = spread(a_query, wide)]
    ppermute x1, waiting for transfers between devices: 0.01 us -> 9.69 us  [ring(): up_high = lax.ppermute(high, axis, shift(axis, 1))]
    all_to_all x1, waiting for transfers between devices: 18.2 us -> 26 us  [block_attention(): b = spread(b, narrow)]
    all_to_all x2 -> x0, waiting for transfers between devices: 6.93 us -> none  [the longest x1 6.92 us: block_attention(): a_query = spread(a_query, wide)]
    all_to_all x1, waiting for transfers between devices: 9.08 us -> 15 us  [block_attention(): a = spread(a, wide)]
  transfers between devices with their start and end apart: 23 -> 21, of which waited for: 6 -> 5; matrix products, arithmetic and copies ran while one was open for 3% -> 4% of each run, Pallas kernels for 22% -> 23%
where the time goes in v2:
time: 237 us; the launch traced here: 236 us
  waiting for transfers between devices  74.9 us (32%)
  blocking collectives  61.5 us (26%)
  Pallas kernels  60.7 us (26%)
  starting transfers between devices  27.8 us (12%)
  local copies, waits for them, and re-layouts  7.14 us (3%)
  matrix products  2.4 us (1%)
    all_to_all x1, blocking collectives, block_attention(): out_b = spread(out_b, narrow)  61.5 us
    pallas_call x3, Pallas kernels, attend(): pl.pallas_call(functools.partial(attend_kernel, sizes=sizes, resume=state...  46.4 us
    all_to_all x1, waiting for transfers between devices, block_attention(): b = spread(b, narrow)  26 us
    ppermute x1, waiting for transfers between devices, block_attention(): lax.ppermute(up_a[:8], 'y', shift('y', 1))  22.8 us
    all_to_all x1, waiting for transfers between devices, block_attention(): a = spread(a, wide)  15 us
    pallas_call x2, Pallas kernels, prepare(): pl.pallas_call(functools.partial(prep_kernel, tensors=kinds, plan=plan),...  12.8 us
    ppermute x1, waiting for transfers between devices, ring(): up_high = lax.ppermute(high, axis, shift(axis, 1))  9.69 us
    all_to_all x1, starting transfers between devices, block_attention(): a = spread(a, wide)  6.4 us
  transfers between devices with their start and end apart: 21, of which 5 were waited for; matrix products, arithmetic and copies ran while one was open for 4% of the time, Pallas kernels for 23%

profile of v2, /device:TPU:24, one launch (start us, length us, event | category | flops | bytes accessed | tf_op | source)
XLA Modules:
  0.0 236.1 jit_solution(18232653582199823974)
XLA Ops:
  0.0 5.5 %shard_map.101 = bf16[16,1,3,128,128]{4,3,2,1,0:T(8,128)(2,1)} custom-call(s32[1]{0:T(128)} %bitcast.block_ref, f32[1,128]{1,0:T(1,128)} %constant.38.inv_hbm, bf16[128,5120]{1,0:T(8,128)(2,1)} %refs_0_.3, bf16[128,5120]{1,0:T(8,128)(2,1)} %refs_1_.3, bf16[128,5120]{1,0:T(8,128)(2,1)} %refs_2_.3, f32[40,128]{1,0:T(8,128)} %bitcast.16, f32[40,128]{1,0:T(8,128)} %bitcast.18), custom_call_target="tpu_custom_call" | custom-call | tf_op jit(solution)/shard_map/pallas_call | solution.py:120
  5.5 6.4 %all-to-all-start = ((bf16[16,1,3,128,128]{4,3,2,1,0:T(8,128)(2,1)}), bf16[16,1,3,128,128]{4,3,2,1,0:T(8,128)(2,1)}, u32[]{:S(2)}, u32[]{:S(2)}) async-start(bf16[16,1,3,128,128]{4,3,2,1,0:T(8,128)(2,1)} %shard_map.101), calls=%async_computation | async-start | bytes 3145728 | tf_op jit(solution)/shard_map/all_to_all | solution.py:381
  11.9 7.3 %shard_map.100 = bf16[8,3,3,128,128]{4,3,2,1,0:T(8,128)(2,1)} custom-call(s32[1]{0:T(128)} %bitcast.block_ref, f32[1,128]{1,0:T(1,128)} %constant.38.inv_hbm, bf16[128,5120]{1,0:T(8,128)(2,1)} %refs_0_.3, bf16[128,5120]{1,0:T(8,128)(2,1)} %refs_1_.3, bf16[128,5120]{1,0:T(8,128)(2,1)} %refs_2_.3, f32[40,128]{1,0:T(8,128)} %bitcast.17, f32[40,128]{1,0:T(8,128)} %bitcast.19), custom_call_target="tpu_custom_call" | custom-call | tf_op jit(solution)/shard_map/pallas_call | solution.py:120
  19.2 15.0 %all-to-all-done.refs_0_ = bf16[16,1,3,128,128]{4,3,2,1,0:T(8,128)(2,1)} async-done(((bf16[16,1,3,128,128]{4,3,2,1,0:T(8,128)(2,1)}), bf16[16,1,3,128,128]{4,3,2,1,0:T(8,128)(2,1)}, u32[]{:S(2)}, u32[]{:S(2)}) %all-to-all-start) | async-done | bytes 1572896 | tf_op jit(solution)/shard_map/all_to_all | solution.py:381
  34.2 3.7 %all-to-all-start.2 = ((bf16[8,3,3,128,128]{4,3,2,1,0:T(8,128)(2,1)}), bf16[8,3,3,128,128]{4,3,2,1,0:T(8,128)(2,1)S(1)}, u32[]{:S(2)}, u32[]{:S(2)}) async-start(bf16[8,3,3,128,128]{4,3,2,1,0:T(8,128)(2,1)} %shard_map.100), calls=%async_computation.2 | async-start | bytes 4718592 | tf_op jit(solution)/shard_map/all_to_all | solution.py:388
  37.9 1.3 slice.20.refs_2_
  39.5 1.8 collective-permute-start.1
  41.3 26.0 %all-to-all-done.2.refs_0_ = bf16[8,3,3,128,128]{4,3,2,1,0:T(8,128)(2,1)S(1)} async-done(((bf16[8,3,3,128,128]{4,3,2,1,0:T(8,128)(2,1)}), bf16[8,3,3,128,128]{4,3,2,1,0:T(8,128)(2,1)S(1)}, u32[]{:S(2)}, u32[]{:S(2)}) %all-to-all-start.2) | async-done | bytes 2359328 | tf_op jit(solution)/shard_map/all_to_all | solution.py:388
  67.3 1.4 fusion.7
  68.9 1.8 collective-permute-start.6
  70.7 1.1 slice.21
  71.8 1.5 collective-permute-start.2
  73.3 1.1 slice.22
  74.4 0.7 collective-permute-start.3
  75.0 2.6 %collective-permute-start.10 = (bf16[4,3,2,128,128]{4,3,2,1,0:T(8,128)(2,1)}, bf16[4,3,2,128,128]{4,3,2,1,0:T(8,128)(2,1)}, u32[]{:S(2)}, u32[]{:S(2)}) collective-permute-start(bf16[4,3,2,128,128]{4,3,2,1,0:T(8,128)(2,1)} %get-tuple-element.13.refs_3_), channel_id=1, source_target_pairs={{0,2},{2,4},{4,6},{6,0},{1,3},{3,5},{5,7},{7,1},{8,10},{10,12},{12... | collective-permute-start | bytes 2359304 | tf_op jit(solution)/shard_map/ppermute | solution.py:348
  77.7 22.8 %collective-permute-done.2.refs_5_ = bf16[8,1,2,128,128]{4,3,2,1,0:T(8,128)(2,1)S(1)} collective-permute-done((bf16[8,1,2,128,128]{4,3,2,1,0:T(8,128)(2,1)S(1)}, bf16[8,1,2,128,128]{4,3,2,1,0:T(8,128)(2,1)S(1)}, u32[]{:S(2)}, u32[]{:S(2)}) %collective-permute-start.2) | collective-permute-done | bytes 524320 | tf_op jit(solution)/shard_map/ppermute | solution.py:385
  100.5 0.7 collective-permute-start.11
  101.4 0.8 copy-done.3
  103.4 1.3 convolution_reduce_fusion
  104.7 1.1 fusion
  105.8 0.8 add_bitcast_fusion
  106.6 9.7 %collective-permute-done.10.refs_6_ = bf16[4,3,2,128,128]{4,3,2,1,0:T(8,128)(2,1)} collective-permute-done((bf16[4,3,2,128,128]{4,3,2,1,0:T(8,128)(2,1)}, bf16[4,3,2,128,128]{4,3,2,1,0:T(8,128)(2,1)}, u32[]{:S(2)}, u32[]{:S(2)}) %collective-permute-start.10) | collective-permute-done | bytes 786464 | tf_op jit(solution)/shard_map/ppermute | solution.py:348
  116.2 1.5 collective-permute-start.5
  117.7 1.4 collective-permute-done.11.refs_7_
  120.0 0.7 broadcast_in_dim.24.refs_1_
  120.7 17.6 %shard_map.102 = bf16[16,1,128,128]{3,2,1,0:T(8,128)(2,1)} custom-call(bf16[16,1,3,128,128]{4,3,2,1,0:T(8,128)(2,1)} %all-to-all-done.refs_0_, f32[1,128,128]{2,1,0:T(8,128)} %broadcast_in_dim.24.refs_1_, bf16[16,1,2,128,128]{4,3,2,1,0:T(8,128)(2,1)} %copy-done.1, bf16[16,1,2,128,128]{4,3,2,1,0:T(8,128)(2,1)} %collective-permute-done.refs_3_, ...), custom_call_target="tpu_custom_call" | custom-call | flops 17179869184 | bytes 4194304 | tf_op jit(solution)/shard_map/pallas_call | solution.py:291
  138.3 4.4 %all-to-all-start.1 = ((bf16[16,1,128,128]{3,2,1,0:T(8,128)(2,1)}), bf16[16,1,128,128]{3,2,1,0:T(8,128)(2,1)S(1)}, u32[]{:S(2)}, u32[]{:S(2)}) async-start(bf16[16,1,128,128]{3,2,1,0:T(8,128)(2,1)} %shard_map.102), calls=%async_computation.1 | async-start | bytes 1048576 | tf_op jit(solution)/shard_map/all_to_all | solution.py:401
  143.5 0.8 broadcast_in_dim.26.refs_1_
  144.3 19.8 %shard_map.103 = (f32[3,16,1024]{2,1,0:T(8,128)}, f32[3,128,1024]{2,1,0:T(8,128)}) custom-call(bf16[8,3,3,128,128]{4,3,2,1,0:T(8,128)(2,1)} %copy-done, f32[3,128,128]{2,1,0:T(8,128)} %broadcast_in_dim.26.refs_1_, bf16[4,3,2,128,128]{4,3,2,1,0:T(8,128)(2,1)} %get-tuple-element.14.refs_2_, bf16[4,3,2,128,128]{4,3,2,1,0:T(8,128)(2,1)} %get-tuple-element.13.refs_3_, ...), custom_call_target="tpu_custom_call" | custom-call | flops 19327352832 | bytes 9437184 | tf_op jit(solution)/shard_map/pallas_call | solution.py:291
  164.1 9.0 %shard_map.104 = bf16[8,3,128,128]{3,2,1,0:T(8,128)(2,1)} custom-call(bf16[8,3,3,128,128]{4,3,2,1,0:T(8,128)(2,1)} %copy-done, f32[3,128,128]{2,1,0:T(8,128)} %broadcast_in_dim.26.refs_1_, bf16[4,3,2,128,128]{4,3,2,1,0:T(8,128)(2,1)} %collective-permute-done.5.refs_2_, bf16[4,3,2,128,128]{4,3,2,1,0:T(8,128)(2,1)} %collective-permute-done.7.refs_3_, ...), custom_call_target="tpu_custom_call" | custom-call | flops 6442450944 | bytes 3145728 | tf_op jit(solution)/shard_map/pallas_call | solution.py:291
  173.2 61.5 %all_to_all.20.refs_1_ = bf16[8,3,128,128]{3,2,1,0:T(8,128)(2,1)S(1)} all-to-all(bf16[8,3,128,128]{3,2,1,0:T(8,128)(2,1)} %shard_map.104), channel_id=1, replica_groups=mesh['expert'=2,'x'=2,'z'=4,'y'=4,'core'=2] {'x','z'}, dimensions={0} | all-to-all | bytes 1572864 | tf_op jit(solution)/shard_map/all_to_all | solution.py:404
  234.6 1.5 post.1
  (35 shorter events, 2.9 us)
Async XLA Ops:
  5.5 28.7 %all-to-all-start = ((bf16[16,1,3,128,128]{4,3,2,1,0:T(8,128)(2,1)}), bf16[16,1,3,128,128]{4,3,2,1,0:T(8,128)(2,1)}, u32[]{:S(2)}, u32[]{:S(2)}) async-start(bf16[16,1,3,128,128]{4,3,2,1,0:T(8,128)(2,1)} %shard_map.101), calls=%async_computation | async-start | bytes 3145728 | tf_op jit(solution)/shard_map/all_to_all | solution.py:381
  34.2 33.1 %all-to-all-start.2 = ((bf16[8,3,3,128,128]{4,3,2,1,0:T(8,128)(2,1)}), bf16[8,3,3,128,128]{4,3,2,1,0:T(8,128)(2,1)S(1)}, u32[]{:S(2)}, u32[]{:S(2)}) async-start(bf16[8,3,3,128,128]{4,3,2,1,0:T(8,128)(2,1)} %shard_map.100), calls=%async_computation.2 | async-start | bytes 4718592 | tf_op jit(solution)/shard_map/all_to_all | solution.py:388
  39.2 35.2 %copy-start.1 = (bf16[16,1,2,128,128]{4,3,2,1,0:T(8,128)(2,1)}, bf16[16,1,2,128,128]{4,3,2,1,0:T(8,128)(2,1)S(1)}, u32[]{:S(2)}) copy-start(bf16[16,1,2,128,128]{4,3,2,1,0:T(8,128)(2,1)S(1)} %slice.20.refs_2_) | copy-start | bytes 3145732
  39.2 31.5 %collective-permute-start = (bf16[16,1,2,128,128]{4,3,2,1,0:T(8,128)(2,1)S(1)}, bf16[16,1,2,128,128]{4,3,2,1,0:T(8,128)(2,1)}, u32[]{:S(2)}, u32[]{:S(2)}) collective-permute-start(bf16[16,1,2,128,128]{4,3,2,1,0:T(8,128)(2,1)S(1)} %slice.20.refs_2_), channel_id=1, source_target_pairs={{0,2},{2,4},{4,6},{6,0},{1,3},{3,5},{5,7},{7,1},{8,10},{10,12},{12... | collective-permute-start | bytes 3145736 | tf_op jit(solution)/shard_map/ppermute | solution.py:383
  39.5 33.8 %collective-permute-start.1 = (bf16[16,1,2,128,128]{4,3,2,1,0:T(8,128)(2,1)S(1)}, bf16[16,1,2,128,128]{4,3,2,1,0:T(8,128)(2,1)}, u32[]{:S(2)}, u32[]{:S(2)}) collective-permute-start(bf16[16,1,2,128,128]{4,3,2,1,0:T(8,128)(2,1)S(1)} %slice.20.refs_2_), channel_id=1, source_target_pairs={{0,6},{2,0},{4,2},{6,4},{1,7},{3,1},{5,3},{7,5},{8,14},{10,8},{12,... | collective-permute-start | bytes 3145736 | tf_op jit(solution)/shard_map/ppermute | solution.py:384
  67.3 7.1 %copy-start = (bf16[8,3,3,128,128]{4,3,2,1,0:T(8,128)(2,1)}, bf16[8,3,3,128,128]{4,3,2,1,0:T(8,128)(2,1)S(1)}, u32[]{:S(2)}) copy-start(bf16[8,3,3,128,128]{4,3,2,1,0:T(8,128)(2,1)S(1)} %all-to-all-done.2.refs_0_) | copy-start | bytes 7077892
  68.7 33.5 %collective-permute-start.4 = (bf16[4,3,2,128,128]{4,3,2,1,0:T(8,128)(2,1)}, bf16[4,3,2,128,128]{4,3,2,1,0:T(8,128)(2,1)}, u32[]{:S(2)}, u32[]{:S(2)}) collective-permute-start(bf16[4,3,2,128,128]{4,3,2,1,0:T(8,128)(2,1)} %get-tuple-element.14.refs_2_), channel_id=1, source_target_pairs={{0,2},{2,4},{4,6},{6,0},{1,3},{3,5},{5,7},{7,1},{8,10},{10,12},{12... | collective-permute-start | bytes 2359304 | tf_op jit(solution)/shard_map/ppermute | solution.py:346
  68.9 33.3 %collective-permute-start.6 = (bf16[4,3,2,128,128]{4,3,2,1,0:T(8,128)(2,1)}, bf16[4,3,2,128,128]{4,3,2,1,0:T(8,128)(2,1)}, u32[]{:S(2)}, u32[]{:S(2)}) collective-permute-start(bf16[4,3,2,128,128]{4,3,2,1,0:T(8,128)(2,1)} %get-tuple-element.13.refs_3_), channel_id=1, source_target_pairs={{0,6},{2,0},{4,2},{6,4},{1,7},{3,1},{5,3},{7,5},{8,14},{10,8},{12,... | collective-permute-start | bytes 2359304 | tf_op jit(solution)/shard_map/ppermute | solution.py:347
  71.8 28.7 %collective-permute-start.2 = (bf16[8,1,2,128,128]{4,3,2,1,0:T(8,128)(2,1)S(1)}, bf16[8,1,2,128,128]{4,3,2,1,0:T(8,128)(2,1)S(1)}, u32[]{:S(2)}, u32[]{:S(2)}) collective-permute-start(bf16[8,1,2,128,128]{4,3,2,1,0:T(8,128)(2,1)S(1)} %slice.21), channel_id=1, source_target_pairs={{0,2},{2,4},{4,6},{6,0},{1,3},{3,5},{5,7},{7,1},{8,10},{10,12},{12... | collective-permute-start | bytes 1572872 | tf_op jit(solution)/shard_map/ppermute | solution.py:385
  74.4 26.9 %collective-permute-start.3 = (bf16[8,1,2,128,128]{4,3,2,1,0:T(8,128)(2,1)S(1)}, bf16[8,1,2,128,128]{4,3,2,1,0:T(8,128)(2,1)S(1)}, u32[]{:S(2)}, u32[]{:S(2)}) collective-permute-start(bf16[8,1,2,128,128]{4,3,2,1,0:T(8,128)(2,1)S(1)} %slice.22), channel_id=1, source_target_pairs={{0,6},{2,0},{4,2},{6,4},{1,7},{3,1},{5,3},{7,5},{8,14},{10,8},{12,... | collective-permute-start | bytes 1572872 | tf_op jit(solution)/shard_map/ppermute | solution.py:386
  75.0 41.2 %collective-permute-start.10 = (bf16[4,3,2,128,128]{4,3,2,1,0:T(8,128)(2,1)}, bf16[4,3,2,128,128]{4,3,2,1,0:T(8,128)(2,1)}, u32[]{:S(2)}, u32[]{:S(2)}) collective-permute-start(bf16[4,3,2,128,128]{4,3,2,1,0:T(8,128)(2,1)} %get-tuple-element.13.refs_3_), channel_id=1, source_target_pairs={{0,2},{2,4},{4,6},{6,0},{1,3},{3,5},{5,7},{7,1},{8,10},{10,12},{12... | collective-permute-start | bytes 2359304 | tf_op jit(solution)/shard_map/ppermute | solution.py:348
  100.5 0.8 copy-start.2
  100.5 18.6 %collective-permute-start.11 = (bf16[4,3,2,128,128]{4,3,2,1,0:T(8,128)(2,1)}, bf16[4,3,2,128,128]{4,3,2,1,0:T(8,128)(2,1)}, u32[]{:S(2)}, u32[]{:S(2)}) collective-permute-start(bf16[4,3,2,128,128]{4,3,2,1,0:T(8,128)(2,1)} %get-tuple-element.14.refs_2_), channel_id=1, source_target_pairs={{0,6},{2,0},{4,2},{6,4},{1,7},{3,1},{5,3},{7,5},{8,14},{10,8},{12,... | collective-permute-start | bytes 2359304 | tf_op jit(solution)/shard_map/ppermute | solution.py:349
  101.3 0.8 copy-start.3
  101.3 17.8 %collective-permute-start.12 = (bf16[4,3,2,128,128]{4,3,2,1,0:T(8,128)(2,1)}, bf16[4,3,2,128,128]{4,3,2,1,0:T(8,128)(2,1)}, u32[]{:S(2)}, u32[]{:S(2)}) collective-permute-start(bf16[4,3,2,128,128]{4,3,2,1,0:T(8,128)(2,1)} %get-tuple-element.14.refs_2_), channel_id=1, source_target_pairs={{0,1},{1,0},{2,3},{3,2},{4,5},{5,4},{6,7},{7,6},{8,9},{9,8},{10,11... | collective-permute-start | bytes 2359304 | tf_op jit(solution)/shard_map/ppermute | solution.py:393
  102.1 17.0 %collective-permute-start.13 = (bf16[4,3,2,128,128]{4,3,2,1,0:T(8,128)(2,1)}, bf16[4,3,2,128,128]{4,3,2,1,0:T(8,128)(2,1)}, u32[]{:S(2)}, u32[]{:S(2)}) collective-permute-start(bf16[4,3,2,128,128]{4,3,2,1,0:T(8,128)(2,1)} %get-tuple-element.13.refs_3_), channel_id=1, source_target_pairs={{0,1},{1,0},{2,3},{3,2},{4,5},{5,4},{6,7},{7,6},{8,9},{9,8},{10,11... | collective-permute-start | bytes 2359304 | tf_op jit(solution)/shard_map/ppermute | solution.py:393
  102.2 17.6 %collective-permute-start.14 = (bf16[4,3,2,128,128]{4,3,2,1,0:T(8,128)(2,1)}, bf16[4,3,2,128,128]{4,3,2,1,0:T(8,128)(2,1)}, u32[]{:S(2)}, u32[]{:S(2)}) collective-permute-start(bf16[4,3,2,128,128]{4,3,2,1,0:T(8,128)(2,1)} %collective-permute-done.4.refs_4_), channel_id=1, source_target_pairs={{0,1},{1,0},{2,3},{3,2},{4,5},{5,4},{6,7},{7,6},{8,9},{9,8},{10,11... | collective-permute-start | bytes 2359304 | tf_op jit(solution)/shard_map/ppermute | solution.py:393
  116.2 26.5 %collective-permute-start.5 = (bf16[4,3,2,128,128]{4,3,2,1,0:T(8,128)(2,1)}, bf16[4,3,2,128,128]{4,3,2,1,0:T(8,128)(2,1)}, u32[]{:S(2)}, u32[]{:S(2)}) collective-permute-start(bf16[4,3,2,128,128]{4,3,2,1,0:T(8,128)(2,1)} %collective-permute-done.4.refs_4_), channel_id=1, source_target_pairs={{0,2},{2,4},{4,6},{6,0},{1,3},{3,5},{5,7},{7,1},{8,10},{10,12},{12... | collective-permute-start | bytes 2359304 | tf_op jit(solution)/shard_map/ppermute | solution.py:350
  119.1 24.4 %collective-permute-start.15 = (bf16[4,3,2,128,128]{4,3,2,1,0:T(8,128)(2,1)}, bf16[4,3,2,128,128]{4,3,2,1,0:T(8,128)(2,1)}, u32[]{:S(2)}, u32[]{:S(2)}) collective-permute-start(bf16[4,3,2,128,128]{4,3,2,1,0:T(8,128)(2,1)} %collective-permute-done.6.refs_5_), channel_id=1, source_target_pairs={{0,1},{1,0},{2,3},{3,2},{4,5},{5,4},{6,7},{7,6},{8,9},{9,8},{10,11... | collective-permute-start | bytes 2359304 | tf_op jit(solution)/shard_map/ppermute | solution.py:393
  119.1 24.1 %collective-permute-start.7 = (bf16[4,3,2,128,128]{4,3,2,1,0:T(8,128)(2,1)}, bf16[4,3,2,128,128]{4,3,2,1,0:T(8,128)(2,1)}, u32[]{:S(2)}, u32[]{:S(2)}) collective-permute-start(bf16[4,3,2,128,128]{4,3,2,1,0:T(8,128)(2,1)} %collective-permute-done.6.refs_5_), channel_id=1, source_target_pairs={{0,6},{2,0},{4,2},{6,4},{1,7},{3,1},{5,3},{7,5},{8,14},{10,8},{12,... | collective-permute-start | bytes 2359304 | tf_op jit(solution)/shard_map/ppermute | solution.py:351
  119.1 24.4 %collective-permute-start.16 = (bf16[4,3,2,128,128]{4,3,2,1,0:T(8,128)(2,1)}, bf16[4,3,2,128,128]{4,3,2,1,0:T(8,128)(2,1)}, u32[]{:S(2)}, u32[]{:S(2)}) collective-permute-start(bf16[4,3,2,128,128]{4,3,2,1,0:T(8,128)(2,1)} %collective-permute-done.10.refs_6_), channel_id=1, source_target_pairs={{0,1},{1,0},{2,3},{3,2},{4,5},{5,4},{6,7},{7,6},{8,9},{9,8},{10,11... | collective-permute-start | bytes 2359304 | tf_op jit(solution)/shard_map/ppermute | solution.py:393
  119.7 23.8 %collective-permute-start.17 = (bf16[4,3,2,128,128]{4,3,2,1,0:T(8,128)(2,1)}, bf16[4,3,2,128,128]{4,3,2,1,0:T(8,128)(2,1)}, u32[]{:S(2)}, u32[]{:S(2)}) collective-permute-start(bf16[4,3,2,128,128]{4,3,2,1,0:T(8,128)(2,1)} %collective-permute-done.11.refs_7_), channel_id=1, source_target_pairs={{0,1},{1,0},{2,3},{3,2},{4,5},{5,4},{6,7},{7,6},{8,9},{9,8},{10,11... | collective-permute-start | bytes 2359304 | tf_op jit(solution)/shard_map/ppermute | solution.py:393
  138.3 34.9 %all-to-all-start.1 = ((bf16[16,1,128,128]{3,2,1,0:T(8,128)(2,1)}), bf16[16,1,128,128]{3,2,1,0:T(8,128)(2,1)S(1)}, u32[]{:S(2)}, u32[]{:S(2)}) async-start(bf16[16,1,128,128]{3,2,1,0:T(8,128)(2,1)} %shard_map.102), calls=%async_computation.1 | async-start | bytes 1048576 | tf_op jit(solution)/shard_map/all_to_all | solution.py:401
  142.7 21.4 %collective-permute-start.8 = (bf16[4,3,2,128,128]{4,3,2,1,0:T(8,128)(2,1)}, bf16[4,3,2,128,128]{4,3,2,1,0:T(8,128)(2,1)}, u32[]{:S(2)}, u32[]{:S(2)}) collective-permute-start(bf16[4,3,2,128,128]{4,3,2,1,0:T(8,128)(2,1)} %collective-permute-done.5.refs_2_), channel_id=1, source_target_pairs={{0,1},{1,0},{2,3},{3,2},{4,5},{5,4},{6,7},{7,6},{8,9},{9,8},{10,11... | collective-permute-start | bytes 2359304 | tf_op jit(solution)/shard_map/ppermute | solution.py:393
  143.2 20.9 %collective-permute-start.9 = (bf16[4,3,2,128,128]{4,3,2,1,0:T(8,128)(2,1)}, bf16[4,3,2,128,128]{4,3,2,1,0:T(8,128)(2,1)}, u32[]{:S(2)}, u32[]{:S(2)}) collective-permute-start(bf16[4,3,2,128,128]{4,3,2,1,0:T(8,128)(2,1)} %collective-permute-done.7.refs_3_), channel_id=1, source_target_pairs={{0,1},{1,0},{2,3},{3,2},{4,5},{5,4},{6,7},{7,6},{8,9},{9,8},{10,11... | collective-permute-start | bytes 2359304 | tf_op jit(solution)/shard_map/ppermute | solution.py:393

commit v3 on v2

--- a/solution.py
+++ b/solution.py
@@ -98,14 +98,13 @@
         r = rms_refs[turned.index(n)][...]
         return (x.astype(F32) * r * g) * cos_ref[...] + (xs * r * gs) * sin_ref[...]
 
-    for dst, (first, peers, heads, kinds) in zip(outs, plan):
+    for dst, (peers, tiles) in zip(outs, plan):
         for peer in range(peers):
-            for h in range(heads):
-                head = first + (step * peers + peer) * heads + h
-                for slot, kind in enumerate(kinds):
-                    n = tensors.index(kind)
-                    y = columns(n, head).astype(F32) if kind == "v" else rotated(n, head)
-                    dst[peer, h, slot] = (y if kind == "k" else y.T).astype(BF16)
+            for slot, (kind, stride, first) in enumerate(tiles):
+                head = first + (step * peers + peer) * stride
+                n = tensors.index(kind)
+                y = columns(n, head).astype(F32) if kind == "v" else rotated(n, head)
+                dst[peer, slot] = (y if kind == "k" else y.T).astype(BF16)
 
 
 def prepare(steps, block, tensors, plan):
@@ -116,12 +115,12 @@
     tile = (HEAD_DIM, tokens)
     gains = [tensors[k][1].reshape(heads, HEAD_DIM) for k in kinds if k != "v"]
     hbm = pl.BlockSpec(memory_space=pltpu.HBM)
-    shapes = [(peers, count, len(slots)) + tile for _, peers, count, slots in plan]
+    shapes = [(peers, len(tiles)) + tile for peers, tiles in plan]
     return pl.pallas_call(
         functools.partial(prep_kernel, tensors=kinds, plan=plan),
         grid=(steps,),
         in_specs=[pl.BlockSpec(memory_space=pltpu.SMEM)] + [hbm] * (1 + len(kinds) + len(gains)),
-        out_specs=[pl.BlockSpec(shape, lambda i: (i, 0, 0, 0, 0)) for shape in shapes],
+        out_specs=[pl.BlockSpec(shape, lambda i: (i, 0, 0, 0)) for shape in shapes],
         out_shape=[jax.ShapeDtypeStruct((steps * shape[0],) + shape[1:], BF16)
                    for shape in shapes],
         scratch_shapes=[
@@ -376,31 +375,43 @@
     gate_of = functools.partial(gates, timestep, gate_base, time_weight)
     q, k, v = (queries, query_gain), (keys, key_gain), (values, None)
 
-    (a,) = prepare(4, block, {"q": q, "k": k, "v": v}, ((0, 4, 1, "qkv"),))
-    (b,) = prepare(8, block, {"q": q, "k": k, "v": v}, ((16, 1, 3, "qkv"),))
-    a = spread(a, wide)
-    own_a = a[:, :, 1:]
+    key_values = tuple((kind, 3, 16 + h) for h in range(3) for kind in "kv")
+    (a,) = prepare(4, block, {"k": k, "v": v}, ((4, (("k", 1, 0), ("v", 1, 0))),))
+    b, b_query = prepare(8, block, {"q": q, "k": k, "v": v}, (
+        (1, key_values + (("q", 2, 0), ("q", 2, 1))),
+        (1, tuple(("q", 3, 16 + h) for h in range(3))),
+    ))
+    own_a = spread(a, wide).reshape(16, 1, 2, HEAD_DIM, -1)
     up_a = lax.ppermute(own_a, "y", shift("y", 1))
     down_a = lax.ppermute(own_a, "y", shift("y", -1))
     far_a = [lax.ppermute(up_a[:8], "y", shift("y", 1)),
              lax.ppermute(down_a[8:], "y", shift("y", -1))]
-    b, a = lax.optimization_barrier((b, a))
+    b, own_a = lax.optimization_barrier((b, own_a))
     b = spread(b, narrow)
-    own_b = [b[:4, :, 1:], b[4:, :, 1:]]
+    own_b = [b[:4, :6].reshape(4, 3, 2, HEAD_DIM, -1), b[4:, :6].reshape(4, 3, 2, HEAD_DIM, -1)]
     near_b, far_b = ring(*own_b, "y")
+    b_query, b = lax.optimization_barrier((b_query, b))
+    b_query = spread(b_query, narrow).reshape(8, 3, 1, HEAD_DIM, -1)
+    mine = lax.dynamic_slice_in_dim(b, 6 + core, 1, 1)
+    sent = lax.dynamic_slice_in_dim(b, 7 - core, 1, 1)
+    a_query = jnp.concatenate([mine, lax.ppermute(sent, "core", shift("core", 1))], axis=0)
+    a_query = a_query.reshape(16, 1, 1, HEAD_DIM, -1)
 
     def other(parts):
         return [lax.ppermute(p, "core", shift("core", 1)) for p in parts]
 
-    near_b = own_b + near_b + other(own_b) + other(near_b)
+    near_b = (own_b + near_b + other(own_b) + other(near_b[:2])
+              + other(near_b[2:]))
     far_b = far_b + other(far_b)
     gate_a = gate_of((x * 4 + z) * 2 + core, 1)
     gate_b = gate_of(16 + (x * 4 + z) * 3, 3)
 
-    out_a = attend(a, gate_a, [own_a, up_a, down_a] + far_a)
-    out_a = spread(out_a, wide)
-    state = attend(b, gate_b, near_b, final=False)
-    out_b = attend(b, gate_b, far_b, state)
+    out_a = attend(a_query, gate_a, [own_a, up_a, down_a] + far_a)
+    out_a = out_a.reshape(2, 8, HEAD_DIM, -1)
+    out_a = jnp.where(core == 0, out_a, out_a[::-1]).transpose(1, 0, 2, 3)
+    out_a = spread(out_a.reshape(16, 1, HEAD_DIM, -1), wide)
+    state = attend(b_query, gate_b, near_b, final=False)
+    out_b = attend(b_query, gate_b, far_b, state)
     out_b = spread(out_b, narrow)
     return collect(out_a, out_b)
 

time: 237 us -> 248 us (1.046)
  waiting for transfers between devices: 74.9 us -> 82.3 us
  starting transfers between devices: 27.8 us -> 30.5 us
    ppermute x1, waiting for transfers between devices: 0.01 us -> 26.3 us  [block_attention(): lax.ppermute(down_a[8:], 'y', shift('y', -1))]
    ppermute x1, waiting for transfers between devices: 22.8 us -> 0.01 us  [block_attention(): lax.ppermute(up_a[:8], 'y', shift('y', 1))]
    ppermute x1, waiting for transfers between devices: 0.01 us -> 9.03 us  [ring(): up_low = lax.ppermute(low, axis, shift(axis, 1))]
    all_to_all x2 -> x3, waiting for transfers between devices: 15 us -> 8.88 us  [the longest x1 8.88 us: block_attention(): own_a = spread(a, wide).reshape(16, 1, 2, HEAD_DIM, -1)]
    ppermute x1, waiting for transfers between devices: 9.69 us -> 15.4 us  [ring(): up_high = lax.ppermute(high, axis, shift(axis, 1))]
    all_to_all x1, waiting for transfers between devices: 26 us -> 22.6 us  [block_attention(): b = spread(b, narrow)]
    all_to_all x2 -> x3, starting transfers between devices: 10.8 us -> 13.8 us  [the longest x1 6.41 us: block_attention(): own_a = spread(a, wide).reshape(16, 1, 2, HEAD_DIM, -1)]
  transfers between devices with their start and end apart: 21 -> 23, of which waited for: 5 -> 5; matrix products, arithmetic and copies ran while one was open for 4% -> 4% of each run, Pallas kernels for 23% -> 22%
where the time goes in v3:
time: 248 us; the launch traced here: 247 us
  waiting for transfers between devices  82.3 us (33%)
  blocking collectives  61.5 us (25%)
  Pallas kernels  59.8 us (24%)
  starting transfers between devices  30.5 us (12%)
  local copies, waits for them, and re-layouts  6.91 us (3%)
  other arithmetic  2.61 us (1%)
    all_to_all x1, blocking collectives, block_attention(): out_b = spread(out_b, narrow)  61.5 us
    pallas_call x3, Pallas kernels, attend(): pl.pallas_call(functools.partial(attend_kernel, sizes=sizes, resume=state...  46.4 us
    ppermute x1, waiting for transfers between devices, block_attention(): lax.ppermute(down_a[8:], 'y', shift('y', -1))  26.3 us
    all_to_all x1, waiting for transfers between devices, block_attention(): b = spread(b, narrow)  22.6 us
    ppermute x1, waiting for transfers between devices, ring(): up_high = lax.ppermute(high, axis, shift(axis, 1))  15.4 us
    pallas_call x2, Pallas kernels, prepare(): pl.pallas_call(functools.partial(prep_kernel, tensors=kinds, plan=plan),...  11.9 us
    ppermute x1, waiting for transfers between devices, ring(): up_low = lax.ppermute(low, axis, shift(axis, 1))  9.03 us
    all_to_all x1, waiting for transfers between devices, block_attention(): own_a = spread(a, wide).reshape(16, 1, 2, HEAD_DIM, -1)  8.88 us
  transfers between devices with their start and end apart: 23, of which 5 were waited for; matrix products, arithmetic and copies ran while one was open for 4% of the time, Pallas kernels for 22%

profile of v3, /device:TPU:24, one launch (start us, length us, event | category | flops | bytes accessed | tf_op | source)
XLA Modules:
  0.0 246.8 jit_solution(10356541623666775841)
XLA Ops:
  0.0 4.1 %shard_map.101 = bf16[16,2,128,128]{3,2,1,0:T(8,128)(2,1)} custom-call(s32[1]{0:T(128)} %bitcast.block_ref, f32[1,128]{1,0:T(1,128)} %constant.47.inv_hbm, bf16[128,5120]{1,0:T(8,128)(2,1)} %refs_0_.3, bf16[128,5120]{1,0:T(8,128)(2,1)} %refs_1_.3, f32[40,128]{1,0:T(8,128)} %bitcast.29), custom_call_target="tpu_custom_call" | custom-call | tf_op jit(solution)/shard_map/pallas_call | solution.py:119
  4.2 6.4 %all-to-all-start = ((bf16[16,2,128,128]{3,2,1,0:T(8,128)(2,1)}), bf16[16,2,128,128]{3,2,1,0:T(8,128)(2,1)}, u32[]{:S(2)}, u32[]{:S(2)}) async-start(bf16[16,2,128,128]{3,2,1,0:T(8,128)(2,1)} %shard_map.101), calls=%async_computation | async-start | bytes 2097152 | tf_op jit(solution)/shard_map/all_to_all | solution.py:384
  10.6 7.7 %shard_map.100 = (bf16[8,8,128,128]{3,2,1,0:T(8,128)(2,1)}, bf16[8,3,128,128]{3,2,1,0:T(8,128)(2,1)}) custom-call(s32[1]{0:T(128)} %bitcast.block_ref, f32[1,128]{1,0:T(1,128)} %constant.47.inv_hbm, bf16[128,5120]{1,0:T(8,128)(2,1)} %refs_0_.2, bf16[128,5120]{1,0:T(8,128)(2,1)} %refs_0_.3, bf16[128,5120]{1,0:T(8,128)(2,1)} %refs_1_.3, f32[40,128]{1,0:T(8,128)} %bitcast.31, ...), custom_call_target="tpu_custom_call" | custom-call | tf_op jit(solution)/shard_map/pallas_call | solution.py:119
  18.3 8.9 %all-to-all-done = bf16[16,2,128,128]{3,2,1,0:T(8,128)(2,1)} async-done(((bf16[16,2,128,128]{3,2,1,0:T(8,128)(2,1)}), bf16[16,2,128,128]{3,2,1,0:T(8,128)(2,1)}, u32[]{:S(2)}, u32[]{:S(2)}) %all-to-all-start) | async-done | bytes 1048608 | tf_op jit(solution)/shard_map/all_to_all | solution.py:384
  27.2 3.6 %all-to-all-start.1 = ((bf16[8,8,128,128]{3,2,1,0:T(8,128)(2,1)}), bf16[8,8,128,128]{3,2,1,0:T(8,128)(2,1)S(1)}, u32[]{:S(2)}, u32[]{:S(2)}) async-start(bf16[8,8,128,128]{3,2,1,0:T(8,128)(2,1)} %get-tuple-element.15), calls=%async_computation.1 | async-start | bytes 4194304 | tf_op jit(solution)/shard_map/all_to_all | solution.py:390
  30.8 0.8 collective-permute-start.2
  31.6 2.5 %collective-permute-start.1 = (bf16[16,1,2,128,128]{4,3,2,1,0:T(8,128)(2,1)}, bf16[16,1,2,128,128]{4,3,2,1,0:T(8,128)(2,1)}, u32[]{:S(2)}, u32[]{:S(2)}) collective-permute-start(bf16[16,1,2,128,128]{4,3,2,1,0:T(8,128)(2,1)} %bitcast.3.refs_2_), channel_id=1, source_target_pairs={{0,2},{2,4},{4,6},{6,0},{1,3},{3,5},{5,7},{7,1},{8,10},{10,12},{12... | collective-permute-start | bytes 3145736 | tf_op jit(solution)/shard_map/ppermute | solution.py:385
  34.1 22.6 %all-to-all-done.1 = bf16[8,8,128,128]{3,2,1,0:T(8,128)(2,1)S(1)} async-done(((bf16[8,8,128,128]{3,2,1,0:T(8,128)(2,1)}), bf16[8,8,128,128]{3,2,1,0:T(8,128)(2,1)S(1)}, u32[]{:S(2)}, u32[]{:S(2)}) %all-to-all-start.1) | async-done | bytes 2097184 | tf_op jit(solution)/shard_map/all_to_all | solution.py:390
  56.7 1.3 fusion.7
  58.7 1.1 slice.17
  60.3 1.1 slice.16
  61.4 2.9 %collective-permute-start.3 = (bf16[8,1,2,128,128]{4,3,2,1,0:T(8,128)(2,1)S(1)}, bf16[8,1,2,128,128]{4,3,2,1,0:T(8,128)(2,1)}, u32[]{:S(2)}, u32[]{:S(2)}) collective-permute-start(bf16[8,1,2,128,128]{4,3,2,1,0:T(8,128)(2,1)S(1)} %slice.16), channel_id=1, source_target_pairs={{0,2},{2,4},{4,6},{6,0},{1,3},{3,5},{5,7},{7,1},{8,10},{10,12},{12... | collective-permute-start | bytes 1572872 | tf_op jit(solution)/shard_map/ppermute | solution.py:387
  64.4 26.3 %collective-permute-done.4.refs_6_ = bf16[8,1,2,128,128]{4,3,2,1,0:T(8,128)(2,1)} collective-permute-done((bf16[8,1,2,128,128]{4,3,2,1,0:T(8,128)(2,1)S(1)}, bf16[8,1,2,128,128]{4,3,2,1,0:T(8,128)(2,1)}, u32[]{:S(2)}, u32[]{:S(2)}) %collective-permute-start.4) | collective-permute-done | bytes 524320 | tf_op jit(solution)/shard_map/ppermute | solution.py:388
  90.7 2.1 collective-permute-start.7
  92.8 1.2 collective-permute-start.11
  94.7 1.3 convolution_reduce_fusion
  96.1 1.1 fusion
  97.9 3.6 %all-to-all-start.3 = ((bf16[8,3,128,128]{3,2,1,0:T(8,128)(2,1)}), bf16[8,3,128,128]{3,2,1,0:T(8,128)(2,1)S(1)}, u32[]{:S(2)}, u32[]{:S(2)}) async-start(bf16[8,3,128,128]{3,2,1,0:T(8,128)(2,1)} %get-tuple-element.18), calls=%async_computation.3 | async-start | bytes 1572864 | tf_op jit(solution)/shard_map/all_to_all | solution.py:394
  101.5 0.8 maximum_bitcast_fusion.refs_0_
  102.4 9.0 %collective-permute-done.5.refs_4_ = bf16[4,3,2,128,128]{4,3,2,1,0:T(8,128)(2,1)} collective-permute-done((bf16[4,3,2,128,128]{4,3,2,1,0:T(8,128)(2,1)}, bf16[4,3,2,128,128]{4,3,2,1,0:T(8,128)(2,1)}, u32[]{:S(2)}, u32[]{:S(2)}) %collective-permute-start.5) | collective-permute-done | bytes 786464 | tf_op jit(solution)/shard_map/ppermute | solution.py:345
  111.4 1.2 collective-permute-start.6
  112.9 15.4 %collective-permute-done.11.refs_6_ = bf16[4,3,2,128,128]{4,3,2,1,0:T(8,128)(2,1)} collective-permute-done((bf16[4,3,2,128,128]{4,3,2,1,0:T(8,128)(2,1)}, bf16[4,3,2,128,128]{4,3,2,1,0:T(8,128)(2,1)}, u32[]{:S(2)}, u32[]{:S(2)}) %collective-permute-start.11) | collective-permute-done | bytes 786464 | tf_op jit(solution)/shard_map/ppermute | solution.py:347
  129.0 17.6 %shard_map.102 = bf16[16,1,128,128]{3,2,1,0:T(8,128)(2,1)} custom-call(bf16[16,1,1,128,128]{4,3,2,1,0:T(8,128)(2,1)} %maximum_bitcast_fusion.refs_0_, f32[1,128,128]{2,1,0:T(8,128)} %broadcast_in_dim.24.refs_1_, bf16[16,1,2,128,128]{4,3,2,1,0:T(8,128)(2,1)} %bitcast.3.refs_2_, bf16[16,1,2,128,128]{4,3,2,1,0:T(8,128)(2,1)} %collective-permute-done.1.refs_3_, ...), custom_call_target="tpu_custom_call" | custom-call | flops 17179869184 | bytes 4194304 | tf_op jit(solution)/shard_map/pallas_call | solution.py:290
  146.6 1.1 copy.19
  147.6 0.9 reverse_select_fusion
  148.6 0.9 copy-done
  149.5 3.8 %all-to-all-start.2 = ((bf16[16,1,128,128]{3,2,1,0:T(8,128)(2,1)}), bf16[16,1,128,128]{3,2,1,0:T(8,128)(2,1)S(1)}, u32[]{:S(2)}, u32[]{:S(2)}) async-start(bf16[16,1,128,128]{3,2,1,0:T(8,128)(2,1)} %bitcast.11), calls=%async_computation.2 | async-start | bytes 1048576 | tf_op jit(solution)/shard_map/all_to_all | solution.py:412
  154.1 0.8 broadcast_in_dim.26.refs_1_
  154.9 19.8 %shard_map.103 = (f32[3,16,1024]{2,1,0:T(8,128)}, f32[3,128,1024]{2,1,0:T(8,128)}) custom-call(bf16[8,3,1,128,128]{4,3,2,1,0:T(8,128)(2,1)} %bitcast.26, f32[3,128,128]{2,1,0:T(8,128)} %broadcast_in_dim.26.refs_1_, bf16[4,3,2,128,128]{4,3,2,1,0:T(8,128)(2,1)} %bitcast.15.refs_2_, bf16[4,3,2,128,128]{4,3,2,1,0:T(8,128)(2,1)} %bitcast.16.refs_3_, ...), custom_call_target="tpu_custom_call" | custom-call | flops 19327352832 | bytes 9437184 | tf_op jit(solution)/shard_map/pallas_call | solution.py:290
  174.8 9.0 %shard_map.104 = bf16[8,3,128,128]{3,2,1,0:T(8,128)(2,1)} custom-call(bf16[8,3,1,128,128]{4,3,2,1,0:T(8,128)(2,1)} %bitcast.27, f32[3,128,128]{2,1,0:T(8,128)} %broadcast_in_dim.26.refs_1_, bf16[4,3,2,128,128]{4,3,2,1,0:T(8,128)(2,1)} %collective-permute-done.6.refs_2_, bf16[4,3,2,128,128]{4,3,2,1,0:T(8,128)(2,1)} %collective-permute-done.8.refs_3_, ...), custom_call_target="tpu_custom_call" | custom-call | flops 6442450944 | bytes 3145728 | tf_op jit(solution)/shard_map/pallas_call | solution.py:290
  183.9 61.5 %all_to_all.25.refs_1_ = bf16[8,3,128,128]{3,2,1,0:T(8,128)(2,1)S(1)} all-to-all(bf16[8,3,128,128]{3,2,1,0:T(8,128)(2,1)} %shard_map.104), channel_id=1, replica_groups=mesh['expert'=2,'x'=2,'z'=4,'y'=4,'core'=2] {'x','z'}, dimensions={0} | all-to-all | bytes 1572864 | tf_op jit(solution)/shard_map/all_to_all | solution.py:415
  245.3 1.5 post.1
  (36 shorter events, 4.0 us)
Async XLA Ops:
  4.2 23.0 %all-to-all-start = ((bf16[16,2,128,128]{3,2,1,0:T(8,128)(2,1)}), bf16[16,2,128,128]{3,2,1,0:T(8,128)(2,1)}, u32[]{:S(2)}, u32[]{:S(2)}) async-start(bf16[16,2,128,128]{3,2,1,0:T(8,128)(2,1)} %shard_map.101), calls=%async_computation | async-start | bytes 2097152 | tf_op jit(solution)/shard_map/all_to_all | solution.py:384
  27.2 29.5 %all-to-all-start.1 = ((bf16[8,8,128,128]{3,2,1,0:T(8,128)(2,1)}), bf16[8,8,128,128]{3,2,1,0:T(8,128)(2,1)S(1)}, u32[]{:S(2)}, u32[]{:S(2)}) async-start(bf16[8,8,128,128]{3,2,1,0:T(8,128)(2,1)} %get-tuple-element.15), calls=%async_computation.1 | async-start | bytes 4194304 | tf_op jit(solution)/shard_map/all_to_all | solution.py:390
  30.8 27.9 %collective-permute-start.2 = (bf16[16,1,2,128,128]{4,3,2,1,0:T(8,128)(2,1)}, bf16[16,1,2,128,128]{4,3,2,1,0:T(8,128)(2,1)}, u32[]{:S(2)}, u32[]{:S(2)}) collective-permute-start(bf16[16,1,2,128,128]{4,3,2,1,0:T(8,128)(2,1)} %bitcast.3.refs_2_), channel_id=1, source_target_pairs={{0,6},{2,0},{4,2},{6,4},{1,7},{3,1},{5,3},{7,5},{8,14},{10,8},{12,... | collective-permute-start | bytes 3145736 | tf_op jit(solution)/shard_map/ppermute | solution.py:386
  31.6 28.7 %collective-permute-start.1 = (bf16[16,1,2,128,128]{4,3,2,1,0:T(8,128)(2,1)}, bf16[16,1,2,128,128]{4,3,2,1,0:T(8,128)(2,1)}, u32[]{:S(2)}, u32[]{:S(2)}) collective-permute-start(bf16[16,1,2,128,128]{4,3,2,1,0:T(8,128)(2,1)} %bitcast.3.refs_2_), channel_id=1, source_target_pairs={{0,2},{2,4},{4,6},{6,0},{1,3},{3,5},{5,7},{7,1},{8,10},{10,12},{12... | collective-permute-start | bytes 3145736 | tf_op jit(solution)/shard_map/ppermute | solution.py:385
  58.0 34.8 %collective-permute-start.13 = (bf16[4,3,2,128,128]{4,3,2,1,0:T(8,128)(2,1)}, bf16[4,3,2,128,128]{4,3,2,1,0:T(8,128)(2,1)}, u32[]{:S(2)}, u32[]{:S(2)}) collective-permute-start(bf16[4,3,2,128,128]{4,3,2,1,0:T(8,128)(2,1)} %bitcast.15.refs_2_), channel_id=1, source_target_pairs={{0,1},{1,0},{2,3},{3,2},{4,5},{5,4},{6,7},{7,6},{8,9},{9,8},{10,11... | collective-permute-start | bytes 2359304 | tf_op jit(solution)/shard_map/ppermute | solution.py:401
  58.0 36.1 %collective-permute-start.12 = (bf16[4,3,2,128,128]{4,3,2,1,0:T(8,128)(2,1)}, bf16[4,3,2,128,128]{4,3,2,1,0:T(8,128)(2,1)}, u32[]{:S(2)}, u32[]{:S(2)}) collective-permute-start(bf16[4,3,2,128,128]{4,3,2,1,0:T(8,128)(2,1)} %bitcast.15.refs_2_), channel_id=1, source_target_pairs={{0,6},{2,0},{4,2},{6,4},{1,7},{3,1},{5,3},{7,5},{8,14},{10,8},{12,... | collective-permute-start | bytes 2359304 | tf_op jit(solution)/shard_map/ppermute | solution.py:348
  59.8 30.9 %collective-permute-start.4 = (bf16[8,1,2,128,128]{4,3,2,1,0:T(8,128)(2,1)S(1)}, bf16[8,1,2,128,128]{4,3,2,1,0:T(8,128)(2,1)}, u32[]{:S(2)}, u32[]{:S(2)}) collective-permute-start(bf16[8,1,2,128,128]{4,3,2,1,0:T(8,128)(2,1)S(1)} %slice.17), channel_id=1, source_target_pairs={{0,6},{2,0},{4,2},{6,4},{1,7},{3,1},{5,3},{7,5},{8,14},{10,8},{12,... | collective-permute-start | bytes 1572872 | tf_op jit(solution)/shard_map/ppermute | solution.py:388
  61.4 29.3 %collective-permute-start.3 = (bf16[8,1,2,128,128]{4,3,2,1,0:T(8,128)(2,1)S(1)}, bf16[8,1,2,128,128]{4,3,2,1,0:T(8,128)(2,1)}, u32[]{:S(2)}, u32[]{:S(2)}) collective-permute-start(bf16[8,1,2,128,128]{4,3,2,1,0:T(8,128)(2,1)S(1)} %slice.16), channel_id=1, source_target_pairs={{0,2},{2,4},{4,6},{6,0},{1,3},{3,5},{5,7},{7,1},{8,10},{10,12},{12... | collective-permute-start | bytes 1572872 | tf_op jit(solution)/shard_map/ppermute | solution.py:387
  64.3 26.4 %collective-permute-start = (bf16[8,1,128,128]{3,2,0,1:T(8,128)(2,1)S(1)}, bf16[8,1,128,128]{3,2,0,1:T(8,128)(2,1)S(1)}, u32[]{:S(2)}, u32[]{:S(2)}) collective-permute-start(bf16[8,1,128,128]{3,2,0,1:T(8,128)(2,1)S(1)} %get-tuple-element.24), channel_id=1, source_target_pairs={{0,1},{1,0},{2,3},{3,2},{4,5},{5,4},{6,7},{7,6},{8,9},{9,8},{10,11... | collective-permute-start | bytes 786440 | tf_op jit(solution)/shard_map/ppermute | solution.py:397
  90.7 20.7 %collective-permute-start.5 = (bf16[4,3,2,128,128]{4,3,2,1,0:T(8,128)(2,1)}, bf16[4,3,2,128,128]{4,3,2,1,0:T(8,128)(2,1)}, u32[]{:S(2)}, u32[]{:S(2)}) collective-permute-start(bf16[4,3,2,128,128]{4,3,2,1,0:T(8,128)(2,1)} %bitcast.15.refs_2_), channel_id=1, source_target_pairs={{0,2},{2,4},{4,6},{6,0},{1,3},{3,5},{5,7},{7,1},{8,10},{10,12},{12... | collective-permute-start | bytes 2359304 | tf_op jit(solution)/shard_map/ppermute | solution.py:345
  90.7 20.7 %collective-permute-start.14 = (bf16[4,3,2,128,128]{4,3,2,1,0:T(8,128)(2,1)}, bf16[4,3,2,128,128]{4,3,2,1,0:T(8,128)(2,1)}, u32[]{:S(2)}, u32[]{:S(2)}) collective-permute-start(bf16[4,3,2,128,128]{4,3,2,1,0:T(8,128)(2,1)} %bitcast.16.refs_3_), channel_id=1, source_target_pairs={{0,1},{1,0},{2,3},{3,2},{4,5},{5,4},{6,7},{7,6},{8,9},{9,8},{10,11... | collective-permute-start | bytes 2359304 | tf_op jit(solution)/shard_map/ppermute | solution.py:401
  90.7 21.9 %collective-permute-start.7 = (bf16[4,3,2,128,128]{4,3,2,1,0:T(8,128)(2,1)}, bf16[4,3,2,128,128]{4,3,2,1,0:T(8,128)(2,1)}, u32[]{:S(2)}, u32[]{:S(2)}) collective-permute-start(bf16[4,3,2,128,128]{4,3,2,1,0:T(8,128)(2,1)} %bitcast.16.refs_3_), channel_id=1, source_target_pairs={{0,6},{2,0},{4,2},{6,4},{1,7},{3,1},{5,3},{7,5},{8,14},{10,8},{12,... | collective-permute-start | bytes 2359304 | tf_op jit(solution)/shard_map/ppermute | solution.py:346
  92.8 35.5 %collective-permute-start.11 = (bf16[4,3,2,128,128]{4,3,2,1,0:T(8,128)(2,1)}, bf16[4,3,2,128,128]{4,3,2,1,0:T(8,128)(2,1)}, u32[]{:S(2)}, u32[]{:S(2)}) collective-permute-start(bf16[4,3,2,128,128]{4,3,2,1,0:T(8,128)(2,1)} %bitcast.16.refs_3_), channel_id=1, source_target_pairs={{0,2},{2,4},{4,6},{6,0},{1,3},{3,5},{5,7},{7,1},{8,10},{10,12},{12... | collective-permute-start | bytes 2359304 | tf_op jit(solution)/shard_map/ppermute | solution.py:347
  94.0 34.2 %collective-permute-start.18 = (bf16[4,3,2,128,128]{4,3,2,1,0:T(8,128)(2,1)}, bf16[4,3,2,128,128]{4,3,2,1,0:T(8,128)(2,1)}, u32[]{:S(2)}, u32[]{:S(2)}) collective-permute-start(bf16[4,3,2,128,128]{4,3,2,1,0:T(8,128)(2,1)} %collective-permute-done.12.refs_7_), channel_id=1, source_target_pairs={{0,1},{1,0},{2,3},{3,2},{4,5},{5,4},{6,7},{7,6},{8,9},{9,8},{10,11... | collective-permute-start | bytes 2359304 | tf_op jit(solution)/shard_map/ppermute | solution.py:401
  97.9 50.7 %all-to-all-start.3 = ((bf16[8,3,128,128]{3,2,1,0:T(8,128)(2,1)}), bf16[8,3,128,128]{3,2,1,0:T(8,128)(2,1)S(1)}, u32[]{:S(2)}, u32[]{:S(2)}) async-start(bf16[8,3,128,128]{3,2,1,0:T(8,128)(2,1)} %get-tuple-element.18), calls=%async_computation.3 | async-start | bytes 1572864 | tf_op jit(solution)/shard_map/all_to_all | solution.py:394
  111.4 42.7 %collective-permute-start.15 = (bf16[4,3,2,128,128]{4,3,2,1,0:T(8,128)(2,1)}, bf16[4,3,2,128,128]{4,3,2,1,0:T(8,128)(2,1)}, u32[]{:S(2)}, u32[]{:S(2)}) collective-permute-start(bf16[4,3,2,128,128]{4,3,2,1,0:T(8,128)(2,1)} %collective-permute-done.5.refs_4_), channel_id=1, source_target_pairs={{0,1},{1,0},{2,3},{3,2},{4,5},{5,4},{6,7},{7,6},{8,9},{9,8},{10,11... | collective-permute-start | bytes 2359304 | tf_op jit(solution)/shard_map/ppermute | solution.py:401
  111.4 41.9 %collective-permute-start.6 = (bf16[4,3,2,128,128]{4,3,2,1,0:T(8,128)(2,1)}, bf16[4,3,2,128,128]{4,3,2,1,0:T(8,128)(2,1)}, u32[]{:S(2)}, u32[]{:S(2)}) collective-permute-start(bf16[4,3,2,128,128]{4,3,2,1,0:T(8,128)(2,1)} %collective-permute-done.5.refs_4_), channel_id=1, source_target_pairs={{0,2},{2,4},{4,6},{6,0},{1,3},{3,5},{5,7},{7,1},{8,10},{10,12},{12... | collective-permute-start | bytes 2359304 | tf_op jit(solution)/shard_map/ppermute | solution.py:349
  112.6 41.5 %collective-permute-start.16 = (bf16[4,3,2,128,128]{4,3,2,1,0:T(8,128)(2,1)}, bf16[4,3,2,128,128]{4,3,2,1,0:T(8,128)(2,1)}, u32[]{:S(2)}, u32[]{:S(2)}) collective-permute-start(bf16[4,3,2,128,128]{4,3,2,1,0:T(8,128)(2,1)} %collective-permute-done.7.refs_5_), channel_id=1, source_target_pairs={{0,1},{1,0},{2,3},{3,2},{4,5},{5,4},{6,7},{7,6},{8,9},{9,8},{10,11... | collective-permute-start | bytes 2359304 | tf_op jit(solution)/shard_map/ppermute | solution.py:401
  128.3 25.5 %collective-permute-start.8 = (bf16[4,3,2,128,128]{4,3,2,1,0:T(8,128)(2,1)}, bf16[4,3,2,128,128]{4,3,2,1,0:T(8,128)(2,1)}, u32[]{:S(2)}, u32[]{:S(2)}) collective-permute-start(bf16[4,3,2,128,128]{4,3,2,1,0:T(8,128)(2,1)} %collective-permute-done.7.refs_5_), channel_id=1, source_target_pairs={{0,6},{2,0},{4,2},{6,4},{1,7},{3,1},{5,3},{7,5},{8,14},{10,8},{12,... | collective-permute-start | bytes 2359304 | tf_op jit(solution)/shard_map/ppermute | solution.py:350
  128.3 25.9 %collective-permute-start.17 = (bf16[4,3,2,128,128]{4,3,2,1,0:T(8,128)(2,1)}, bf16[4,3,2,128,128]{4,3,2,1,0:T(8,128)(2,1)}, u32[]{:S(2)}, u32[]{:S(2)}) collective-permute-start(bf16[4,3,2,128,128]{4,3,2,1,0:T(8,128)(2,1)} %collective-permute-done.11.refs_6_), channel_id=1, source_target_pairs={{0,1},{1,0},{2,3},{3,2},{4,5},{5,4},{6,7},{7,6},{8,9},{9,8},{10,11... | collective-permute-start | bytes 2359304 | tf_op jit(solution)/shard_map/ppermute | solution.py:401
  148.6 0.9 copy-start
  149.5 34.4 %all-to-all-start.2 = ((bf16[16,1,128,128]{3,2,1,0:T(8,128)(2,1)}), bf16[16,1,128,128]{3,2,1,0:T(8,128)(2,1)S(1)}, u32[]{:S(2)}, u32[]{:S(2)}) async-start(bf16[16,1,128,128]{3,2,1,0:T(8,128)(2,1)} %bitcast.11), calls=%async_computation.2 | async-start | bytes 1048576 | tf_op jit(solution)/shard_map/all_to_all | solution.py:412
  153.3 21.5 %collective-permute-start.9 = (bf16[4,3,2,128,128]{4,3,2,1,0:T(8,128)(2,1)}, bf16[4,3,2,128,128]{4,3,2,1,0:T(8,128)(2,1)}, u32[]{:S(2)}, u32[]{:S(2)}) collective-permute-start(bf16[4,3,2,128,128]{4,3,2,1,0:T(8,128)(2,1)} %collective-permute-done.6.refs_2_), channel_id=1, source_target_pairs={{0,1},{1,0},{2,3},{3,2},{4,5},{5,4},{6,7},{7,6},{8,9},{9,8},{10,11... | collective-permute-start | bytes 2359304 | tf_op jit(solution)/shard_map/ppermute | solution.py:401
  153.8 21.0 %collective-permute-start.10 = (bf16[4,3,2,128,128]{4,3,2,1,0:T(8,128)(2,1)}, bf16[4,3,2,128,128]{4,3,2,1,0:T(8,128)(2,1)}, u32[]{:S(2)}, u32[]{:S(2)}) collective-permute-start(bf16[4,3,2,128,128]{4,3,2,1,0:T(8,128)(2,1)} %collective-permute-done.8.refs_3_), channel_id=1, source_target_pairs={{0,1},{1,0},{2,3},{3,2},{4,5},{5,4},{6,7},{7,6},{8,9},{9,8},{10,11... | collective-permute-start | bytes 2359304 | tf_op jit(solution)/shard_map/ppermute | solution.py:401

commit v4 on v3

--- a/solution.py
+++ b/solution.py
@@ -341,6 +341,11 @@
     return [(i, (i + amount) % size) for i in range(size)]
 
 
+def opposed(amount):
+    steps = (amount, -amount)
+    return [(2 * y + c, 2 * ((y + steps[c]) % 4) + c) for y in range(4) for c in range(2)]
+
+
 def ring(low, high, axis):
     up_low = lax.ppermute(low, axis, shift(axis, 1))
     down_high = lax.ppermute(high, axis, shift(axis, -1))
@@ -382,10 +387,9 @@
         (1, tuple(("q", 3, 16 + h) for h in range(3))),
     ))
     own_a = spread(a, wide).reshape(16, 1, 2, HEAD_DIM, -1)
-    up_a = lax.ppermute(own_a, "y", shift("y", 1))
-    down_a = lax.ppermute(own_a, "y", shift("y", -1))
-    far_a = [lax.ppermute(up_a[:8], "y", shift("y", 1)),
-             lax.ppermute(down_a[8:], "y", shift("y", -1))]
+    first_a = lax.ppermute(own_a, ("y", "core"), opposed(1))
+    second_a = lax.ppermute(own_a, ("y", "core"), opposed(-1))
+    far_a = lax.ppermute(first_a, ("y", "core"), opposed(1))
     b, own_a = lax.optimization_barrier((b, own_a))
     b = spread(b, narrow)
     own_b = [b[:4, :6].reshape(4, 3, 2, HEAD_DIM, -1), b[4:, :6].reshape(4, 3, 2, HEAD_DIM, -1)]
@@ -400,13 +404,12 @@
     def other(parts):
         return [lax.ppermute(p, "core", shift("core", 1)) for p in parts]
 
-    near_b = (own_b + near_b + other(own_b) + other(near_b[:2])
-              + other(near_b[2:]))
-    far_b = far_b + other(far_b)
+    far_b = other(near_b[2:]) + far_b + other(far_b)
+    near_b = own_b + near_b + other(own_b) + other(near_b[:2])
     gate_a = gate_of((x * 4 + z) * 2 + core, 1)
     gate_b = gate_of(16 + (x * 4 + z) * 3, 3)
 
-    out_a = attend(a_query, gate_a, [own_a, up_a, down_a] + far_a)
+    out_a = attend(a_query, gate_a, [own_a, first_a, second_a, far_a])
     out_a = out_a.reshape(2, 8, HEAD_DIM, -1)
     out_a = jnp.where(core == 0, out_a, out_a[::-1]).transpose(1, 0, 2, 3)
     out_a = spread(out_a.reshape(16, 1, HEAD_DIM, -1), wide)

time: 248 us -> 234 us (0.944)
  waiting for transfers between devices: 82.3 us -> 67.5 us
    all_to_all x1, waiting for transfers between devices: 22.6 us -> 0.01 us  [block_attention(): b = spread(b, narrow)]
    ppermute x4 -> x3, waiting for transfers between devices: 26.3 us -> 39.1 us  [the longest x1 23.3 us: block_attention(): first_a = lax.ppermute(own_a, ('y', 'core'), opposed(1))]
    ppermute x4 -> x3, starting transfers between devices: 6.68 us -> 3.19 us  [the longest x1 1.8 us: block_attention(): second_a = lax.ppermute(own_a, ('y', 'core'), opposed(-1))]
    ppermute x1, waiting for transfers between devices: 15.4 us -> 12.8 us  [ring(): up_high = lax.ppermute(high, axis, shift(axis, 1))]
  transfers between devices with their start and end apart: 23 -> 22, of which waited for: 5 -> 5; matrix products, arithmetic and copies ran while one was open for 4% -> 4% of each run, Pallas kernels for 22% -> 23%
where the time goes in v4:
time: 234 us; the launch traced here: 233 us
  waiting for transfers between devices  67.5 us (29%)
  blocking collectives  61.6 us (26%)
  Pallas kernels  59.9 us (26%)
  starting transfers between devices  32.3 us (14%)
  local copies, waits for them, and re-layouts  5.46 us (2%)
  other arithmetic  2.71 us (1%)
  matrix products  2.4 us (1%)
    all_to_all x1, blocking collectives, block_attention(): out_b = spread(out_b, narrow)  61.6 us
    pallas_call x3, Pallas kernels, attend(): pl.pallas_call(functools.partial(attend_kernel, sizes=sizes, resume=state...  46.5 us
    ppermute x1, waiting for transfers between devices, block_attention(): first_a = lax.ppermute(own_a, ('y', 'core'), opposed(1))  23.3 us
    ppermute x1, waiting for transfers between devices, block_attention(): far_a = lax.ppermute(first_a, ('y', 'core'), opposed(1))  15.8 us
    ppermute x1, waiting for transfers between devices, ring(): up_high = lax.ppermute(high, axis, shift(axis, 1))  12.8 us
    pallas_call x2, Pallas kernels, prepare(): pl.pallas_call(functools.partial(prep_kernel, tensors=kinds, plan=plan),...  11.9 us
    all_to_all x1, waiting for transfers between devices, block_attention(): own_a = spread(a, wide).reshape(16, 1, 2, HEAD_DIM, -1)  8.8 us
    ppermute x1, waiting for transfers between devices, ring(): up_low = lax.ppermute(low, axis, shift(axis, 1))  6.76 us
  transfers between devices with their start and end apart: 22, of which 5 were waited for; matrix products, arithmetic and copies ran while one was open for 4% of the time, Pallas kernels for 23%

profile of v4, /device:TPU:24, one launch (start us, length us, event | category | flops | bytes accessed | tf_op | source)
XLA Modules:
  0.0 232.8 jit_solution(2973178407944893987)
XLA Ops:
  0.0 4.1 %shard_map.101 = bf16[16,2,128,128]{3,2,1,0:T(8,128)(2,1)} custom-call(s32[1]{0:T(128)} %bitcast.block_ref, f32[1,128]{1,0:T(1,128)} %constant.47.inv_hbm, bf16[128,5120]{1,0:T(8,128)(2,1)} %refs_0_.3, bf16[128,5120]{1,0:T(8,128)(2,1)} %refs_1_.3, f32[40,128]{1,0:T(8,128)} %bitcast.29), custom_call_target="tpu_custom_call" | custom-call | tf_op jit(solution)/shard_map/pallas_call | solution.py:119
  4.2 6.4 %all-to-all-start = ((bf16[16,2,128,128]{3,2,1,0:T(8,128)(2,1)}), bf16[16,2,128,128]{3,2,1,0:T(8,128)(2,1)}, u32[]{:S(2)}, u32[]{:S(2)}) async-start(bf16[16,2,128,128]{3,2,1,0:T(8,128)(2,1)} %shard_map.101), calls=%async_computation | async-start | bytes 2097152 | tf_op jit(solution)/shard_map/all_to_all | solution.py:389
  10.6 7.8 %shard_map.100 = (bf16[8,8,128,128]{3,2,1,0:T(8,128)(2,1)}, bf16[8,3,128,128]{3,2,1,0:T(8,128)(2,1)}) custom-call(s32[1]{0:T(128)} %bitcast.block_ref, f32[1,128]{1,0:T(1,128)} %constant.47.inv_hbm, bf16[128,5120]{1,0:T(8,128)(2,1)} %refs_0_.2, bf16[128,5120]{1,0:T(8,128)(2,1)} %refs_0_.3, bf16[128,5120]{1,0:T(8,128)(2,1)} %refs_1_.3, f32[40,128]{1,0:T(8,128)} %bitcast.31, ...), custom_call_target="tpu_custom_call" | custom-call | tf_op jit(solution)/shard_map/pallas_call | solution.py:119
  18.4 8.8 %all-to-all-done = bf16[16,2,128,128]{3,2,1,0:T(8,128)(2,1)} async-done(((bf16[16,2,128,128]{3,2,1,0:T(8,128)(2,1)}), bf16[16,2,128,128]{3,2,1,0:T(8,128)(2,1)}, u32[]{:S(2)}, u32[]{:S(2)}) %all-to-all-start) | async-done | bytes 1048608 | tf_op jit(solution)/shard_map/all_to_all | solution.py:389
  27.2 3.6 %all-to-all-start.1 = ((bf16[8,8,128,128]{3,2,1,0:T(8,128)(2,1)}), bf16[8,8,128,128]{3,2,1,0:T(8,128)(2,1)S(1)}, u32[]{:S(2)}, u32[]{:S(2)}) async-start(bf16[8,8,128,128]{3,2,1,0:T(8,128)(2,1)} %get-tuple-element.15), calls=%async_computation.1 | async-start | bytes 4194304 | tf_op jit(solution)/shard_map/all_to_all | solution.py:394
  31.1 1.8 collective-permute-start.2
  32.9 23.3 %collective-permute-done.1.refs_3_ = bf16[16,1,2,128,128]{4,3,2,1,0:T(8,128)(2,1)S(1)} collective-permute-done((bf16[16,1,2,128,128]{4,3,2,1,0:T(8,128)(2,1)}, bf16[16,1,2,128,128]{4,3,2,1,0:T(8,128)(2,1)S(1)}, u32[]{:S(2)}, u32[]{:S(2)}) %collective-permute-start.1) | collective-permute-done | bytes 1048608 | tf_op jit(solution)/shard_map/ppermute | solution.py:390
  56.1 1.1 collective-permute-start.3
  57.4 1.2 fusion.7
  58.6 1.6 collective-permute-start.8
  60.6 2.8 %collective-permute-start.4 = (bf16[4,3,2,128,128]{4,3,2,1,0:T(8,128)(2,1)}, bf16[4,3,2,128,128]{4,3,2,1,0:T(8,128)(2,1)}, u32[]{:S(2)}, u32[]{:S(2)}) collective-permute-start(bf16[4,3,2,128,128]{4,3,2,1,0:T(8,128)(2,1)} %bitcast.15.refs_3_), channel_id=1, source_target_pairs={{0,2},{2,4},{4,6},{6,0},{1,3},{3,5},{5,7},{7,1},{8,10},{10,12},{12... | collective-permute-start | bytes 2359304 | tf_op jit(solution)/shard_map/ppermute | solution.py:352
  63.5 0.7 copy-done.1
  64.2 15.8 %collective-permute-done.3.refs_5_ = bf16[16,1,2,128,128]{4,3,2,1,0:T(8,128)(2,1)} collective-permute-done((bf16[16,1,2,128,128]{4,3,2,1,0:T(8,128)(2,1)S(1)}, bf16[16,1,2,128,128]{4,3,2,1,0:T(8,128)(2,1)}, u32[]{:S(2)}, u32[]{:S(2)}) %collective-permute-start.3) | collective-permute-done | bytes 1048608 | tf_op jit(solution)/shard_map/ppermute | solution.py:392
  80.7 1.3 convolution_reduce_fusion
  82.1 1.1 fusion
  83.2 0.8 add_bitcast_fusion
  83.9 4.7 %all-to-all-start.3 = ((bf16[8,3,128,128]{3,2,1,0:T(8,128)(2,1)}), bf16[8,3,128,128]{3,2,1,0:T(8,128)(2,1)S(1)}, u32[]{:S(2)}, u32[]{:S(2)}) async-start(bf16[8,3,128,128]{3,2,1,0:T(8,128)(2,1)} %get-tuple-element.18), calls=%async_computation.3 | async-start | bytes 1572864 | tf_op jit(solution)/shard_map/all_to_all | solution.py:398
  88.7 0.9 maximum_bitcast_fusion.refs_0_
  89.5 6.8 %collective-permute-done.8.refs_4_ = bf16[4,3,2,128,128]{4,3,2,1,0:T(8,128)(2,1)} collective-permute-done((bf16[4,3,2,128,128]{4,3,2,1,0:T(8,128)(2,1)}, bf16[4,3,2,128,128]{4,3,2,1,0:T(8,128)(2,1)}, u32[]{:S(2)}, u32[]{:S(2)}) %collective-permute-start.8) | collective-permute-done | bytes 786464 | tf_op jit(solution)/shard_map/ppermute | solution.py:350
  96.8 12.8 %collective-permute-done.4.refs_6_ = bf16[4,3,2,128,128]{4,3,2,1,0:T(8,128)(2,1)} collective-permute-done((bf16[4,3,2,128,128]{4,3,2,1,0:T(8,128)(2,1)}, bf16[4,3,2,128,128]{4,3,2,1,0:T(8,128)(2,1)}, u32[]{:S(2)}, u32[]{:S(2)}) %collective-permute-start.4) | collective-permute-done | bytes 786464 | tf_op jit(solution)/shard_map/ppermute | solution.py:352
  109.7 1.1 collective-permute-start.9
  110.8 1.2 collective-permute-start.11
  112.6 17.6 %shard_map.102 = bf16[16,1,128,128]{3,2,1,0:T(8,128)(2,1)} custom-call(bf16[16,1,1,128,128]{4,3,2,1,0:T(8,128)(2,1)} %maximum_bitcast_fusion.refs_0_, f32[1,128,128]{2,1,0:T(8,128)} %broadcast_in_dim.24.refs_1_, bf16[16,1,2,128,128]{4,3,2,1,0:T(8,128)(2,1)} %bitcast.3.refs_2_, bf16[16,1,2,128,128]{4,3,2,1,0:T(8,128)(2,1)} %copy-done.3, ...), custom_call_target="tpu_custom_call" | custom-call | flops 17179869184 | bytes 4194304 | tf_op jit(solution)/shard_map/pallas_call | solution.py:290
  130.2 1.1 copy.19
  131.3 1.0 reverse_select_fusion
  132.3 0.9 copy-done
  133.2 5.4 %all-to-all-start.2 = ((bf16[16,1,128,128]{3,2,1,0:T(8,128)(2,1)}), bf16[16,1,128,128]{3,2,1,0:T(8,128)(2,1)S(1)}, u32[]{:S(2)}, u32[]{:S(2)}) async-start(bf16[16,1,128,128]{3,2,1,0:T(8,128)(2,1)} %bitcast.11), calls=%async_computation.2 | async-start | bytes 1048576 | tf_op jit(solution)/shard_map/all_to_all | solution.py:415
  139.9 0.8 broadcast_in_dim.26.refs_1_
  140.7 17.1 %shard_map.103 = (f32[3,16,1024]{2,1,0:T(8,128)}, f32[3,128,1024]{2,1,0:T(8,128)}) custom-call(bf16[8,3,1,128,128]{4,3,2,1,0:T(8,128)(2,1)} %bitcast.26, f32[3,128,128]{2,1,0:T(8,128)} %broadcast_in_dim.26.refs_1_, bf16[4,3,2,128,128]{4,3,2,1,0:T(8,128)(2,1)} %bitcast.16.refs_2_, bf16[4,3,2,128,128]{4,3,2,1,0:T(8,128)(2,1)} %bitcast.15.refs_3_, ...), custom_call_target="tpu_custom_call" | custom-call | flops 16106127360 | bytes 7864320 | tf_op jit(solution)/shard_map/pallas_call | solution.py:290
  157.9 11.8 %shard_map.104 = bf16[8,3,128,128]{3,2,1,0:T(8,128)(2,1)} custom-call(bf16[8,3,1,128,128]{4,3,2,1,0:T(8,128)(2,1)} %bitcast.27, f32[3,128,128]{2,1,0:T(8,128)} %broadcast_in_dim.26.refs_1_, bf16[4,3,2,128,128]{4,3,2,1,0:T(8,128)(2,1)} %collective-permute-done.5.refs_2_, bf16[4,3,2,128,128]{4,3,2,1,0:T(8,128)(2,1)} %collective-permute-done.7.refs_3_, ...), custom_call_target="tpu_custom_call" | custom-call | flops 9663676416 | bytes 4718592 | tf_op jit(solution)/shard_map/pallas_call | solution.py:290
  169.7 61.6 %all_to_all.25.refs_1_ = bf16[8,3,128,128]{3,2,1,0:T(8,128)(2,1)S(1)} all-to-all(bf16[8,3,128,128]{3,2,1,0:T(8,128)(2,1)} %shard_map.104), channel_id=1, replica_groups=mesh['expert'=2,'x'=2,'z'=4,'y'=4,'core'=2] {'x','z'}, dimensions={0} | all-to-all | bytes 1572864 | tf_op jit(solution)/shard_map/all_to_all | solution.py:418
  231.3 1.5 post.1
  (38 shorter events, 3.4 us)
Async XLA Ops:
  4.2 23.0 %all-to-all-start = ((bf16[16,2,128,128]{3,2,1,0:T(8,128)(2,1)}), bf16[16,2,128,128]{3,2,1,0:T(8,128)(2,1)}, u32[]{:S(2)}, u32[]{:S(2)}) async-start(bf16[16,2,128,128]{3,2,1,0:T(8,128)(2,1)} %shard_map.101), calls=%async_computation | async-start | bytes 2097152 | tf_op jit(solution)/shard_map/all_to_all | solution.py:389
  27.2 30.1 %all-to-all-start.1 = ((bf16[8,8,128,128]{3,2,1,0:T(8,128)(2,1)}), bf16[8,8,128,128]{3,2,1,0:T(8,128)(2,1)S(1)}, u32[]{:S(2)}, u32[]{:S(2)}) async-start(bf16[8,8,128,128]{3,2,1,0:T(8,128)(2,1)} %get-tuple-element.15), calls=%async_computation.1 | async-start | bytes 4194304 | tf_op jit(solution)/shard_map/all_to_all | solution.py:394
  30.8 25.3 %collective-permute-start.1 = (bf16[16,1,2,128,128]{4,3,2,1,0:T(8,128)(2,1)}, bf16[16,1,2,128,128]{4,3,2,1,0:T(8,128)(2,1)S(1)}, u32[]{:S(2)}, u32[]{:S(2)}) collective-permute-start(bf16[16,1,2,128,128]{4,3,2,1,0:T(8,128)(2,1)} %bitcast.3.refs_2_), channel_id=1, source_target_pairs={{0,2},{1,7},{2,4},{3,1},{4,6},{5,3},{6,0},{7,5},{8,10},{9,15},{10,... | collective-permute-start | bytes 3145736 | tf_op jit(solution)/shard_map/ppermute | solution.py:390
  31.1 29.6 %collective-permute-start.2 = (bf16[16,1,2,128,128]{4,3,2,1,0:T(8,128)(2,1)}, bf16[16,1,2,128,128]{4,3,2,1,0:T(8,128)(2,1)}, u32[]{:S(2)}, u32[]{:S(2)}) collective-permute-start(bf16[16,1,2,128,128]{4,3,2,1,0:T(8,128)(2,1)} %bitcast.3.refs_2_), channel_id=1, source_target_pairs={{0,6},{1,3},{2,0},{3,5},{4,2},{5,7},{6,4},{7,1},{8,14},{9,11},{10,... | collective-permute-start | bytes 3145736 | tf_op jit(solution)/shard_map/ppermute | solution.py:391
  56.1 2.5 %copy-start.3 = (bf16[16,1,2,128,128]{4,3,2,1,0:T(8,128)(2,1)}, bf16[16,1,2,128,128]{4,3,2,1,0:T(8,128)(2,1)S(1)}, u32[]{:S(2)}) copy-start(bf16[16,1,2,128,128]{4,3,2,1,0:T(8,128)(2,1)S(1)} %collective-permute-done.1.refs_3_) | copy-start | bytes 3145732
  56.1 23.9 %collective-permute-start.3 = (bf16[16,1,2,128,128]{4,3,2,1,0:T(8,128)(2,1)S(1)}, bf16[16,1,2,128,128]{4,3,2,1,0:T(8,128)(2,1)}, u32[]{:S(2)}, u32[]{:S(2)}) collective-permute-start(bf16[16,1,2,128,128]{4,3,2,1,0:T(8,128)(2,1)S(1)} %collective-permute-done.1.refs_3_), channel_id=1, source_target_pairs={{0,2},{1,7},{2,4},{3,1},{4,6},{5,3},{6,0},{7,5},{8,10},{9,15},{10,... | collective-permute-start | bytes 3145736 | tf_op jit(solution)/shard_map/ppermute | solution.py:392
  57.3 6.2 %collective-permute-start = (bf16[8,1,128,128]{3,2,0,1:T(8,128)(2,1)S(1)}, bf16[8,1,128,128]{3,2,0,1:T(8,128)(2,1)S(1)}, u32[]{:S(2)}, u32[]{:S(2)}) collective-permute-start(bf16[8,1,128,128]{3,2,0,1:T(8,128)(2,1)S(1)} %get-tuple-element.24), channel_id=1, source_target_pairs={{0,1},{1,0},{2,3},{3,2},{4,5},{5,4},{6,7},{7,6},{8,9},{9,8},{10,11... | collective-permute-start | bytes 786440 | tf_op jit(solution)/shard_map/ppermute | solution.py:401
  58.6 37.7 %collective-permute-start.8 = (bf16[4,3,2,128,128]{4,3,2,1,0:T(8,128)(2,1)}, bf16[4,3,2,128,128]{4,3,2,1,0:T(8,128)(2,1)}, u32[]{:S(2)}, u32[]{:S(2)}) collective-permute-start(bf16[4,3,2,128,128]{4,3,2,1,0:T(8,128)(2,1)} %bitcast.16.refs_2_), channel_id=1, source_target_pairs={{0,2},{2,4},{4,6},{6,0},{1,3},{3,5},{5,7},{7,1},{8,10},{10,12},{12... | collective-permute-start | bytes 2359304 | tf_op jit(solution)/shard_map/ppermute | solution.py:350
  60.2 36.1 %collective-permute-start.10 = (bf16[4,3,2,128,128]{4,3,2,1,0:T(8,128)(2,1)}, bf16[4,3,2,128,128]{4,3,2,1,0:T(8,128)(2,1)}, u32[]{:S(2)}, u32[]{:S(2)}) collective-permute-start(bf16[4,3,2,128,128]{4,3,2,1,0:T(8,128)(2,1)} %bitcast.15.refs_3_), channel_id=1, source_target_pairs={{0,6},{2,0},{4,2},{6,4},{1,7},{3,1},{5,3},{7,5},{8,14},{10,8},{12,... | collective-permute-start | bytes 2359304 | tf_op jit(solution)/shard_map/ppermute | solution.py:351
  60.6 49.0 %collective-permute-start.4 = (bf16[4,3,2,128,128]{4,3,2,1,0:T(8,128)(2,1)}, bf16[4,3,2,128,128]{4,3,2,1,0:T(8,128)(2,1)}, u32[]{:S(2)}, u32[]{:S(2)}) collective-permute-start(bf16[4,3,2,128,128]{4,3,2,1,0:T(8,128)(2,1)} %bitcast.15.refs_3_), channel_id=1, source_target_pairs={{0,2},{2,4},{4,6},{6,0},{1,3},{3,5},{5,7},{7,1},{8,10},{10,12},{12... | collective-permute-start | bytes 2359304 | tf_op jit(solution)/shard_map/ppermute | solution.py:352
  63.5 0.7 copy-start.1
  64.2 46.6 %collective-permute-start.6 = (bf16[4,3,2,128,128]{4,3,2,1,0:T(8,128)(2,1)}, bf16[4,3,2,128,128]{4,3,2,1,0:T(8,128)(2,1)}, u32[]{:S(2)}, u32[]{:S(2)}) collective-permute-start(bf16[4,3,2,128,128]{4,3,2,1,0:T(8,128)(2,1)} %bitcast.16.refs_2_), channel_id=1, source_target_pairs={{0,6},{2,0},{4,2},{6,4},{1,7},{3,1},{5,3},{7,5},{8,14},{10,8},{12,... | collective-permute-start | bytes 2359304 | tf_op jit(solution)/shard_map/ppermute | solution.py:353
  64.2 24.4 %copy-start.2 = (bf16[8,1,128,128]{3,2,0,1:T(8,128)(2,1)S(1)}, bf16[8,1,128,128]{3,2,0,1:T(8,128)(2,1)}, u32[]{:S(2)}) copy-start(bf16[8,1,128,128]{3,2,0,1:T(8,128)(2,1)} %copy-done.1) | copy-start | bytes 786436
  80.0 30.7 %collective-permute-start.14 = (bf16[4,3,2,128,128]{4,3,2,1,0:T(8,128)(2,1)}, bf16[4,3,2,128,128]{4,3,2,1,0:T(8,128)(2,1)}, u32[]{:S(2)}, u32[]{:S(2)}) collective-permute-start(bf16[4,3,2,128,128]{4,3,2,1,0:T(8,128)(2,1)} %bitcast.16.refs_2_), channel_id=1, source_target_pairs={{0,1},{1,0},{2,3},{3,2},{4,5},{5,4},{6,7},{7,6},{8,9},{9,8},{10,11... | collective-permute-start | bytes 2359304 | tf_op jit(solution)/shard_map/ppermute | solution.py:405
  83.9 48.4 %all-to-all-start.3 = ((bf16[8,3,128,128]{3,2,1,0:T(8,128)(2,1)}), bf16[8,3,128,128]{3,2,1,0:T(8,128)(2,1)S(1)}, u32[]{:S(2)}, u32[]{:S(2)}) async-start(bf16[8,3,128,128]{3,2,1,0:T(8,128)(2,1)} %get-tuple-element.18), calls=%async_computation.3 | async-start | bytes 1572864 | tf_op jit(solution)/shard_map/all_to_all | solution.py:398
  96.3 42.3 %collective-permute-start.15 = (bf16[4,3,2,128,128]{4,3,2,1,0:T(8,128)(2,1)}, bf16[4,3,2,128,128]{4,3,2,1,0:T(8,128)(2,1)}, u32[]{:S(2)}, u32[]{:S(2)}) collective-permute-start(bf16[4,3,2,128,128]{4,3,2,1,0:T(8,128)(2,1)} %bitcast.15.refs_3_), channel_id=1, source_target_pairs={{0,1},{1,0},{2,3},{3,2},{4,5},{5,4},{6,7},{7,6},{8,9},{9,8},{10,11... | collective-permute-start | bytes 2359304 | tf_op jit(solution)/shard_map/ppermute | solution.py:405
  96.3 42.8 %collective-permute-start.16 = (bf16[4,3,2,128,128]{4,3,2,1,0:T(8,128)(2,1)}, bf16[4,3,2,128,128]{4,3,2,1,0:T(8,128)(2,1)}, u32[]{:S(2)}, u32[]{:S(2)}) collective-permute-start(bf16[4,3,2,128,128]{4,3,2,1,0:T(8,128)(2,1)} %collective-permute-done.8.refs_4_), channel_id=1, source_target_pairs={{0,1},{1,0},{2,3},{3,2},{4,5},{5,4},{6,7},{7,6},{8,9},{9,8},{10,11... | collective-permute-start | bytes 2359304 | tf_op jit(solution)/shard_map/ppermute | solution.py:405
  109.7 29.5 %collective-permute-start.9 = (bf16[4,3,2,128,128]{4,3,2,1,0:T(8,128)(2,1)}, bf16[4,3,2,128,128]{4,3,2,1,0:T(8,128)(2,1)}, u32[]{:S(2)}, u32[]{:S(2)}) collective-permute-start(bf16[4,3,2,128,128]{4,3,2,1,0:T(8,128)(2,1)} %collective-permute-done.8.refs_4_), channel_id=1, source_target_pairs={{0,2},{2,4},{4,6},{6,0},{1,3},{3,5},{5,7},{7,1},{8,10},{10,12},{12... | collective-permute-start | bytes 2359304 | tf_op jit(solution)/shard_map/ppermute | solution.py:354
  110.8 29.1 %collective-permute-start.17 = (bf16[4,3,2,128,128]{4,3,2,1,0:T(8,128)(2,1)}, bf16[4,3,2,128,128]{4,3,2,1,0:T(8,128)(2,1)}, u32[]{:S(2)}, u32[]{:S(2)}) collective-permute-start(bf16[4,3,2,128,128]{4,3,2,1,0:T(8,128)(2,1)} %collective-permute-done.10.refs_5_), channel_id=1, source_target_pairs={{0,1},{1,0},{2,3},{3,2},{4,5},{5,4},{6,7},{7,6},{8,9},{9,8},{10,11... | collective-permute-start | bytes 2359304 | tf_op jit(solution)/shard_map/ppermute | solution.py:405
  110.8 28.8 %collective-permute-start.11 = (bf16[4,3,2,128,128]{4,3,2,1,0:T(8,128)(2,1)}, bf16[4,3,2,128,128]{4,3,2,1,0:T(8,128)(2,1)}, u32[]{:S(2)}, u32[]{:S(2)}) collective-permute-start(bf16[4,3,2,128,128]{4,3,2,1,0:T(8,128)(2,1)} %collective-permute-done.10.refs_5_), channel_id=1, source_target_pairs={{0,6},{2,0},{4,2},{6,4},{1,7},{3,1},{5,3},{7,5},{8,14},{10,8},{12,... | collective-permute-start | bytes 2359304 | tf_op jit(solution)/shard_map/ppermute | solution.py:355
  132.3 0.9 copy-start
  133.2 36.5 %all-to-all-start.2 = ((bf16[16,1,128,128]{3,2,1,0:T(8,128)(2,1)}), bf16[16,1,128,128]{3,2,1,0:T(8,128)(2,1)S(1)}, u32[]{:S(2)}, u32[]{:S(2)}) async-start(bf16[16,1,128,128]{3,2,1,0:T(8,128)(2,1)} %bitcast.11), calls=%async_computation.2 | async-start | bytes 1048576 | tf_op jit(solution)/shard_map/all_to_all | solution.py:415
  138.6 19.3 %collective-permute-start.5 = (bf16[4,3,2,128,128]{4,3,2,1,0:T(8,128)(2,1)}, bf16[4,3,2,128,128]{4,3,2,1,0:T(8,128)(2,1)}, u32[]{:S(2)}, u32[]{:S(2)}) collective-permute-start(bf16[4,3,2,128,128]{4,3,2,1,0:T(8,128)(2,1)} %collective-permute-done.4.refs_6_), channel_id=1, source_target_pairs={{0,1},{1,0},{2,3},{3,2},{4,5},{5,4},{6,7},{7,6},{8,9},{9,8},{10,11... | collective-permute-start | bytes 2359304 | tf_op jit(solution)/shard_map/ppermute | solution.py:405
  139.1 18.8 %collective-permute-start.7 = (bf16[4,3,2,128,128]{4,3,2,1,0:T(8,128)(2,1)}, bf16[4,3,2,128,128]{4,3,2,1,0:T(8,128)(2,1)}, u32[]{:S(2)}, u32[]{:S(2)}) collective-permute-start(bf16[4,3,2,128,128]{4,3,2,1,0:T(8,128)(2,1)} %collective-permute-done.6.refs_7_), channel_id=1, source_target_pairs={{0,1},{1,0},{2,3},{3,2},{4,5},{5,4},{6,7},{7,6},{8,9},{9,8},{10,11... | collective-permute-start | bytes 2359304 | tf_op jit(solution)/shard_map/ppermute | solution.py:405
  139.2 18.7 %collective-permute-start.12 = (bf16[4,3,2,128,128]{4,3,2,1,0:T(8,128)(2,1)}, bf16[4,3,2,128,128]{4,3,2,1,0:T(8,128)(2,1)}, u32[]{:S(2)}, u32[]{:S(2)}) collective-permute-start(bf16[4,3,2,128,128]{4,3,2,1,0:T(8,128)(2,1)} %collective-permute-done.9.refs_4_), channel_id=1, source_target_pairs={{0,1},{1,0},{2,3},{3,2},{4,5},{5,4},{6,7},{7,6},{8,9},{9,8},{10,11... | collective-permute-start | bytes 2359304 | tf_op jit(solution)/shard_map/ppermute | solution.py:405
  139.6 18.3 %collective-permute-start.13 = (bf16[4,3,2,128,128]{4,3,2,1,0:T(8,128)(2,1)}, bf16[4,3,2,128,128]{4,3,2,1,0:T(8,128)(2,1)}, u32[]{:S(2)}, u32[]{:S(2)}) collective-permute-start(bf16[4,3,2,128,128]{4,3,2,1,0:T(8,128)(2,1)} %collective-permute-done.11.refs_5_), channel_id=1, source_target_pairs={{0,1},{1,0},{2,3},{3,2},{4,5},{5,4},{6,7},{7,6},{8,9},{9,8},{10,11... | collective-permute-start | bytes 2359304 | tf_op jit(solution)/shard_map/ppermute | solution.py:405

commit v5 on v3

--- a/solution.py
+++ b/solution.py
@@ -376,7 +376,7 @@
     q, k, v = (queries, query_gain), (keys, key_gain), (values, None)
 
     key_values = tuple((kind, 3, 16 + h) for h in range(3) for kind in "kv")
-    (a,) = prepare(4, block, {"k": k, "v": v}, ((4, (("k", 1, 0), ("v", 1, 0))),))
+    (a,) = prepare(2, block, {"k": k, "v": v}, ((8, (("k", 1, 0), ("v", 1, 0))),))
     b, b_query = prepare(8, block, {"q": q, "k": k, "v": v}, (
         (1, key_values + (("q", 2, 0), ("q", 2, 1))),
         (1, tuple(("q", 3, 16 + h) for h in range(3))),
@@ -400,9 +400,8 @@
     def other(parts):
         return [lax.ppermute(p, "core", shift("core", 1)) for p in parts]
 
-    near_b = (own_b + near_b + other(own_b) + other(near_b[:2])
-              + other(near_b[2:]))
-    far_b = far_b + other(far_b)
+    far_b = other(near_b[2:]) + far_b + other(far_b)
+    near_b = own_b + near_b + other(own_b) + other(near_b[:2])
     gate_a = gate_of((x * 4 + z) * 2 + core, 1)
     gate_b = gate_of(16 + (x * 4 + z) * 3, 3)
 

time: 248 us -> 228 us (0.919)
  waiting for transfers between devices: 82.3 us -> 58.2 us
  starting transfers between devices: 30.5 us -> 34.3 us
    ppermute x1, waiting for transfers between devices: 26.3 us -> 1.15 us  [block_attention(): lax.ppermute(down_a[8:], 'y', shift('y', -1))]
    ppermute x1, waiting for transfers between devices: 0.01 us -> 22.9 us  [block_attention(): up_a = lax.ppermute(own_a, 'y', shift('y', 1))]
    all_to_all x1, waiting for transfers between devices: 22.6 us -> 0.01 us  [block_attention(): b = spread(b, narrow)]
    ppermute x1, waiting for transfers between devices: 0.01 us -> 7.62 us  [block_attention(): lax.ppermute(up_a[:8], 'y', shift('y', 1))]
    ppermute x1, waiting for transfers between devices: 9.03 us -> 2.22 us  [ring(): up_low = lax.ppermute(low, axis, shift(axis, 1))]
    ppermute x1, waiting for transfers between devices: 15.4 us -> 10.7 us  [ring(): up_high = lax.ppermute(high, axis, shift(axis, 1))]
    ppermute x1, waiting for transfers between devices: 0.01 us -> 3.86 us  [ring(): down_high = lax.ppermute(high, axis, shift(axis, -1))]
    ppermute x1, starting transfers between devices: 0.01 us -> 2.71 us  [ring(): up_low = lax.ppermute(low, axis, shift(axis, 1))]
  transfers between devices with their start and end apart: 23 -> 23, of which waited for: 5 -> 8; matrix products, arithmetic and copies ran while one was open for 4% -> 5% of each run, Pallas kernels for 22% -> 24%
where the time goes in v5:
time: 228 us; the launch traced here: 227 us
  blocking collectives  61.6 us (27%)
  Pallas kernels  59.4 us (26%)
  waiting for transfers between devices  58.2 us (26%)
  starting transfers between devices  34.3 us (15%)
  local copies, waits for them, and re-layouts  7.61 us (3%)
  other arithmetic  2.66 us (1%)
  matrix products  2.4 us (1%)
    all_to_all x1, blocking collectives, block_attention(): out_b = spread(out_b, narrow)  61.6 us
    pallas_call x3, Pallas kernels, attend(): pl.pallas_call(functools.partial(attend_kernel, sizes=sizes, resume=state...  46.5 us
    ppermute x1, waiting for transfers between devices, block_attention(): up_a = lax.ppermute(own_a, 'y', shift('y', 1))  22.9 us
    pallas_call x2, Pallas kernels, prepare(): pl.pallas_call(functools.partial(prep_kernel, tensors=kinds, plan=plan),...  11.4 us
    ppermute x1, waiting for transfers between devices, ring(): up_high = lax.ppermute(high, axis, shift(axis, 1))  10.7 us
    all_to_all x1, waiting for transfers between devices, block_attention(): own_a = spread(a, wide).reshape(16, 1, 2, HEAD_DIM, -1)  8.84 us
    ppermute x1, waiting for transfers between devices, block_attention(): lax.ppermute(up_a[:8], 'y', shift('y', 1))  7.62 us
    all_to_all x1, starting transfers between devices, block_attention(): own_a = spread(a, wide).reshape(16, 1, 2, HEAD_DIM, -1)  6.41 us
  transfers between devices with their start and end apart: 23, of which 8 were waited for; matrix products, arithmetic and copies ran while one was open for 5% of the time, Pallas kernels for 24%

profile of v5, /device:TPU:24, one launch (start us, length us, event | category | flops | bytes accessed | tf_op | source)
XLA Modules:
  0.0 227.1 jit_solution(8229420258429856061)
XLA Ops:
  0.0 3.7 %shard_map.101 = bf16[16,2,128,128]{3,2,1,0:T(8,128)(2,1)} custom-call(s32[1]{0:T(128)} %bitcast.block_ref, f32[1,128]{1,0:T(1,128)} %constant.47.inv_hbm, bf16[128,5120]{1,0:T(8,128)(2,1)} %refs_0_.3, bf16[128,5120]{1,0:T(8,128)(2,1)} %refs_1_.3, f32[40,128]{1,0:T(8,128)} %bitcast.29), custom_call_target="tpu_custom_call" | custom-call | tf_op jit(solution)/shard_map/pallas_call | solution.py:119
  3.7 6.4 %all-to-all-start = ((bf16[16,2,128,128]{3,2,1,0:T(8,128)(2,1)}), bf16[16,2,128,128]{3,2,1,0:T(8,128)(2,1)}, u32[]{:S(2)}, u32[]{:S(2)}) async-start(bf16[16,2,128,128]{3,2,1,0:T(8,128)(2,1)} %shard_map.101), calls=%async_computation | async-start | bytes 2097152 | tf_op jit(solution)/shard_map/all_to_all | solution.py:384
  10.1 7.7 %shard_map.100 = (bf16[8,8,128,128]{3,2,1,0:T(8,128)(2,1)}, bf16[8,3,128,128]{3,2,1,0:T(8,128)(2,1)}) custom-call(s32[1]{0:T(128)} %bitcast.block_ref, f32[1,128]{1,0:T(1,128)} %constant.47.inv_hbm, bf16[128,5120]{1,0:T(8,128)(2,1)} %refs_0_.2, bf16[128,5120]{1,0:T(8,128)(2,1)} %refs_0_.3, bf16[128,5120]{1,0:T(8,128)(2,1)} %refs_1_.3, f32[40,128]{1,0:T(8,128)} %bitcast.31, ...), custom_call_target="tpu_custom_call" | custom-call | tf_op jit(solution)/shard_map/pallas_call | solution.py:119
  17.9 8.8 %all-to-all-done = bf16[16,2,128,128]{3,2,1,0:T(8,128)(2,1)} async-done(((bf16[16,2,128,128]{3,2,1,0:T(8,128)(2,1)}), bf16[16,2,128,128]{3,2,1,0:T(8,128)(2,1)}, u32[]{:S(2)}, u32[]{:S(2)}) %all-to-all-start) | async-done | bytes 1048608 | tf_op jit(solution)/shard_map/all_to_all | solution.py:384
  26.7 3.6 %all-to-all-start.1 = ((bf16[8,8,128,128]{3,2,1,0:T(8,128)(2,1)}), bf16[8,8,128,128]{3,2,1,0:T(8,128)(2,1)S(1)}, u32[]{:S(2)}, u32[]{:S(2)}) async-start(bf16[8,8,128,128]{3,2,1,0:T(8,128)(2,1)} %get-tuple-element.15), calls=%async_computation.1 | async-start | bytes 4194304 | tf_op jit(solution)/shard_map/all_to_all | solution.py:390
  30.6 1.8 collective-permute-start.2
  32.4 22.9 %collective-permute-done.1.refs_3_ = bf16[16,1,2,128,128]{4,3,2,1,0:T(8,128)(2,1)} collective-permute-done((bf16[16,1,2,128,128]{4,3,2,1,0:T(8,128)(2,1)}, bf16[16,1,2,128,128]{4,3,2,1,0:T(8,128)(2,1)}, u32[]{:S(2)}, u32[]{:S(2)}) %collective-permute-start.1) | collective-permute-done | bytes 1048608 | tf_op jit(solution)/shard_map/ppermute | solution.py:385
  55.3 1.1 slice.16
  56.4 1.6 collective-permute-start.3
  57.9 1.1 slice.17
  59.8 1.2 fusion.7
  61.0 2.7 %collective-permute-start.9 = (bf16[4,3,2,128,128]{4,3,2,1,0:T(8,128)(2,1)}, bf16[4,3,2,128,128]{4,3,2,1,0:T(8,128)(2,1)}, u32[]{:S(2)}, u32[]{:S(2)}) collective-permute-start(bf16[4,3,2,128,128]{4,3,2,1,0:T(8,128)(2,1)} %bitcast.16.refs_2_), channel_id=1, source_target_pairs={{0,2},{2,4},{4,6},{6,0},{1,3},{3,5},{5,7},{7,1},{8,10},{10,12},{12... | collective-permute-start | bytes 2359304 | tf_op jit(solution)/shard_map/ppermute | solution.py:345
  63.7 7.6 %collective-permute-done.3.refs_5_ = bf16[8,1,2,128,128]{4,3,2,1,0:T(8,128)(2,1)} collective-permute-done((bf16[8,1,2,128,128]{4,3,2,1,0:T(8,128)(2,1)S(1)}, bf16[8,1,2,128,128]{4,3,2,1,0:T(8,128)(2,1)}, u32[]{:S(2)}, u32[]{:S(2)}) %collective-permute-start.3) | collective-permute-done | bytes 524320 | tf_op jit(solution)/shard_map/ppermute | solution.py:387
  71.3 2.7 %collective-permute-start.5 = (bf16[4,3,2,128,128]{4,3,2,1,0:T(8,128)(2,1)}, bf16[4,3,2,128,128]{4,3,2,1,0:T(8,128)(2,1)}, u32[]{:S(2)}, u32[]{:S(2)}) collective-permute-start(bf16[4,3,2,128,128]{4,3,2,1,0:T(8,128)(2,1)} %bitcast.15.refs_3_), channel_id=1, source_target_pairs={{0,2},{2,4},{4,6},{6,0},{1,3},{3,5},{5,7},{7,1},{8,10},{10,12},{12... | collective-permute-start | bytes 2359304 | tf_op jit(solution)/shard_map/ppermute | solution.py:347
  74.1 1.2 collective-permute-done.4.refs_6_
  76.7 1.3 convolution_reduce_fusion
  78.0 1.1 fusion
  79.9 5.3 %all-to-all-start.3 = ((bf16[8,3,128,128]{3,2,1,0:T(8,128)(2,1)}), bf16[8,3,128,128]{3,2,1,0:T(8,128)(2,1)S(1)}, u32[]{:S(2)}, u32[]{:S(2)}) async-start(bf16[8,3,128,128]{3,2,1,0:T(8,128)(2,1)} %get-tuple-element.18), calls=%async_computation.3 | async-start | bytes 1572864 | tf_op jit(solution)/shard_map/all_to_all | solution.py:394
  86.0 2.2 collective-permute-done.9.refs_4_
  88.2 3.9 %collective-permute-done.11.refs_5_ = bf16[4,3,2,128,128]{4,3,2,1,0:T(8,128)(2,1)} collective-permute-done((bf16[4,3,2,128,128]{4,3,2,1,0:T(8,128)(2,1)}, bf16[4,3,2,128,128]{4,3,2,1,0:T(8,128)(2,1)}, u32[]{:S(2)}, u32[]{:S(2)}) %collective-permute-start.11) | collective-permute-done | bytes 786464 | tf_op jit(solution)/shard_map/ppermute | solution.py:346
  92.1 10.7 %collective-permute-done.5.refs_6_ = bf16[4,3,2,128,128]{4,3,2,1,0:T(8,128)(2,1)} collective-permute-done((bf16[4,3,2,128,128]{4,3,2,1,0:T(8,128)(2,1)}, bf16[4,3,2,128,128]{4,3,2,1,0:T(8,128)(2,1)}, u32[]{:S(2)}, u32[]{:S(2)}) %collective-permute-start.5) | collective-permute-done | bytes 786464 | tf_op jit(solution)/shard_map/ppermute | solution.py:347
  102.8 2.8 %collective-permute-start.10 = (bf16[4,3,2,128,128]{4,3,2,1,0:T(8,128)(2,1)}, bf16[4,3,2,128,128]{4,3,2,1,0:T(8,128)(2,1)}, u32[]{:S(2)}, u32[]{:S(2)}) collective-permute-start(bf16[4,3,2,128,128]{4,3,2,1,0:T(8,128)(2,1)} %collective-permute-done.9.refs_4_), channel_id=1, source_target_pairs={{0,2},{2,4},{4,6},{6,0},{1,3},{3,5},{5,7},{7,1},{8,10},{10,12},{12... | collective-permute-start | bytes 2359304 | tf_op jit(solution)/shard_map/ppermute | solution.py:349
  105.5 0.9 collective-permute-done.7.refs_7_
  107.1 17.6 %shard_map.102 = bf16[16,1,128,128]{3,2,1,0:T(8,128)(2,1)} custom-call(bf16[16,1,1,128,128]{4,3,2,1,0:T(8,128)(2,1)} %maximum_bitcast_fusion.refs_0_, f32[1,128,128]{2,1,0:T(8,128)} %broadcast_in_dim.24.refs_1_, bf16[16,1,2,128,128]{4,3,2,1,0:T(8,128)(2,1)} %bitcast.3.refs_2_, bf16[16,1,2,128,128]{4,3,2,1,0:T(8,128)(2,1)} %collective-permute-done.1.refs_3_, ...), custom_call_target="tpu_custom_call" | custom-call | flops 17179869184 | bytes 4194304 | tf_op jit(solution)/shard_map/pallas_call | solution.py:290
  124.7 1.1 copy.19
  125.8 1.0 reverse_select_fusion
  126.8 0.9 copy-done
  127.7 5.2 %all-to-all-start.2 = ((bf16[16,1,128,128]{3,2,1,0:T(8,128)(2,1)}), bf16[16,1,128,128]{3,2,1,0:T(8,128)(2,1)S(1)}, u32[]{:S(2)}, u32[]{:S(2)}) async-start(bf16[16,1,128,128]{3,2,1,0:T(8,128)(2,1)} %bitcast.11), calls=%async_computation.2 | async-start | bytes 1048576 | tf_op jit(solution)/shard_map/all_to_all | solution.py:411
  135.0 17.1 %shard_map.103 = (f32[3,16,1024]{2,1,0:T(8,128)}, f32[3,128,1024]{2,1,0:T(8,128)}) custom-call(bf16[8,3,1,128,128]{4,3,2,1,0:T(8,128)(2,1)} %bitcast.26, f32[3,128,128]{2,1,0:T(8,128)} %broadcast_in_dim.26.refs_1_, bf16[4,3,2,128,128]{4,3,2,1,0:T(8,128)(2,1)} %bitcast.16.refs_2_, bf16[4,3,2,128,128]{4,3,2,1,0:T(8,128)(2,1)} %bitcast.15.refs_3_, ...), custom_call_target="tpu_custom_call" | custom-call | flops 16106127360 | bytes 7864320 | tf_op jit(solution)/shard_map/pallas_call | solution.py:290
  152.2 11.8 %shard_map.104 = bf16[8,3,128,128]{3,2,1,0:T(8,128)(2,1)} custom-call(bf16[8,3,1,128,128]{4,3,2,1,0:T(8,128)(2,1)} %bitcast.27, f32[3,128,128]{2,1,0:T(8,128)} %broadcast_in_dim.26.refs_1_, bf16[4,3,2,128,128]{4,3,2,1,0:T(8,128)(2,1)} %collective-permute-done.6.refs_2_, bf16[4,3,2,128,128]{4,3,2,1,0:T(8,128)(2,1)} %collective-permute-done.8.refs_3_, ...), custom_call_target="tpu_custom_call" | custom-call | flops 9663676416 | bytes 4718592 | tf_op jit(solution)/shard_map/pallas_call | solution.py:290
  164.1 61.6 %all_to_all.25.refs_1_ = bf16[8,3,128,128]{3,2,1,0:T(8,128)(2,1)S(1)} all-to-all(bf16[8,3,128,128]{3,2,1,0:T(8,128)(2,1)} %shard_map.104), channel_id=1, replica_groups=mesh['expert'=2,'x'=2,'z'=4,'y'=4,'core'=2] {'x','z'}, dimensions={0} | all-to-all | bytes 1572864 | tf_op jit(solution)/shard_map/all_to_all | solution.py:414
  225.6 1.5 post.1
  (40 shorter events, 6.3 us)
Async XLA Ops:
  3.7 23.0 %all-to-all-start = ((bf16[16,2,128,128]{3,2,1,0:T(8,128)(2,1)}), bf16[16,2,128,128]{3,2,1,0:T(8,128)(2,1)}, u32[]{:S(2)}, u32[]{:S(2)}) async-start(bf16[16,2,128,128]{3,2,1,0:T(8,128)(2,1)} %shard_map.101), calls=%async_computation | async-start | bytes 2097152 | tf_op jit(solution)/shard_map/all_to_all | solution.py:384
  26.7 32.9 %all-to-all-start.1 = ((bf16[8,8,128,128]{3,2,1,0:T(8,128)(2,1)}), bf16[8,8,128,128]{3,2,1,0:T(8,128)(2,1)S(1)}, u32[]{:S(2)}, u32[]{:S(2)}) async-start(bf16[8,8,128,128]{3,2,1,0:T(8,128)(2,1)} %get-tuple-element.15), calls=%async_computation.1 | async-start | bytes 4194304 | tf_op jit(solution)/shard_map/all_to_all | solution.py:390
  30.3 25.0 %collective-permute-start.1 = (bf16[16,1,2,128,128]{4,3,2,1,0:T(8,128)(2,1)}, bf16[16,1,2,128,128]{4,3,2,1,0:T(8,128)(2,1)}, u32[]{:S(2)}, u32[]{:S(2)}) collective-permute-start(bf16[16,1,2,128,128]{4,3,2,1,0:T(8,128)(2,1)} %bitcast.3.refs_2_), channel_id=1, source_target_pairs={{0,2},{2,4},{4,6},{6,0},{1,3},{3,5},{5,7},{7,1},{8,10},{10,12},{12... | collective-permute-start | bytes 3145736 | tf_op jit(solution)/shard_map/ppermute | solution.py:385
  30.6 27.3 %collective-permute-start.2 = (bf16[16,1,2,128,128]{4,3,2,1,0:T(8,128)(2,1)}, bf16[16,1,2,128,128]{4,3,2,1,0:T(8,128)(2,1)}, u32[]{:S(2)}, u32[]{:S(2)}) collective-permute-start(bf16[16,1,2,128,128]{4,3,2,1,0:T(8,128)(2,1)} %bitcast.3.refs_2_), channel_id=1, source_target_pairs={{0,6},{2,0},{4,2},{6,4},{1,7},{3,1},{5,3},{7,5},{8,14},{10,8},{12,... | collective-permute-start | bytes 3145736 | tf_op jit(solution)/shard_map/ppermute | solution.py:386
  56.4 15.0 %collective-permute-start.3 = (bf16[8,1,2,128,128]{4,3,2,1,0:T(8,128)(2,1)S(1)}, bf16[8,1,2,128,128]{4,3,2,1,0:T(8,128)(2,1)}, u32[]{:S(2)}, u32[]{:S(2)}) collective-permute-start(bf16[8,1,2,128,128]{4,3,2,1,0:T(8,128)(2,1)S(1)} %slice.16), channel_id=1, source_target_pairs={{0,2},{2,4},{4,6},{6,0},{1,3},{3,5},{5,7},{7,1},{8,10},{10,12},{12... | collective-permute-start | bytes 1572872 | tf_op jit(solution)/shard_map/ppermute | solution.py:387
  59.0 16.2 %collective-permute-start.4 = (bf16[8,1,2,128,128]{4,3,2,1,0:T(8,128)(2,1)S(1)}, bf16[8,1,2,128,128]{4,3,2,1,0:T(8,128)(2,1)}, u32[]{:S(2)}, u32[]{:S(2)}) collective-permute-start(bf16[8,1,2,128,128]{4,3,2,1,0:T(8,128)(2,1)S(1)} %slice.17), channel_id=1, source_target_pairs={{0,6},{2,0},{4,2},{6,4},{1,7},{3,1},{5,3},{7,5},{8,14},{10,8},{12,... | collective-permute-start | bytes 1572872 | tf_op jit(solution)/shard_map/ppermute | solution.py:388
  59.7 15.5 %collective-permute-start = (bf16[8,1,128,128]{3,2,0,1:T(8,128)(2,1)S(1)}, bf16[8,1,128,128]{3,2,0,1:T(8,128)(2,1)S(1)}, u32[]{:S(2)}, u32[]{:S(2)}) collective-permute-start(bf16[8,1,128,128]{3,2,0,1:T(8,128)(2,1)S(1)} %get-tuple-element.24), channel_id=1, source_target_pairs={{0,1},{1,0},{2,3},{3,2},{4,5},{5,4},{6,7},{7,6},{8,9},{9,8},{10,11... | collective-permute-start | bytes 786440 | tf_op jit(solution)/shard_map/ppermute | solution.py:397
  61.0 27.2 %collective-permute-start.9 = (bf16[4,3,2,128,128]{4,3,2,1,0:T(8,128)(2,1)}, bf16[4,3,2,128,128]{4,3,2,1,0:T(8,128)(2,1)}, u32[]{:S(2)}, u32[]{:S(2)}) collective-permute-start(bf16[4,3,2,128,128]{4,3,2,1,0:T(8,128)(2,1)} %bitcast.16.refs_2_), channel_id=1, source_target_pairs={{0,2},{2,4},{4,6},{6,0},{1,3},{3,5},{5,7},{7,1},{8,10},{10,12},{12... | collective-permute-start | bytes 2359304 | tf_op jit(solution)/shard_map/ppermute | solution.py:345
  63.7 28.3 %collective-permute-start.11 = (bf16[4,3,2,128,128]{4,3,2,1,0:T(8,128)(2,1)}, bf16[4,3,2,128,128]{4,3,2,1,0:T(8,128)(2,1)}, u32[]{:S(2)}, u32[]{:S(2)}) collective-permute-start(bf16[4,3,2,128,128]{4,3,2,1,0:T(8,128)(2,1)} %bitcast.15.refs_3_), channel_id=1, source_target_pairs={{0,6},{2,0},{4,2},{6,4},{1,7},{3,1},{5,3},{7,5},{8,14},{10,8},{12,... | collective-permute-start | bytes 2359304 | tf_op jit(solution)/shard_map/ppermute | solution.py:346
  71.3 31.4 %collective-permute-start.5 = (bf16[4,3,2,128,128]{4,3,2,1,0:T(8,128)(2,1)}, bf16[4,3,2,128,128]{4,3,2,1,0:T(8,128)(2,1)}, u32[]{:S(2)}, u32[]{:S(2)}) collective-permute-start(bf16[4,3,2,128,128]{4,3,2,1,0:T(8,128)(2,1)} %bitcast.15.refs_3_), channel_id=1, source_target_pairs={{0,2},{2,4},{4,6},{6,0},{1,3},{3,5},{5,7},{7,1},{8,10},{10,12},{12... | collective-permute-start | bytes 2359304 | tf_op jit(solution)/shard_map/ppermute | solution.py:347
  75.2 31.2 %collective-permute-start.7 = (bf16[4,3,2,128,128]{4,3,2,1,0:T(8,128)(2,1)}, bf16[4,3,2,128,128]{4,3,2,1,0:T(8,128)(2,1)}, u32[]{:S(2)}, u32[]{:S(2)}) collective-permute-start(bf16[4,3,2,128,128]{4,3,2,1,0:T(8,128)(2,1)} %bitcast.16.refs_2_), channel_id=1, source_target_pairs={{0,6},{2,0},{4,2},{6,4},{1,7},{3,1},{5,3},{7,5},{8,14},{10,8},{12,... | collective-permute-start | bytes 2359304 | tf_op jit(solution)/shard_map/ppermute | solution.py:348
  75.2 0.7 copy-start.1
  75.9 30.5 %collective-permute-start.15 = (bf16[4,3,2,128,128]{4,3,2,1,0:T(8,128)(2,1)}, bf16[4,3,2,128,128]{4,3,2,1,0:T(8,128)(2,1)}, u32[]{:S(2)}, u32[]{:S(2)}) collective-permute-start(bf16[4,3,2,128,128]{4,3,2,1,0:T(8,128)(2,1)} %bitcast.16.refs_2_), channel_id=1, source_target_pairs={{0,1},{1,0},{2,3},{3,2},{4,5},{5,4},{6,7},{7,6},{8,9},{9,8},{10,11... | collective-permute-start | bytes 2359304 | tf_op jit(solution)/shard_map/ppermute | solution.py:401
  75.9 9.2 %copy-start.2 = (bf16[8,1,128,128]{3,2,0,1:T(8,128)(2,1)S(1)}, bf16[8,1,128,128]{3,2,0,1:T(8,128)(2,1)}, u32[]{:S(2)}) copy-start(bf16[8,1,128,128]{3,2,0,1:T(8,128)(2,1)} %copy-done.1) | copy-start | bytes 786436
  79.9 47.0 %all-to-all-start.3 = ((bf16[8,3,128,128]{3,2,1,0:T(8,128)(2,1)}), bf16[8,3,128,128]{3,2,1,0:T(8,128)(2,1)S(1)}, u32[]{:S(2)}, u32[]{:S(2)}) async-start(bf16[8,3,128,128]{3,2,1,0:T(8,128)(2,1)} %get-tuple-element.18), calls=%async_computation.3 | async-start | bytes 1572864 | tf_op jit(solution)/shard_map/all_to_all | solution.py:394
  88.2 44.7 %collective-permute-start.16 = (bf16[4,3,2,128,128]{4,3,2,1,0:T(8,128)(2,1)}, bf16[4,3,2,128,128]{4,3,2,1,0:T(8,128)(2,1)}, u32[]{:S(2)}, u32[]{:S(2)}) collective-permute-start(bf16[4,3,2,128,128]{4,3,2,1,0:T(8,128)(2,1)} %bitcast.15.refs_3_), channel_id=1, source_target_pairs={{0,1},{1,0},{2,3},{3,2},{4,5},{5,4},{6,7},{7,6},{8,9},{9,8},{10,11... | collective-permute-start | bytes 2359304 | tf_op jit(solution)/shard_map/ppermute | solution.py:401
  92.1 41.4 %collective-permute-start.17 = (bf16[4,3,2,128,128]{4,3,2,1,0:T(8,128)(2,1)}, bf16[4,3,2,128,128]{4,3,2,1,0:T(8,128)(2,1)}, u32[]{:S(2)}, u32[]{:S(2)}) collective-permute-start(bf16[4,3,2,128,128]{4,3,2,1,0:T(8,128)(2,1)} %collective-permute-done.9.refs_4_), channel_id=1, source_target_pairs={{0,1},{1,0},{2,3},{3,2},{4,5},{5,4},{6,7},{7,6},{8,9},{9,8},{10,11... | collective-permute-start | bytes 2359304 | tf_op jit(solution)/shard_map/ppermute | solution.py:401
  102.8 30.8 %collective-permute-start.10 = (bf16[4,3,2,128,128]{4,3,2,1,0:T(8,128)(2,1)}, bf16[4,3,2,128,128]{4,3,2,1,0:T(8,128)(2,1)}, u32[]{:S(2)}, u32[]{:S(2)}) collective-permute-start(bf16[4,3,2,128,128]{4,3,2,1,0:T(8,128)(2,1)} %collective-permute-done.9.refs_4_), channel_id=1, source_target_pairs={{0,2},{2,4},{4,6},{6,0},{1,3},{3,5},{5,7},{7,1},{8,10},{10,12},{12... | collective-permute-start | bytes 2359304 | tf_op jit(solution)/shard_map/ppermute | solution.py:349
  106.4 27.8 %collective-permute-start.18 = (bf16[4,3,2,128,128]{4,3,2,1,0:T(8,128)(2,1)}, bf16[4,3,2,128,128]{4,3,2,1,0:T(8,128)(2,1)}, u32[]{:S(2)}, u32[]{:S(2)}) collective-permute-start(bf16[4,3,2,128,128]{4,3,2,1,0:T(8,128)(2,1)} %collective-permute-done.11.refs_5_), channel_id=1, source_target_pairs={{0,1},{1,0},{2,3},{3,2},{4,5},{5,4},{6,7},{7,6},{8,9},{9,8},{10,11... | collective-permute-start | bytes 2359304 | tf_op jit(solution)/shard_map/ppermute | solution.py:401
  106.4 27.5 %collective-permute-start.12 = (bf16[4,3,2,128,128]{4,3,2,1,0:T(8,128)(2,1)}, bf16[4,3,2,128,128]{4,3,2,1,0:T(8,128)(2,1)}, u32[]{:S(2)}, u32[]{:S(2)}) collective-permute-start(bf16[4,3,2,128,128]{4,3,2,1,0:T(8,128)(2,1)} %collective-permute-done.11.refs_5_), channel_id=1, source_target_pairs={{0,6},{2,0},{4,2},{6,4},{1,7},{3,1},{5,3},{7,5},{8,14},{10,8},{12,... | collective-permute-start | bytes 2359304 | tf_op jit(solution)/shard_map/ppermute | solution.py:350
  126.8 0.9 copy-start
  127.7 36.3 %all-to-all-start.2 = ((bf16[16,1,128,128]{3,2,1,0:T(8,128)(2,1)}), bf16[16,1,128,128]{3,2,1,0:T(8,128)(2,1)S(1)}, u32[]{:S(2)}, u32[]{:S(2)}) async-start(bf16[16,1,128,128]{3,2,1,0:T(8,128)(2,1)} %bitcast.11), calls=%async_computation.2 | async-start | bytes 1048576 | tf_op jit(solution)/shard_map/all_to_all | solution.py:411
  132.9 19.2 %collective-permute-start.6 = (bf16[4,3,2,128,128]{4,3,2,1,0:T(8,128)(2,1)}, bf16[4,3,2,128,128]{4,3,2,1,0:T(8,128)(2,1)}, u32[]{:S(2)}, u32[]{:S(2)}) collective-permute-start(bf16[4,3,2,128,128]{4,3,2,1,0:T(8,128)(2,1)} %collective-permute-done.5.refs_6_), channel_id=1, source_target_pairs={{0,1},{1,0},{2,3},{3,2},{4,5},{5,4},{6,7},{7,6},{8,9},{9,8},{10,11... | collective-permute-start | bytes 2359304 | tf_op jit(solution)/shard_map/ppermute | solution.py:401
  133.4 18.8 %collective-permute-start.8 = (bf16[4,3,2,128,128]{4,3,2,1,0:T(8,128)(2,1)}, bf16[4,3,2,128,128]{4,3,2,1,0:T(8,128)(2,1)}, u32[]{:S(2)}, u32[]{:S(2)}) collective-permute-start(bf16[4,3,2,128,128]{4,3,2,1,0:T(8,128)(2,1)} %collective-permute-done.7.refs_7_), channel_id=1, source_target_pairs={{0,1},{1,0},{2,3},{3,2},{4,5},{5,4},{6,7},{7,6},{8,9},{9,8},{10,11... | collective-permute-start | bytes 2359304 | tf_op jit(solution)/shard_map/ppermute | solution.py:401
  133.5 18.7 %collective-permute-start.13 = (bf16[4,3,2,128,128]{4,3,2,1,0:T(8,128)(2,1)}, bf16[4,3,2,128,128]{4,3,2,1,0:T(8,128)(2,1)}, u32[]{:S(2)}, u32[]{:S(2)}) collective-permute-start(bf16[4,3,2,128,128]{4,3,2,1,0:T(8,128)(2,1)} %collective-permute-done.10.refs_4_), channel_id=1, source_target_pairs={{0,1},{1,0},{2,3},{3,2},{4,5},{5,4},{6,7},{7,6},{8,9},{9,8},{10,11... | collective-permute-start | bytes 2359304 | tf_op jit(solution)/shard_map/ppermute | solution.py:401
  133.9 18.3 %collective-permute-start.14 = (bf16[4,3,2,128,128]{4,3,2,1,0:T(8,128)(2,1)}, bf16[4,3,2,128,128]{4,3,2,1,0:T(8,128)(2,1)}, u32[]{:S(2)}, u32[]{:S(2)}) collective-permute-start(bf16[4,3,2,128,128]{4,3,2,1,0:T(8,128)(2,1)} %collective-permute-done.12.refs_5_), channel_id=1, source_target_pairs={{0,1},{1,0},{2,3},{3,2},{4,5},{5,4},{6,7},{7,6},{8,9},{9,8},{10,11... | collective-permute-start | bytes 2359304 | tf_op jit(solution)/shard_map/ppermute | solution.py:401
